TPU v7x, 128 devices: a whole 4x4x4 slice. The times are simulated.
128 devices in a mesh: gx: 16 (over z_lo, x, core), gy: 8 (over y, z_hi).
Axes of the slice: x: 4, y: 4, z: 4 (z_hi: 2, z_lo: 2; z = z_hi * 2 + z_lo), core: 2. Of those that a mesh axis runs over, the one named last changes fastest.
Arguments:
- pair_in: bfloat16 [1024, 1024, 128], P(('gx', 'gy')), may hold values from -6 to 6
- residue_mask: int32 [1024], P(('gx', 'gy')), may hold values 0 or 1
- norm_start: float32 [128], replicated, may hold values from 0.25 to 1.75
- proj_start: bfloat16 [128, 512], replicated, may hold values from -0.5 to 0.5
- gate_bias_start: float32 [128], replicated, may hold values from -4 to 4
- bias_w_start: bfloat16 [128, 4], replicated, may hold values from -1.5 to 1.5
- out_w_start: bfloat16 [128, 128], replicated, may hold values from -1 to 1
- norm_end: float32 [128], replicated, may hold values from 0.25 to 1.75
- proj_end: bfloat16 [128, 512], replicated, may hold values from -0.5 to 0.5
- gate_bias_end: float32 [128], replicated, may hold values from -4 to 4
- bias_w_end: bfloat16 [128, 4], replicated, may hold values from -1.5 to 1.5
- out_w_end: bfloat16 [128, 128], replicated, may hold values from -1 to 1
- norm_trans: float32 [128], replicated, may hold values from 0.25 to 1.75
- trans_in: bfloat16 [128, 512], replicated, may hold values from -0.5 to 0.5
- trans_bias: float32 [512], replicated, may hold values from -4 to 4
- trans_out: bfloat16 [512, 128], replicated, may hold values from -0.375 to 0.375
Outputs:
- pair_out: bfloat16 [1024, 1024, 128], P(('gx', 'gy'))
Inputs may be any that keep to these rules, and one draw needn't show every extreme that they name: residue_mask holds only 0 and 1.
All inputs are finite; a program needn't handle non-finite values.
Results may differ from a plain program's by a relative error of at most 0.02.
Values may be sent and summed in bfloat16 or wider, within the bound.
A program may use at most 192 MiB of HBM per device.

v0:
```python
import jax
import jax.numpy as jnp
from jax import lax
from jax.sharding import PartitionSpec as P

HEADS = 4
HEAD_DIM = 32


big_negative = 1000000000.0


def layer_norm(values, norm_gain):
    widened = values.astype(jnp.float32)
    row_mean = jnp.mean(widened, axis=-1, keepdims=True)
    row_var = jnp.mean(jnp.square(widened - row_mean), axis=-1, keepdims=True)
    return ((widened - row_mean) * lax.rsqrt(row_var + 1e-05) * norm_gain).astype(jnp.bfloat16)


def project(normed, weight):
    flat = normed.reshape(-1, normed.shape[-1])
    result = jnp.dot(flat, weight, preferred_element_type=jnp.float32)
    return result.reshape(normed.shape[:-1] + (weight.shape[1],))


def split_heads(merged):
    return merged.astype(jnp.bfloat16).reshape(merged.shape[:-1] + (HEADS, HEAD_DIM))


def attend_block(query, keys, values, pair_bias, key_bias):
    score_scale = HEAD_DIM ** (-0.5)
    scores = jnp.einsum("jhd,khd->hjk", query, keys, preferred_element_type=jnp.float32)
    scores = scores * score_scale + pair_bias + key_bias
    attn_weights = jax.nn.softmax(scores, axis=-1)
    mixed = jnp.einsum(
        "hjk,khd->jhd", attn_weights, values.astype(jnp.float32), precision=lax.Precision.DEFAULT
    )
    return mixed.reshape(query.shape[0], HEADS * HEAD_DIM)


def gated_residual(residual, mixed, gate_logit, gate_bias, out_weight):
    gated = (mixed * jax.nn.sigmoid(gate_logit + gate_bias)).astype(jnp.bfloat16)
    return (residual.astype(jnp.float32) + project(gated, out_weight)).astype(jnp.bfloat16)


def projections(normed, weight, channels):
    projected = project(normed, weight)
    query = split_heads(projected[..., :channels])
    keys = split_heads(projected[..., channels : 2 * channels])
    values = split_heads(projected[..., 2 * channels : 3 * channels])
    return (query, keys, values, projected[..., 3 * channels :])


def local(
    pair_in,
    residue_mask,
    norm_start,
    proj_start,
    gate_bias_start,
    bias_w_start,
    out_w_start,
    norm_end,
    proj_end,
    gate_bias_end,
    bias_w_end,
    out_w_end,
    norm_trans,
    trans_in,
    trans_bias,
    trans_out,
):
    row_count, total_res, channels = pair_in.shape
    full_mask = lax.all_gather(residue_mask, ("gx", "gy"), axis=0, tiled=True)
    key_bias = (full_mask.astype(jnp.float32) - 1.0) * big_negative
    normed = layer_norm(pair_in, norm_start)
    query, keys, values, gate_logit = projections(normed, proj_start, channels)
    local_bias = project(normed, bias_w_start).astype(jnp.bfloat16)

    def start_block(portion):
        span = portion.shape[0]
        pair_bias = jnp.transpose(portion, (2, 0, 1)).astype(jnp.float32)
        query_part = lax.slice_in_dim(query, 0, span, axis=1)

        def per_row(operands):
            query_row, key_row, value_row = operands
            return attend_block(query_row, key_row, value_row, pair_bias, key_bias)

        return lax.map(per_row, (query_part, keys, values))

    mixed = start_block(lax.all_gather(local_bias, ("gx", "gy"), axis=0, tiled=True))
    after_start = gated_residual(pair_in, mixed, gate_logit, gate_bias_start, out_w_start)
    column_pair = lax.all_to_all(after_start, ("gx", "gy"), split_axis=1, concat_axis=0, tiled=True)
    normed = layer_norm(column_pair, norm_end)
    query, keys, values, gate_logit = projections(normed, proj_end, channels)
    local_bias = project(normed, bias_w_end).astype(jnp.bfloat16)
    key_cols = jnp.swapaxes(keys, 0, 1)
    value_cols = jnp.swapaxes(values, 0, 1)

    def end_block(portion):
        span = portion.shape[1]
        pair_bias = jnp.transpose(portion, (2, 1, 0)).astype(jnp.float32)
        query_part = jnp.swapaxes(lax.slice_in_dim(query, 0, span, axis=0), 0, 1)

        def per_column(operands):
            query_col, key_col, value_col = operands
            return attend_block(query_col, key_col, value_col, pair_bias, key_bias)

        return jnp.swapaxes(lax.map(per_column, (query_part, key_cols, value_cols)), 0, 1)

    mixed = end_block(lax.all_gather(local_bias, ("gx", "gy"), axis=1, tiled=True))
    after_end = gated_residual(column_pair, mixed, gate_logit, gate_bias_end, out_w_end)
    row_pair = lax.all_to_all(after_end, ("gx", "gy"), split_axis=0, concat_axis=1, tiled=True)
    normed = layer_norm(row_pair, norm_trans)
    hidden = jax.nn.relu(project(normed, trans_in) + trans_bias).astype(jnp.bfloat16)
    return (row_pair.astype(jnp.float32) + project(hidden, trans_out)).astype(jnp.bfloat16)


def solution(mesh):
    placed = (
        P(("gx", "gy"), None, None),
        P(("gx", "gy")),
        P(),
        P(),
        P(),
        P(),
        P(),
        P(),
        P(),
        P(),
        P(),
        P(),
        P(),
        P(),
        P(),
        P(),
    )
    return jax.shard_map(
        local, mesh=mesh, in_specs=placed, out_specs=P(("gx", "gy"), None, None), check_vma=False
    )
```

profile of v0, /device:TPU:1, one launch (start us, length us, event | category | flops | bytes accessed | tf_op | source)
XLA Modules:
  0.0 1321.9 jit_solution(4363286661396572859)
XLA Ops:
  16.5 69.2 %all-reduce = s32[1024]{0:T(1024)S(1)} all-reduce(s32[1024]{0:T(1024)S(1)} %dynamic-update-slice), channel_id=1, replica_groups=mesh['gx'=16,'gy'=8] {'gx','gy'}, use_global_device_ids=true, to_apply=%add | all-reduce | flops 1024 | bytes 8192
  85.7 7.1 fusion.95
  95.7 242.7 %all-gather.3.cloned.1.call-done = bf16[1024,1024,4]{1,2,0:T(4,128)(2,1)} async-done(((bf16[8,1024,4]{1,2,0:T(4,128)(2,1)}), bf16[1024,1024,4]{1,2,0:T(4,128)(2,1)}) %all-gather.3.cloned.1.call-update) | async-done | bytes 8388624 | tf_op jit(solution)/shard_map/all_gather | solution.py:90
  338.4 10.2 convert_bitcast_fusion.1
  348.6 19.2 %copy.60 = f32[4,1024,1024]{1,2,0:T(8,128)} copy(f32[4,1024,1024]{2,0,1:T(4,128)} %convert_bitcast_fusion.1) | data formatting | bytes 33554432 | tf_op jit(solution)/shard_map/while | solution.py:88
  370.4 248.7 %while.20 = (s32[]{:T(128)}, f32[8,1024,128]{1,2,0:T(8,128)}, bf16[8,1024,4,32]{1,3,2,0:T(8,128)(2,1)}, bf16[8,1024,4,32]{1,3,2,0:T(8,128)(2,1)}, bf16[8,1024,4,...) while((s32[]{:T(128)}, f32[8,1024,128]{1,2,0:T(8,128)}, ...), condition=%wide.region_5.6_spmd, body=%wide.region_2.5_spmd.sunk | while | flops 570417152 | bytes 69556312 | solution.py:88
  370.4 15.1 %fusion.109 = (f32[4,1024]{1,0:T(4,128)S(1)}, f32[4,1024,1024]{1,2,0:T(8,128)}) fusion(f32[1024]{0:T(1024)S(1)} %get-tuple-element.271, f32[4,1024,1024]{1,2,0:T(8,128)} %get-tuple-element.270, bf16[8,1024,4,32]{1,3,2,0:T(8,128)(2,1)} %get-tuple-element.269, s32[]{:T(128)} %get-tuple-element.257, bf16[8,1024,4,32]{1,3,2,0:T(8,128)(2,1)} %get-tuple-element.268), kind=kOutput, calls=%fused_computation.109.clone.1 | convolution fusion | flops 285208576 | bytes 34100224 | tf_op jit(solution)/shard_map/while/body/eval_jaxpr/jhd,khd->hjk/dot_general | solution.py:32
  385.5 8.0 fusion.110
  393.4 7.2 fusion.111
  401.5 15.0 %fusion.109 = (f32[4,1024]{1,0:T(4,128)S(1)}, f32[4,1024,1024]{1,2,0:T(8,128)}) fusion(f32[1024]{0:T(1024)S(1)} %get-tuple-element.271, f32[4,1024,1024]{1,2,0:T(8,128)} %get-tuple-element.270, bf16[8,1024,4,32]{1,3,2,0:T(8,128)(2,1)} %get-tuple-element.269, s32[]{:T(128)} %get-tuple-element.257, bf16[8,1024,4,32]{1,3,2,0:T(8,128)(2,1)} %get-tuple-element.268), kind=kOutput, calls=%fused_computation.109.clone.1 | convolution fusion | flops 285208576 | bytes 34100224 | tf_op jit(solution)/shard_map/while/body/eval_jaxpr/jhd,khd->hjk/dot_general | solution.py:32
  416.5 8.0 fusion.110
  424.5 7.2 fusion.111
  432.6 15.0 %fusion.109 = (f32[4,1024]{1,0:T(4,128)S(1)}, f32[4,1024,1024]{1,2,0:T(8,128)}) fusion(f32[1024]{0:T(1024)S(1)} %get-tuple-element.271, f32[4,1024,1024]{1,2,0:T(8,128)} %get-tuple-element.270, bf16[8,1024,4,32]{1,3,2,0:T(8,128)(2,1)} %get-tuple-element.269, s32[]{:T(128)} %get-tuple-element.257, bf16[8,1024,4,32]{1,3,2,0:T(8,128)(2,1)} %get-tuple-element.268), kind=kOutput, calls=%fused_computation.109.clone.1 | convolution fusion | flops 285208576 | bytes 34100224 | tf_op jit(solution)/shard_map/while/body/eval_jaxpr/jhd,khd->hjk/dot_general | solution.py:32
  447.6 8.0 fusion.110
  455.6 7.2 fusion.111
  463.7 15.0 %fusion.109 = (f32[4,1024]{1,0:T(4,128)S(1)}, f32[4,1024,1024]{1,2,0:T(8,128)}) fusion(f32[1024]{0:T(1024)S(1)} %get-tuple-element.271, f32[4,1024,1024]{1,2,0:T(8,128)} %get-tuple-element.270, bf16[8,1024,4,32]{1,3,2,0:T(8,128)(2,1)} %get-tuple-element.269, s32[]{:T(128)} %get-tuple-element.257, bf16[8,1024,4,32]{1,3,2,0:T(8,128)(2,1)} %get-tuple-element.268), kind=kOutput, calls=%fused_computation.109.clone.1 | convolution fusion | flops 285208576 | bytes 34100224 | tf_op jit(solution)/shard_map/while/body/eval_jaxpr/jhd,khd->hjk/dot_general | solution.py:32
  478.6 8.0 fusion.110
  486.6 7.2 fusion.111
  494.7 15.0 %fusion.109 = (f32[4,1024]{1,0:T(4,128)S(1)}, f32[4,1024,1024]{1,2,0:T(8,128)}) fusion(f32[1024]{0:T(1024)S(1)} %get-tuple-element.271, f32[4,1024,1024]{1,2,0:T(8,128)} %get-tuple-element.270, bf16[8,1024,4,32]{1,3,2,0:T(8,128)(2,1)} %get-tuple-element.269, s32[]{:T(128)} %get-tuple-element.257, bf16[8,1024,4,32]{1,3,2,0:T(8,128)(2,1)} %get-tuple-element.268), kind=kOutput, calls=%fused_computation.109.clone.1 | convolution fusion | flops 285208576 | bytes 34100224 | tf_op jit(solution)/shard_map/while/body/eval_jaxpr/jhd,khd->hjk/dot_general | solution.py:32
  509.7 8.0 fusion.110
  517.7 7.2 fusion.111
  525.8 15.0 %fusion.109 = (f32[4,1024]{1,0:T(4,128)S(1)}, f32[4,1024,1024]{1,2,0:T(8,128)}) fusion(f32[1024]{0:T(1024)S(1)} %get-tuple-element.271, f32[4,1024,1024]{1,2,0:T(8,128)} %get-tuple-element.270, bf16[8,1024,4,32]{1,3,2,0:T(8,128)(2,1)} %get-tuple-element.269, s32[]{:T(128)} %get-tuple-element.257, bf16[8,1024,4,32]{1,3,2,0:T(8,128)(2,1)} %get-tuple-element.268), kind=kOutput, calls=%fused_computation.109.clone.1 | convolution fusion | flops 285208576 | bytes 34100224 | tf_op jit(solution)/shard_map/while/body/eval_jaxpr/jhd,khd->hjk/dot_general | solution.py:32
  540.7 8.0 fusion.110
  548.7 7.2 fusion.111
  556.8 15.0 %fusion.109 = (f32[4,1024]{1,0:T(4,128)S(1)}, f32[4,1024,1024]{1,2,0:T(8,128)}) fusion(f32[1024]{0:T(1024)S(1)} %get-tuple-element.271, f32[4,1024,1024]{1,2,0:T(8,128)} %get-tuple-element.270, bf16[8,1024,4,32]{1,3,2,0:T(8,128)(2,1)} %get-tuple-element.269, s32[]{:T(128)} %get-tuple-element.257, bf16[8,1024,4,32]{1,3,2,0:T(8,128)(2,1)} %get-tuple-element.268), kind=kOutput, calls=%fused_computation.109.clone.1 | convolution fusion | flops 285208576 | bytes 34100224 | tf_op jit(solution)/shard_map/while/body/eval_jaxpr/jhd,khd->hjk/dot_general | solution.py:32
  571.8 8.0 fusion.110
  579.8 7.2 fusion.111
  587.9 15.0 %fusion.109 = (f32[4,1024]{1,0:T(4,128)S(1)}, f32[4,1024,1024]{1,2,0:T(8,128)}) fusion(f32[1024]{0:T(1024)S(1)} %get-tuple-element.271, f32[4,1024,1024]{1,2,0:T(8,128)} %get-tuple-element.270, bf16[8,1024,4,32]{1,3,2,0:T(8,128)(2,1)} %get-tuple-element.269, s32[]{:T(128)} %get-tuple-element.257, bf16[8,1024,4,32]{1,3,2,0:T(8,128)(2,1)} %get-tuple-element.268), kind=kOutput, calls=%fused_computation.109.clone.1 | convolution fusion | flops 285208576 | bytes 34100224 | tf_op jit(solution)/shard_map/while/body/eval_jaxpr/jhd,khd->hjk/dot_general | solution.py:32
  602.8 8.0 fusion.110
  610.8 7.2 fusion.111
  619.1 5.3 fusion.31
  625.7 37.8 %all_to_all.8 = bf16[8,1024,128]{2,0,1:T(8,128)(2,1)S(1)} all-to-all(bf16[8,1024,128]{2,0,1:T(8,128)(2,1)S(1)} %copy.62), channel_id=1, replica_groups=mesh['gx'=16,'gy'=8] {'gx','gy'}, dimensions={1} | all-to-all | bytes 4194304 | tf_op jit(solution)/shard_map/all_to_all | solution.py:92
  680.6 8.9 fusion.96
  692.2 306.5 %all-gather.5.cloned.1.call-done = bf16[1024,1024,4]{0,2,1:T(4,128)(2,1)} async-done(((bf16[1024,8,4]{0,2,1:T(4,128)(2,1)}), bf16[1024,1024,4]{0,2,1:T(4,128)(2,1)}) %all-gather.5.cloned.1.call-update) | async-done | bytes 8388624 | tf_op jit(solution)/shard_map/all_gather | solution.py:110
  998.7 10.2 convert_bitcast_fusion
  1008.9 19.2 %copy.71 = f32[4,1024,1024]{1,2,0:T(8,128)} copy(f32[4,1024,1024]{2,0,1:T(4,128)} %convert_bitcast_fusion) | data formatting | bytes 33554432 | tf_op jit(solution)/shard_map/while | solution.py:108
  1030.7 217.3 %while.21 = (s32[]{:T(128)}, f32[8,1024,128]{1,2,0:T(8,128)}, bf16[8,1024,4,32]{1,3,2,0:T(8,128)(2,1)}, bf16[8,1024,4,32]{1,3,2,0:T(8,128)(2,1)}, bf16[8,1024,4,...) while((s32[]{:T(128)}, f32[8,1024,128]{1,2,0:T(8,128)}, ...), condition=%wide.region_11.12_spmd, body=%wide.region_8.11_spmd.sunk | while | flops 570417152 | bytes 69556312 | solution.py:108
  1030.8 11.1 fusion.114
  1041.9 8.0 fusion.115
  1049.9 7.2 fusion.116
  1058.0 11.1 fusion.114
  1069.1 8.0 fusion.115
  1077.0 7.2 fusion.116
  1085.1 11.1 fusion.114
  1096.2 8.0 fusion.115
  1104.2 7.2 fusion.116
  1112.3 11.1 fusion.114
  1123.3 8.0 fusion.115
  1131.3 7.2 fusion.116
  1139.4 11.1 fusion.114
  1150.4 8.0 fusion.115
  1158.4 7.2 fusion.116
  1166.6 11.1 fusion.114
  1177.6 8.0 fusion.115
  1185.6 7.2 fusion.116
  1193.7 11.1 fusion.114
  1204.7 8.0 fusion.115
  1212.7 7.2 fusion.116
  1220.8 11.1 fusion.114
  1231.9 8.0 fusion.115
  1239.9 7.2 fusion.116
  1248.0 6.5 fusion.51
  1255.9 37.5 %all_to_all.9 = bf16[1024,8,128]{2,1,0:T(8,128)(2,1)S(1)} all-to-all(bf16[1024,8,128]{2,1,0:T(8,128)(2,1)S(1)} %copy.73), channel_id=1, replica_groups=mesh['gx'=16,'gy'=8] {'gx','gy'}, dimensions={0} | all-to-all | bytes 4194304 | tf_op jit(solution)/shard_map/all_to_all | solution.py:112
  1305.6 9.1 fusion.45
  (99 shorter events, 66.0 us)
Async XLA Ops:
  6.5 79.2 %copy-start = (bf16[128,512]{1,0:T(8,128)(2,1)S(1)}, bf16[128,512]{1,0:T(8,128)(2,1)}, u32[]{:S(2)}) copy-start(bf16[128,512]{1,0:T(8,128)(2,1)} %param.23) | copy-start | bytes 393220
  6.5 6.1 copy-start.4
  6.5 6.1 copy-start.7
  6.5 6.1 copy-start.14
  6.5 9.7 copy-start.16
  6.5 331.8 %all-gather.3.cloned.1.call-start = ((), (), s32[]{:S(2)}) async-start(), calls=%async_computation.2 | async-start | bytes 8454144 | tf_op jit(solution)/shard_map/all_gather | solution.py:90
  16.2 982.5 %all-gather.5.cloned.1.call-start = ((), (), s32[]{:S(2)}) async-start(), calls=%async_computation.3 | async-start | bytes 8454144 | tf_op jit(solution)/shard_map/all_gather | solution.py:110
  370.4 248.7 %copy-start.5 = (bf16[8,1024,128]{2,1,0:T(8,128)(2,1)S(1)}, bf16[8,1024,128]{2,1,0:T(8,128)(2,1)}, u32[]{:S(2)}) copy-start(bf16[8,1024,128]{2,1,0:T(8,128)(2,1)} %param.20) | copy-start | bytes 6291460
  370.4 248.7 %copy-start.11 = (bf16[128,128]{1,0:T(8,128)(2,1)S(1)}, bf16[128,128]{1,0:T(8,128)(2,1)}, u32[]{:S(2)}) copy-start(bf16[128,128]{1,0:T(8,128)(2,1)} %param.26) | copy-start | bytes 98308
  370.4 248.7 %copy-start.17 = (f32[128]{0:T(128)S(1)}, f32[128]{0:T(128)}, u32[]{:S(2)}) copy-start(f32[128]{0:T(128)} %param.24) | copy-start | bytes 1540
  666.2 1.9 copy-start.2
  669.5 6.3 copy-start.8
  669.5 6.3 copy-start.15
  674.8 5.8 copy-start.6
  1030.6 217.3 %copy-start.12 = (bf16[128,128]{1,0:T(8,128)(2,1)S(1)}, bf16[128,128]{1,0:T(8,128)(2,1)}, u32[]{:S(2)}) copy-start(bf16[128,128]{1,0:T(8,128)(2,1)} %param.31) | copy-start | bytes 98308
  1030.6 217.3 %copy-start.18 = (f32[128]{0:T(128)S(1)}, f32[128]{0:T(128)}, u32[]{:S(2)}) copy-start(f32[128]{0:T(128)} %param.29) | copy-start | bytes 1540
  1296.0 2.0 copy-start.3
  1299.3 6.3 copy-start.9
  1299.3 6.3 copy-start.10
  1299.3 6.3 copy-start.13
  1299.3 6.3 copy-start.19
  1305.6 9.1 copy-start.1
Sparse Core Ops, SparseCore 0:
  16.3 322.0 all-gather.2
  680.7 317.9 all-gather.4
where the time goes:
time: 1330 us; the launch traced here: 1320 us
  waiting for transfers between devices  549 us (41%)
  matrix products  369 us (28%)
  other arithmetic  171 us (13%)
  blocking collectives  145 us (11%)
  local copies, waits for them, and re-layouts  72.7 us (5%)
  between operations  14 us (1%)
    all_gather x1, waiting for transfers between devices, local(): lax.all_gather(local_bias, ('gx', 'gy'), axis=1, tiled=True)  307 us
    all_gather x1, waiting for transfers between devices, local(): lax.all_gather(local_bias, ('gx', 'gy'), axis=0, tiled=True)  243 us
    dot_general x16, matrix products, attend_block(): jnp.einsum('jhd,khd->hjk', query, keys, preferred_element_type=jnp.float32)  208 us
    reduce_sum x16, other arithmetic, attend_block(): attn_weights = jax.nn.softmax(scores, axis=-1)  128 us
    dot_general x16, matrix products, attend_block(): jnp.einsum('hjk,khd->jhd', attn_weights, values.astype(jnp.float32), prec...  116 us
    unnamed x1, blocking collectives  69.2 us
    dot_general x7, matrix products, project(): result = jnp.dot(flat, weight, preferred_element_type=jnp.float32)  45.1 us
    all_to_all x1, blocking collectives, local(): lax.all_to_all(after_start, ('gx', 'gy'), split_axis=1, concat_axis=0, ti...  37.8 us
  transfers between devices with their start and end apart: 2, of which 2 were waited for; matrix products, arithmetic and copies ran while one was open for 2% of the time, Pallas kernels for 0%

commit v1 on v0

v1 whole, which is shorter than its diff:
```python
import functools

import jax
import jax.numpy as jnp
from jax import lax
from jax.experimental import pallas as pl
from jax.experimental.pallas import tpu as pltpu
from jax.sharding import PartitionSpec as P

HEADS = 4
HEAD_DIM = 32
LOG2E = 1.4426950408889634
JB = 256
KB = 128
F32 = jnp.float32
BF16 = jnp.bfloat16
NT = (((1,), (1,)), ((), ()))
TN = (((0,), (0,)), ((), ()))
VMEM = pl.BlockSpec(memory_space=pltpu.VMEM)


def layer_norm(t, gain):
    mean = jnp.mean(t, axis=-1, keepdims=True)
    cent = t - mean
    var = jnp.mean(cent * cent, axis=-1, keepdims=True)
    return (cent * lax.rsqrt(var + 1e-05) * gain).astype(BF16)


def bias_kernel(x_ref, g_ref, bw_ref, o_ref):
    bwt = bw_ref[...].astype(F32).T.astype(BF16)
    gain = g_ref[...]
    for r in range(x_ref.shape[0]):
        a = layer_norm(x_ref[r].astype(F32), gain)
        b = lax.dot_general(bwt, a, NT, preferred_element_type=F32) * LOG2E
        o_ref[:, r, :] = b[:HEADS].astype(BF16)


def pair_bias(x, gain, bias_w):
    rows, res, chan = x.shape
    bw = jnp.pad(bias_w, ((0, 0), (0, 128 - HEADS)))
    return pl.pallas_call(
        bias_kernel,
        out_shape=jax.ShapeDtypeStruct((HEADS, rows, res), BF16),
        in_specs=[VMEM] * 3,
        out_specs=VMEM,
    )(x, gain, bw)


def attn_kernel(trans, *refs):
    (x_ref, g_ref, w_ref, gb_ref, ow_ref, mrow_ref, mcol_ref, b_ref), refs = refs[:8], refs[8:]
    if trans:
        (ng_ref, ti_ref, tb_ref, to_ref), refs = refs[:4], refs[4:]
    o_ref, km, qs, vx, gt, bt, pp, ot, wk, wq, ss = refs
    rows, res, chan = x_ref.shape
    jb = pl.program_id(0)
    groups = rows // 4
    nk = res // KB

    @pl.when(jb == 0)
    def _():
        w = w_ref[...].astype(F32)
        wqt = w[:, :chan].T
        for s in range(4):
            cut = chan - 32 * s
            wk[s] = (pltpu.roll(w[:, chan : 2 * chan], 32 * s, 1) if s else w[:, chan : 2 * chan]).astype(BF16)
            wq[s] = (jnp.concatenate([wqt[cut:], wqt[:cut]], axis=0) if s else wqt).astype(BF16)
        wvt = w[:, 2 * chan : 3 * chan].T.astype(BF16)
        wgt = w[:, 3 * chan :].T.astype(BF16)
        gain = g_ref[...]
        gb = gb_ref[...].T
        mrow = mrow_ref[...]
        lane = lax.broadcasted_iota(jnp.int32, (res, chan), 1) // HEAD_DIM

        def project(r, carry):
            s = lax.rem(r, 4)
            grp = r // 4
            a = layer_norm(x_ref[r].astype(F32), gain)
            kk = jnp.dot(a, wk[s], preferred_element_type=F32)
            qt = (
                lax.dot_general(wq[s], a, NT, preferred_element_type=F32)
                * (HEAD_DIM**-0.5 * LOG2E)
            ).astype(BF16)
            vt = lax.dot_general(wvt, a, NT, preferred_element_type=F32) * mrow
            gt[r] = jax.nn.sigmoid(lax.dot_general(wgt, a, NT, preferred_element_type=F32) + gb)
            for h in range(HEADS):
                slot = lax.rem(h + s, 4)
                km[r, h] = jnp.where(lane == slot, kk, 0.0).astype(BF16)
                vx[r, h, :HEAD_DIM] = vt[HEAD_DIM * h : HEAD_DIM * (h + 1)].astype(BF16)
                vx[r, h, HEAD_DIM:] = jnp.broadcast_to(mrow, (16, res)).astype(BF16)
            for t in range(4):
                hh = lax.rem(t - s + 4, 4)
                qs[grp, hh, pl.ds(32 * t, 32)] = qt[32 * t : 32 * (t + 1)]
            return carry

        lax.fori_loop(0, rows, project, 0)

    for h in range(HEADS):
        for kb in range(nk):
            sl = slice(KB * kb, KB * (kb + 1))
            bt[h, sl] = b_ref[h, :, sl].T

    eye = (
        lax.broadcasted_iota(jnp.int32, (KB, KB), 0) == lax.broadcasted_iota(jnp.int32, (KB, KB), 1)
    ).astype(F32).astype(BF16)
    joff = pl.multiple_of(jb * JB, JB)

    def head_body(it, carry):
        grp = it // HEADS
        h = lax.rem(it, HEADS)
        q = qs[grp, h, :, pl.ds(joff, JB)]
        for kb in range(nk):
            sl = slice(KB * kb, KB * (kb + 1))
            rhs = jnp.concatenate([bt[h, sl], q], axis=0)
            lhs = jnp.concatenate(
                [jnp.concatenate([eye, km[grp * 4 + r, h, sl]], axis=1) for r in range(4)], axis=0
            )
            s4 = jnp.dot(lhs, rhs, preferred_element_type=F32)
            p4 = jnp.exp2(s4).astype(BF16)
            for r in range(4):
                pp[r, sl] = p4[KB * r : KB * (r + 1)]
        good = None
        for r in range(4):
            oe = jnp.dot(vx[grp * 4 + r, h], pp[r], preferred_element_type=F32)
            den = oe[HEAD_DIM : HEAD_DIM + 1]
            fine = (den > 2.0**-60) & (den < 2.0**100)
            good = fine if good is None else good & fine
            ot[grp * 4 + r, pl.ds(pl.multiple_of(HEAD_DIM * h, HEAD_DIM), HEAD_DIM)] = (
                oe[:HEAD_DIM] / den
            )

        @pl.when(jnp.min(good.astype(F32)) < 0.5)
        def _():
            def slow_row(r, carry):
                row = grp * 4 + r

                def scores(kb, carry):
                    ks = pl.ds(pl.multiple_of(kb * KB, KB), KB)
                    rhs = jnp.concatenate([bt[h, ks], q], axis=0)
                    lhs = jnp.concatenate([eye, km[row, h, ks]], axis=1)
                    s1 = jnp.dot(lhs, rhs, preferred_element_type=F32)
                    s1 = jnp.where(mcol_ref[ks] > 0.5, s1, -1e30)
                    ss[ks] = s1
                    return jnp.maximum(carry, jnp.max(s1, axis=0, keepdims=True))

                top = lax.fori_loop(0, nk, scores, jnp.full((1, JB), -1e30, F32))

                def weights(kb, carry):
                    ks = pl.ds(pl.multiple_of(kb * KB, KB), KB)
                    pp[0, ks] = jnp.exp2(ss[ks] - top).astype(BF16)
                    return carry

                lax.fori_loop(0, nk, weights, 0)
                oe = jnp.dot(vx[row, h], pp[0], preferred_element_type=F32)
                ot[row, pl.ds(pl.multiple_of(HEAD_DIM * h, HEAD_DIM), HEAD_DIM)] = (
                    oe[:HEAD_DIM] / oe[HEAD_DIM : HEAD_DIM + 1]
                )
                return carry

            lax.fori_loop(0, 4, slow_row, 0)

        return carry

    lax.fori_loop(0, groups * HEADS, head_body, 0)

    def finish(r, carry):
        gated = (ot[r] * gt[r, :, pl.ds(joff, JB)]).T.astype(BF16)
        z = x_ref[r, pl.ds(joff, JB)].astype(F32) + jnp.dot(
            gated, ow_ref[...], preferred_element_type=F32
        )
        z = z.astype(BF16)
        if trans:
            zf = z.astype(F32)
            a = layer_norm(zf, ng_ref[...])
            hid = jnp.dot(a, ti_ref[...], preferred_element_type=F32) + tb_ref[...]
            hid = jnp.maximum(hid, 0.0).astype(BF16)
            z = (zf + jnp.dot(hid, to_ref[...], preferred_element_type=F32)).astype(BF16)
        o_ref[r] = z
        return carry

    lax.fori_loop(0, rows, finish, 0)


def attention(x, gain, proj, gate_bias, out_w, mrow, mcol, bias, trans=()):
    rows, res, chan = x.shape
    full = lambda a: pl.BlockSpec(a.shape, lambda j, n=a.ndim: (0,) * n)
    ins = [x, gain, proj, gate_bias, out_w, mrow, mcol]
    specs = [full(a) for a in ins] + [pl.BlockSpec((HEADS, JB, res), lambda j: (0, j, 0))]
    ins.append(bias)
    ins += trans
    specs += [full(a) for a in trans]
    return pl.pallas_call(
        functools.partial(attn_kernel, bool(trans)),
        grid=(res // JB,),
        out_shape=jax.ShapeDtypeStruct((rows, res, chan), BF16),
        in_specs=specs,
        out_specs=pl.BlockSpec((rows, JB, chan), lambda j: (0, j, 0)),
        scratch_shapes=[
            pltpu.VMEM((rows, HEADS, res, chan), BF16),
            pltpu.VMEM((rows // 4, HEADS, chan, res), BF16),
            pltpu.VMEM((rows, HEADS, HEAD_DIM + 16, res), BF16),
            pltpu.VMEM((rows, chan, res), F32),
            pltpu.VMEM((HEADS, res, JB), BF16),
            pltpu.VMEM((4, res, JB), BF16),
            pltpu.VMEM((rows, chan, JB), F32),
            pltpu.VMEM((4, chan, chan), BF16),
            pltpu.VMEM((4, chan, chan), BF16),
            pltpu.VMEM((res, JB), F32),
        ],
        compiler_params=pltpu.CompilerParams(
            dimension_semantics=("arbitrary",), vmem_limit_bytes=60 * 1024 * 1024
        ),
    )(*ins)


def local(
    pair_in,
    residue_mask,
    norm_start,
    proj_start,
    gate_bias_start,
    bias_w_start,
    out_w_start,
    norm_end,
    proj_end,
    gate_bias_end,
    bias_w_end,
    out_w_end,
    norm_trans,
    trans_in,
    trans_bias,
    trans_out,
):
    rows, res, chan = pair_in.shape
    axes = ("gx", "gy")
    row = lambda v: v.reshape(1, -1)
    mask = lax.all_gather(residue_mask, axes, axis=0, tiled=True).astype(F32)
    mask = jnp.where(jnp.max(mask) > 0.5, mask, 1.0)
    mrow, mcol = mask.reshape(1, res), mask.reshape(res, 1)

    bias = pair_bias(pair_in, row(norm_start), bias_w_start)
    bias = lax.all_gather(bias, axes, axis=1, tiled=True)
    z1 = attention(
        pair_in, row(norm_start), proj_start, row(gate_bias_start), out_w_start, mrow, mcol, bias
    )
    cols = lax.all_to_all(z1, axes, split_axis=1, concat_axis=0, tiled=True)
    cols = jnp.swapaxes(cols, 0, 1)
    bias = pair_bias(cols, row(norm_end), bias_w_end)
    bias = lax.all_gather(bias, axes, axis=1, tiled=True)
    out = attention(
        cols, row(norm_end), proj_end, row(gate_bias_end), out_w_end, mrow, mcol, bias,
        (row(norm_trans), trans_in, row(trans_bias), trans_out),
    )
    out = lax.all_to_all(jnp.swapaxes(out, 0, 1), axes, split_axis=0, concat_axis=1, tiled=True)
    return out


def solution(mesh):
    spec = P(("gx", "gy"), None, None)
    placed = (spec, P(("gx", "gy"))) + (P(),) * 14
    return jax.shard_map(local, mesh=mesh, in_specs=placed, out_specs=spec, check_vma=False)
```

time: 1330 us -> 880 us (0.66)
  matrix products: 369 us -> 0 us
  other arithmetic: 171 us -> 0.66 us
  Pallas kernels: 0 us -> 139 us
  local copies, waits for them, and re-layouts: 72.7 us -> 14.1 us
  waiting for transfers between devices: 549 us -> 597 us
  blocking collectives: 145 us -> 106 us
    dot_general x39 -> x0, matrix products: 369 us -> none  [the longest x16 208 us: attend_block(): jnp.einsum('jhd,khd->hjk', query, keys, preferred_element_type=jnp.float32)]
    reduce_sum x22 -> x0, other arithmetic: 146 us -> none  [the longest x16 128 us: attend_block(): attn_weights = jax.nn.softmax(scores, axis=-1)]
    pallas_call x0 -> x4, Pallas kernels: none -> 139 us  [the longest x2 129 us: attention(): pl.pallas_call(functools.partial(attn_kernel, bool(trans)), grid=(res //...]
    while x2 -> x0, local copies, waits for them, and re-layouts: 38.5 us -> none  [the longest x1 19.2 us: start_block(): return lax.map(per_row, (query_part, keys, values))]
    all_to_all x2 -> x1, blocking collectives: 75.4 us -> 37.3 us  [local(): lax.all_to_all(jnp.swapaxes(out, 0, 1), axes, split_axis=0, concat_axis=1...]
    all_to_all x0 -> x1, waiting for transfers between devices: none -> 29.1 us  [local(): cols = lax.all_to_all(z1, axes, split_axis=1, concat_axis=0, tiled=True)]
    convert_element_type x4 -> x0, other arithmetic: 25.6 us -> none  [the longest x1 10.2 us: start_block(): pair_bias = jnp.transpose(portion, (2, 0, 1)).astype(jnp.float32)]
    all_gather x2, waiting for transfers between devices: 549 us -> 568 us  [local(): bias = lax.all_gather(bias, axes, axis=1, tiled=True)]
  transfers between devices with their start and end apart: 2 -> 3, of which waited for: 2 -> 3; matrix products, arithmetic and copies ran while one was open for 2% -> 0% of each run, Pallas kernels for 0% -> 0%
where the time goes in v1:
time: 880 us; the launch traced here: 879 us
  waiting for transfers between devices  597 us (68%)
  Pallas kernels  139 us (16%)
  blocking collectives  106 us (12%)
  local copies, waits for them, and re-layouts  14.1 us (2%)
  between operations  14.1 us (2%)
    all_gather x2, waiting for transfers between devices, local(): bias = lax.all_gather(bias, axes, axis=1, tiled=True)  568 us
    pallas_call x2, Pallas kernels, attention(): pl.pallas_call(functools.partial(attn_kernel, bool(trans)), grid=(res //...  129 us
    unnamed x1, blocking collectives  68.7 us
    all_to_all x1, blocking collectives, local(): lax.all_to_all(jnp.swapaxes(out, 0, 1), axes, split_axis=0, concat_axis=1...  37.3 us
    all_to_all x1, waiting for transfers between devices, local(): cols = lax.all_to_all(z1, axes, split_axis=1, concat_axis=0, tiled=True)  29.1 us
  transfers between devices with their start and end apart: 3, of which 3 were waited for; matrix products, arithmetic and copies ran while one was open for 0% of the time, Pallas kernels for 0%

profile of v1, /device:TPU:1, one launch (start us, length us, event | category | flops | bytes accessed | tf_op | source)
XLA Modules:
  0.0 878.6 jit_solution(17329085397381359276)
XLA Ops:
  6.5 0.0 copy-start.2
  6.5 0.0 all-gather.3.cloned.1.call-start
  6.5 0.8 copy.27
  7.4 0.6 pad.7.bw_ref
  8.0 4.8 shard_map.154
  12.7 0.0 all-gather.3.cloned.1.call-update
  12.8 0.0 copy-done.2
  12.8 0.2 dynamic-update-slice
  13.0 68.7 %all-reduce.2 = s32[1024]{0:T(1024)S(1)} all-reduce(s32[1024]{0:T(1024)S(1)} %dynamic-update-slice), channel_id=1, replica_groups=mesh['gx'=16,'gy'=8] {'gx','gy'}, use_global_device_ids=true, to_apply=%add.2 | all-reduce | flops 1024 | bytes 8192
  81.7 0.7 convert_reduce_fusion
  83.0 0.0 copy-start
  83.0 1.1 copy.28.refs_6_
  84.1 251.1 %all-gather.3.cloned.1.call-done.refs_7_ = bf16[4,1024,1024]{2,1,0:T(8,128)(2,1)} async-done(((bf16[4,8,1024]{2,1,0:T(8,128)(2,1)}), bf16[4,1024,1024]{2,1,0:T(8,128)(2,1)}) %all-gather.3.cloned.1.call-update) | async-done | bytes 8388624 | tf_op jit(solution)/shard_map/all_gather | solution.py:241
  335.1 0.0 copy-done
  335.1 56.5 %shard_map.155 = bf16[8,1024,128]{2,1,0:T(8,128)(2,1)} custom-call(bf16[8,1024,128]{2,1,0:T(8,128)(2,1)} %refs_0_.1, f32[1,128]{1,0:T(1,128)} %bitcast.33, bf16[128,512]{1,0:T(8,128)(2,1)} %refs_2_.2, f32[1,128]{1,0:T(1,128)} %bitcast.36, bf16[128,128]{1,0:T(8,128)(2,1)} %refs_4_.2, f32[1,1024]{1,0:T(1,128)} %bitcast.29, f32[1024,1]{1,0:T(8,128)} %copy.28.refs_6_, ...), custom_call_target="tpu_custom_call" | custom-call | tf_op jit(solution)/shard_map/pallas_call | solution.py:191
  391.7 4.3 copy.29
  395.9 0.0 copy-start.1
  395.9 8.1 all-to-all-start
  404.0 0.2 all-gather.5.cloned.1.call-start
  404.2 0.0 copy-done.1
  404.2 0.1 copy.31
  404.4 0.6 pad.8.bw_ref
  405.0 29.1 %all-to-all-done = bf16[8,1024,128]{2,0,1:T(8,128)(2,1)S(1)} async-done(((bf16[8,1024,128]{2,0,1:T(8,128)(2,1)}), bf16[8,1024,128]{2,0,1:T(8,128)(2,1)S(1)}, u32[]{:S(2)}, u32[]{:S(2)}) %all-to-all-start) | async-done | bytes 2097184 | tf_op jit(solution)/shard_map/all_to_all | solution.py:245
  434.1 1.7 copy.38
  435.8 4.7 shard_map.156
  440.6 0.0 all-gather.5.cloned.1.call-update
  440.6 316.6 %all-gather.5.cloned.1.call-done.refs_7_ = bf16[4,1024,1024]{2,1,0:T(8,128)(2,1)} async-done(((bf16[4,8,1024]{2,1,0:T(8,128)(2,1)}), bf16[4,1024,1024]{2,1,0:T(8,128)(2,1)}) %all-gather.5.cloned.1.call-update) | async-done | bytes 8388624 | tf_op jit(solution)/shard_map/all_gather | solution.py:248
  757.2 72.7 %shard_map.157 = bf16[8,1024,128]{2,1,0:T(8,128)(2,1)} custom-call(bf16[8,1024,128]{2,1,0:T(8,128)(2,1)} %bitcast.24, f32[1,128]{1,0:T(1,128)} %bitcast.35, bf16[128,512]{1,0:T(8,128)(2,1)} %refs_2_.3, f32[1,128]{1,0:T(1,128)} %bitcast.37, bf16[128,128]{1,0:T(8,128)(2,1)} %refs_4_.3, f32[1,1024]{1,0:T(1,128)} %bitcast.30, f32[1024,1]{1,0:T(8,128)} %copy.28.refs_6_, ...), custom_call_target="tpu_custom_call" | custom-call | tf_op jit(solution)/shard_map/pallas_call | solution.py:191
  829.9 2.9 copy.33
  832.8 37.3 %all_to_all.36 = bf16[1024,8,128]{2,1,0:T(8,128)(2,1)S(1)} all-to-all(bf16[1024,8,128]{2,1,0:T(8,128)(2,1)S(1)} %copy.33), channel_id=1, replica_groups=mesh['gx'=16,'gy'=8] {'gx','gy'}, dimensions={0} | all-to-all | bytes 4194304 | tf_op jit(solution)/shard_map/all_to_all | solution.py:253
  870.1 1.7 copy.37
  (2 shorter events, 0.0 us)
Async XLA Ops:
  6.5 6.2 copy-start.2
  6.5 328.6 %all-gather.3.cloned.1.call-start = ((), (), s32[]{:S(2)}) async-start(), calls=%async_computation.2 | async-start | bytes 8454144 | tf_op jit(solution)/shard_map/all_gather | solution.py:241
  83.0 252.1 %copy-start = (f32[1024]{0:T(1024)}, f32[1024]{0:T(1024)S(1)}, u32[]{:S(2)}) copy-start(f32[1024]{0:T(1024)S(1)} %convert_select_fusion) | copy-start | bytes 12292
  395.9 8.3 copy-start.1
  395.9 38.2 %all-to-all-start = ((bf16[8,1024,128]{2,0,1:T(8,128)(2,1)}), bf16[8,1024,128]{2,0,1:T(8,128)(2,1)S(1)}, u32[]{:S(2)}, u32[]{:S(2)}) async-start(bf16[8,1024,128]{2,0,1:T(8,128)(2,1)} %copy.29), calls=%async_computation | async-start | bytes 4194304 | tf_op jit(solution)/shard_map/all_to_all | solution.py:245
  404.0 353.2 %all-gather.5.cloned.1.call-start = ((), (), s32[]{:S(2)}) async-start(), calls=%async_computation.3 | async-start | bytes 8454144 | tf_op jit(solution)/shard_map/all_gather | solution.py:248
Sparse Core Ops, SparseCore 0:
  12.9 322.2 all-gather.2
  440.7 316.4 all-gather.4

commit v2 on v1

--- a/solution.py
+++ b/solution.py
@@ -44,6 +44,175 @@
         in_specs=[VMEM] * 3,
         out_specs=VMEM,
     )(x, gain, bw)
+
+
+ORDERS = (
+    ("xyz", "yzx", "zxy", "xyz", "yzx"),
+    ("yzx", "zxy", "xyz", "yzx", "xyz"),
+)
+
+
+def place():
+    gx, gy = lax.axis_index("gx"), lax.axis_index("gy")
+    return {
+        "x": lax.rem(gx // 2, 4),
+        "y": gy // 2,
+        "z": 2 * lax.rem(gy, 2) + gx // 8,
+        "c": lax.rem(gx, 2),
+    }
+
+
+def device(at):
+    z_lo, z_hi = lax.rem(at["z"], 2), at["z"] // 2
+    return {"gx": (z_lo * 4 + at["x"]) * 2 + at["c"], "gy": at["y"] * 2 + z_hi}
+
+
+def shift(at, dim, by):
+    return {**at, dim: lax.rem(at[dim] + by + 4, 4)}
+
+
+def part(ref, lead, at, free, tail=()):
+    z = "z" in free
+    pick = lambda d: slice(None) if d in free else at[d]
+    z_lo = slice(None) if z else lax.rem(at["z"], 2)
+    z_hi = slice(None) if z else at["z"] // 2
+    return ref.at[lead + (z_lo, pick("x"), at["c"], pick("y"), z_hi) + tail]
+
+
+def gather_kernel(n_out, *refs):
+    ins, outs = refs[:n_out], refs[n_out : 2 * n_out]
+    ring_send, ring_recv, pair_send, pair_recv, own_sem = refs[2 * n_out :]
+    me = place()
+    barrier = pltpu.get_barrier_semaphore()
+    sib = {**me, "c": 1 - me["c"]}
+    partners = [shift(me, d, by) for d in "xyz" for by in (1, -1)] + [sib]
+    for at in partners:
+        pl.semaphore_signal(barrier, inc=1, device_id=device(at), device_id_type=pl.DeviceIdType.MESH)
+    pl.semaphore_wait(barrier, len(partners))
+
+    def items(core):
+        half = outs[0].shape[-1] // 2
+        got = []
+        for h in range(HEADS):
+            got.append((h, ins[0].at[h], functools.partial(part, outs[0], (h,)), half))
+        if n_out == 2:
+            got.append((HEADS, ins[1], functools.partial(part, outs[1], ()), 0))
+        return got
+
+    def copy(src, dst, sems, idx, to):
+        return pltpu.make_async_remote_copy(
+            src_ref=src, dst_ref=dst, send_sem=sems[0].at[idx], recv_sem=sems[1].at[idx],
+            device_id=device(to), device_id_type=pl.DeviceIdType.MESH,
+        )
+
+    ring, pair = (ring_send, ring_recv), (pair_send, pair_recv)
+
+    def run(core):
+        at = {**me, "c": core}
+        other = {**me, "c": 1 - core}
+        todo = items(core)
+        sends = []
+
+        def step0(p, idx, own, sets, half):
+            d, free = ORDERS[core][idx][p], ORDERS[core][idx][:p]
+            src = sets(at, free)
+            for k, by in enumerate((1, -1)):
+                c = copy(own if p == 0 else src, src, ring, (idx, p, k), shift(at, d, by))
+                c.start()
+                sends.append(c)
+
+        def step1(p, idx, own, sets, half):
+            d, free = ORDERS[core][idx][p], ORDERS[core][idx][:p]
+            for k, by in enumerate((1, -1)):
+                got = sets(shift(at, d, -by), free)
+                copy(got, got, ring, (idx, p, k), shift(at, d, by)).wait_recv()
+                if half:
+                    tail = (slice(None), pl.ds(k * half, half))
+                    piece = sets(shift(at, d, -by), free, tail)
+                elif k == 0:
+                    piece = got
+                else:
+                    continue
+                c = copy(piece, piece, ring, (idx, p, 2 + k), shift(at, d, by))
+                c.start()
+                sends.append(c)
+
+        def step2(p, idx, own, sets, half):
+            d, free = ORDERS[core][idx][p], ORDERS[core][idx][:p]
+            for k, by in enumerate((1, -1)):
+                if half:
+                    tail = (slice(None), pl.ds(k * half, half))
+                    piece = sets(shift(at, d, 2), free, tail)
+                elif k == 0:
+                    piece = sets(shift(at, d, 2), free)
+                else:
+                    continue
+                copy(piece, piece, ring, (idx, p, 2 + k), shift(at, d, by)).wait_recv()
+
+        def across(idx, sets, hop):
+            d, free = ORDERS[core][idx][2], ORDERS[core][idx][:2]
+            piece = sets(shift(at, d, hop), free)
+            c = copy(piece, piece, pair, (idx, hop), other)
+            c.start()
+            sends.append(c)
+
+        own_copies = []
+        for idx, own, sets, half in todo:
+            step0(0, idx, own, sets, half)
+            mine = pltpu.make_async_copy(own, sets(at, ""), own_sem.at[idx])
+            mine.start()
+            own_copies.append(mine)
+        for p in range(3):
+            for t in todo:
+                step1(p, *t)
+                if p == 2:
+                    for hop in (1, 3):
+                        across(t[0], t[2], hop)
+            for i, t in enumerate(todo):
+                if p == 0:
+                    own_copies[i].wait()
+                step2(p, *t)
+                if p < 2:
+                    step0(p + 1, *t)
+                if p == 1:
+                    across(t[0], t[2], 0)
+                if p == 2:
+                    across(t[0], t[2], 2)
+        for idx, own, sets, half in todo:
+            d, free = ORDERS[1 - core][idx][2], ORDERS[1 - core][idx][:2]
+            for hop in range(4):
+                piece = sets(shift(other, d, hop), free)
+                copy(piece, piece, pair, (idx, hop), other).wait_recv()
+        for c in sends:
+            c.wait_send()
+
+    for core in range(2):
+        pl.when(me["c"] == core)(functools.partial(run, core))
+
+
+def gather(cid, bias, *mask):
+    heads, rows, res = bias.shape
+    grid = (2, 4, 2, 4, 2)
+    outs = [jax.ShapeDtypeStruct((heads,) + grid + (rows, res), BF16)]
+    if mask:
+        outs.append(jax.ShapeDtypeStruct(grid + mask[0].shape, F32))
+    n = len(outs)
+    got = pl.pallas_call(
+        functools.partial(gather_kernel, n),
+        out_shape=outs,
+        in_specs=[VMEM] * n,
+        out_specs=[pl.BlockSpec(memory_space=pl.ANY)] * n,
+        scratch_shapes=[
+            pltpu.SemaphoreType.DMA((5, 3, 4)),
+            pltpu.SemaphoreType.DMA((5, 3, 4)),
+            pltpu.SemaphoreType.DMA((5, 4)),
+            pltpu.SemaphoreType.DMA((5, 4)),
+            pltpu.SemaphoreType.DMA((5,)),
+        ],
+        compiler_params=pltpu.CompilerParams(collective_id=cid, has_side_effects=True),
+    )(bias, *mask)
+    full = got[0].reshape(heads, -1, res)
+    return (full, got[1].reshape((-1,) + mask[0].shape)) if mask else full
 
 
 def attn_kernel(trans, *refs):
@@ -233,19 +402,20 @@
     rows, res, chan = pair_in.shape
     axes = ("gx", "gy")
     row = lambda v: v.reshape(1, -1)
-    mask = lax.all_gather(residue_mask, axes, axis=0, tiled=True).astype(F32)
+    mine = jnp.pad(residue_mask.astype(F32).reshape(1, rows), ((0, 7), (0, 128 - rows)))
+    bias = pair_bias(pair_in, row(norm_start), bias_w_start)
+    bias, mask = gather(0, bias, mine)
+    mask = mask[:, 0, :rows].reshape(res)
     mask = jnp.where(jnp.max(mask) > 0.5, mask, 1.0)
     mrow, mcol = mask.reshape(1, res), mask.reshape(res, 1)
 
-    bias = pair_bias(pair_in, row(norm_start), bias_w_start)
-    bias = lax.all_gather(bias, axes, axis=1, tiled=True)
     z1 = attention(
         pair_in, row(norm_start), proj_start, row(gate_bias_start), out_w_start, mrow, mcol, bias
     )
     cols = lax.all_to_all(z1, axes, split_axis=1, concat_axis=0, tiled=True)
     cols = jnp.swapaxes(cols, 0, 1)
     bias = pair_bias(cols, row(norm_end), bias_w_end)
-    bias = lax.all_gather(bias, axes, axis=1, tiled=True)
+    bias = gather(1, bias)
     out = attention(
         cols, row(norm_end), proj_end, row(gate_bias_end), out_w_end, mrow, mcol, bias,
         (row(norm_trans), trans_in, row(trans_bias), trans_out),

time: 880 us -> 308 us (0.35)
  waiting for transfers between devices: 597 us -> 29.8 us
  Pallas kernels: 139 us -> 217 us
  blocking collectives: 106 us -> 35.3 us
  between operations: 14.1 us -> 0.71 us
    all_gather x2 -> x0, waiting for transfers between devices: 568 us -> none  [local(): bias = lax.all_gather(bias, axes, axis=1, tiled=True)]
    pallas_call x0 -> x2, Pallas kernels: none -> 78.6 us  [gather(): pl.pallas_call(functools.partial(gather_kernel, n), out_shape=outs, in_sp...]
    unnamed x1 -> x0, blocking collectives: 68.7 us -> none
  transfers between devices with their start and end apart: 3 -> 1, of which waited for: 3 -> 1; matrix products, arithmetic and copies ran while one was open for 0% -> 0% of each run, Pallas kernels for 0% -> 0%
where the time goes in v2:
time: 308 us; the launch traced here: 307 us
  Pallas kernels  217 us (70%)
  blocking collectives  35.3 us (11%)
  waiting for transfers between devices  29.8 us (10%)
  local copies, waits for them, and re-layouts  16.2 us (5%)
  starting transfers between devices  6.21 us (2%)
    pallas_call x2, Pallas kernels, attention(): pl.pallas_call(functools.partial(attn_kernel, bool(trans)), grid=(res //...  129 us
    pallas_call x2, Pallas kernels, gather(): pl.pallas_call(functools.partial(gather_kernel, n), out_shape=outs, in_sp...  78.6 us
    all_to_all x1, blocking collectives, local(): lax.all_to_all(jnp.swapaxes(out, 0, 1), axes, split_axis=0, concat_axis=1...  35.3 us
    all_to_all x1, waiting for transfers between devices, local(): cols = lax.all_to_all(z1, axes, split_axis=1, concat_axis=0, tiled=True)  29.8 us
    pallas_call x2, Pallas kernels, pair_bias(): pl.pallas_call(bias_kernel, out_shape=jax.ShapeDtypeStruct((HEADS, rows,...  9.5 us
    all_to_all x1, starting transfers between devices, local(): cols = lax.all_to_all(z1, axes, split_axis=1, concat_axis=0, tiled=True)  6.21 us
  transfers between devices with their start and end apart: 1, of which 1 were waited for; matrix products, arithmetic and copies ran while one was open for 0% of the time, Pallas kernels for 0%

profile of v2, /device:TPU:1, one launch (start us, length us, event | category | flops | bytes accessed | tf_op | source)
XLA Modules:
  0.0 306.8 jit_solution(9231533458636296908)
XLA Ops:
  0.0 0.7 convert_bitcast_fusion
  0.7 0.8 copy.29
  1.5 0.6 pad.12.refs_1_
  2.1 0.6 pad.11.bw_ref
  2.7 4.7 %shard_map.154.refs_0_ = bf16[4,8,1024]{2,1,0:T(8,128)(2,1)} custom-call(bf16[8,1024,128]{2,1,0:T(8,128)(2,1)} %refs_0_.1, f32[1,128]{1,0:T(1,128)} %bitcast.42, bf16[128,128]{1,0:T(8,128)(2,1)} %pad.11.bw_ref), custom_call_target="tpu_custom_call" | custom-call | tf_op jit(solution)/shard_map/pallas_call | solution.py:41
  7.4 42.0 %shard_map.155 = (bf16[4,2,4,2,4,2,8,1024]{7,6,5,4,3,2,1,0:T(8,128)(2,1)}, f32[2,4,2,4,2,8,128]{6,5,4,3,2,1,0:T(8,128)}) custom-call(bf16[4,8,1024]{2,1,0:T(8,128)(2,1)} %shard_map.154.refs_0_, f32[8,128]{1,0:T(8,128)} %pad.12.refs_1_), custom_call_target="tpu_custom_call" | custom-call | tf_op jit(solution)/shard_map/pallas_call | solution.py:200
  49.4 1.1 slice.4
  50.5 0.6 reduce_max.9
  51.8 0.7 select_n.30.refs_5_
  52.5 1.0 select_n.32.refs_6_
  53.5 56.5 %shard_map.156 = bf16[8,1024,128]{2,1,0:T(8,128)(2,1)} custom-call(bf16[8,1024,128]{2,1,0:T(8,128)(2,1)} %refs_0_.1, f32[1,128]{1,0:T(1,128)} %bitcast.43, bf16[128,512]{1,0:T(8,128)(2,1)} %refs_2_.2, f32[1,128]{1,0:T(1,128)} %bitcast.46, bf16[128,128]{1,0:T(8,128)(2,1)} %refs_4_.2, f32[1,1024]{1,0:T(1,128)} %select_n.30.refs_5_, ...), custom_call_target="tpu_custom_call" | custom-call | tf_op jit(solution)/shard_map/pallas_call | solution.py:360
  110.0 4.3 %copy.32 = bf16[8,1024,128]{2,0,1:T(8,128)(2,1)} copy(bf16[8,1024,128]{2,1,0:T(8,128)(2,1)} %shard_map.156) | data formatting | bytes 4194304 | tf_op jit(solution)/shard_map/pallas_call | solution.py:360
  114.3 0.0 copy-start
  114.3 6.2 %all-to-all-start = ((bf16[8,1024,128]{2,0,1:T(8,128)(2,1)}), bf16[8,1024,128]{2,0,1:T(8,128)(2,1)S(1)}, u32[]{:S(2)}, u32[]{:S(2)}) async-start(bf16[8,1024,128]{2,0,1:T(8,128)(2,1)} %copy.32), calls=%async_computation | async-start | bytes 4194304 | tf_op jit(solution)/shard_map/all_to_all | solution.py:415
  120.5 0.0 copy-done
  120.5 0.1 copy.34
  120.6 0.6 pad.13.bw_ref
  121.3 29.8 %all-to-all-done = bf16[8,1024,128]{2,0,1:T(8,128)(2,1)S(1)} async-done(((bf16[8,1024,128]{2,0,1:T(8,128)(2,1)}), bf16[8,1024,128]{2,0,1:T(8,128)(2,1)S(1)}, u32[]{:S(2)}, u32[]{:S(2)}) %all-to-all-start) | async-done | bytes 2097184 | tf_op jit(solution)/shard_map/all_to_all | solution.py:415
  151.0 1.7 copy.42
  152.7 4.8 %shard_map.157.refs_0_ = bf16[4,8,1024]{2,1,0:T(8,128)(2,1)} custom-call(bf16[8,1024,128]{2,1,0:T(8,128)(2,1)} %bitcast.32, f32[1,128]{1,0:T(1,128)} %bitcast.44, bf16[128,128]{1,0:T(8,128)(2,1)} %pad.13.bw_ref), custom_call_target="tpu_custom_call" | custom-call | tf_op jit(solution)/shard_map/pallas_call | solution.py:41
  157.5 36.7 %shard_map.158 = bf16[4,2,4,2,4,2,8,1024]{7,6,5,4,3,2,1,0:T(8,128)(2,1)} custom-call(bf16[4,8,1024]{2,1,0:T(8,128)(2,1)} %shard_map.157.refs_0_), custom_call_target="tpu_custom_call" | custom-call | tf_op jit(solution)/shard_map/pallas_call | solution.py:200
  194.2 72.7 %shard_map.159 = bf16[8,1024,128]{2,1,0:T(8,128)(2,1)} custom-call(bf16[8,1024,128]{2,1,0:T(8,128)(2,1)} %bitcast.33, f32[1,128]{1,0:T(1,128)} %bitcast.45, bf16[128,512]{1,0:T(8,128)(2,1)} %refs_2_.3, f32[1,128]{1,0:T(1,128)} %bitcast.47, bf16[128,128]{1,0:T(8,128)(2,1)} %refs_4_.3, f32[1,1024]{1,0:T(1,128)} %select_n.30.refs_5_, ...), custom_call_target="tpu_custom_call" | custom-call | tf_op jit(solution)/shard_map/pallas_call | solution.py:360
  266.9 2.9 copy.36
  269.8 35.3 %all_to_all.36 = bf16[1024,8,128]{2,1,0:T(8,128)(2,1)S(1)} all-to-all(bf16[1024,8,128]{2,1,0:T(8,128)(2,1)S(1)} %copy.36), channel_id=1, replica_groups=mesh['gx'=16,'gy'=8] {'gx','gy'}, dimensions={0} | all-to-all | bytes 4194304 | tf_op jit(solution)/shard_map/all_to_all | solution.py:423
  305.1 1.7 copy.41
  (1 shorter events, 0.0 us)
Async XLA Ops:
  114.3 6.2 %copy-start = (bf16[128,4]{0,1:T(4,128)(2,1)S(1)}, bf16[128,4]{0,1:T(4,128)(2,1)}, u32[]{:S(2)}) copy-start(bf16[128,4]{0,1:T(4,128)(2,1)} %param.26) | copy-start | bytes 3076
  114.3 36.8 %all-to-all-start = ((bf16[8,1024,128]{2,0,1:T(8,128)(2,1)}), bf16[8,1024,128]{2,0,1:T(8,128)(2,1)S(1)}, u32[]{:S(2)}, u32[]{:S(2)}) async-start(bf16[8,1024,128]{2,0,1:T(8,128)(2,1)} %copy.32), calls=%async_computation | async-start | bytes 4194304 | tf_op jit(solution)/shard_map/all_to_all | solution.py:415

commit v3 on v2

--- a/solution.py
+++ b/solution.py
@@ -12,6 +12,7 @@
 LOG2E = 1.4426950408889634
 JB = 256
 KB = 128
+UNROLL = 4
 F32 = jnp.float32
 BF16 = jnp.bfloat16
 NT = (((1,), (1,)), ((), ()))
@@ -20,17 +21,19 @@
 
 
 def layer_norm(t, gain):
-    mean = jnp.mean(t, axis=-1, keepdims=True)
-    cent = t - mean
+    chan = t.shape[1]
+    mean = jnp.dot(t, jnp.full((chan, chan), 1.0 / chan, BF16), preferred_element_type=F32)
+    cent = t.astype(F32) - mean
     var = jnp.mean(cent * cent, axis=-1, keepdims=True)
     return (cent * lax.rsqrt(var + 1e-05) * gain).astype(BF16)
 
 
-def bias_kernel(x_ref, g_ref, bw_ref, o_ref):
+def bias_kernel(x_ref, g_ref, bw_ref, o_ref, a_ref):
     bwt = bw_ref[...].astype(F32).T.astype(BF16)
     gain = g_ref[...]
     for r in range(x_ref.shape[0]):
-        a = layer_norm(x_ref[r].astype(F32), gain)
+        a = layer_norm(x_ref[r], gain)
+        a_ref[r] = a
         b = lax.dot_general(bwt, a, NT, preferred_element_type=F32) * LOG2E
         o_ref[:, r, :] = b[:HEADS].astype(BF16)
 
@@ -40,9 +43,12 @@
     bw = jnp.pad(bias_w, ((0, 0), (0, 128 - HEADS)))
     return pl.pallas_call(
         bias_kernel,
-        out_shape=jax.ShapeDtypeStruct((HEADS, rows, res), BF16),
+        out_shape=[
+            jax.ShapeDtypeStruct((HEADS, rows, res), BF16),
+            jax.ShapeDtypeStruct(x.shape, BF16),
+        ],
         in_specs=[VMEM] * 3,
-        out_specs=VMEM,
+        out_specs=[VMEM] * 2,
     )(x, gain, bw)
 
 
@@ -216,10 +222,10 @@
 
 
 def attn_kernel(trans, *refs):
-    (x_ref, g_ref, w_ref, gb_ref, ow_ref, mrow_ref, mcol_ref, b_ref), refs = refs[:8], refs[8:]
+    (x_ref, a_ref, w_ref, gb_ref, ow_ref, mrow_ref, mcol_ref, b_ref), refs = refs[:8], refs[8:]
     if trans:
         (ng_ref, ti_ref, tb_ref, to_ref), refs = refs[:4], refs[4:]
-    o_ref, km, qs, vx, gt, bt, pp, ot, wk, wq, ss = refs
+    o_ref, km, qs, vx, gt, bt, pa, pb, ot, wk, wq, ss, gd, zz = refs
     rows, res, chan = x_ref.shape
     jb = pl.program_id(0)
     groups = rows // 4
@@ -235,16 +241,15 @@
             wq[s] = (jnp.concatenate([wqt[cut:], wqt[:cut]], axis=0) if s else wqt).astype(BF16)
         wvt = w[:, 2 * chan : 3 * chan].T.astype(BF16)
         wgt = w[:, 3 * chan :].T.astype(BF16)
-        gain = g_ref[...]
         gb = gb_ref[...].T
         mrow = mrow_ref[...]
-        lane = lax.broadcasted_iota(jnp.int32, (res, chan), 1) // HEAD_DIM
+        lane = lax.broadcasted_iota(jnp.int32, (1, chan), 1) // HEAD_DIM
 
         def project(r, carry):
             s = lax.rem(r, 4)
             grp = r // 4
-            a = layer_norm(x_ref[r].astype(F32), gain)
-            kk = jnp.dot(a, wk[s], preferred_element_type=F32)
+            a = a_ref[r]
+            kk = jnp.dot(a, wk[s], preferred_element_type=F32).astype(BF16)
             qt = (
                 lax.dot_general(wq[s], a, NT, preferred_element_type=F32)
                 * (HEAD_DIM**-0.5 * LOG2E)
@@ -253,7 +258,7 @@
             gt[r] = jax.nn.sigmoid(lax.dot_general(wgt, a, NT, preferred_element_type=F32) + gb)
             for h in range(HEADS):
                 slot = lax.rem(h + s, 4)
-                km[r, h] = jnp.where(lane == slot, kk, 0.0).astype(BF16)
+                km[r, h] = kk * (lane == slot).astype(F32).astype(BF16)
                 vx[r, h, :HEAD_DIM] = vt[HEAD_DIM * h : HEAD_DIM * (h + 1)].astype(BF16)
                 vx[r, h, HEAD_DIM:] = jnp.broadcast_to(mrow, (16, res)).astype(BF16)
             for t in range(4):
@@ -263,75 +268,37 @@
 
         lax.fori_loop(0, rows, project, 0)
 
-    for h in range(HEADS):
-        for kb in range(nk):
-            sl = slice(KB * kb, KB * (kb + 1))
-            bt[h, sl] = b_ref[h, :, sl].T
-
     eye = (
         lax.broadcasted_iota(jnp.int32, (KB, KB), 0) == lax.broadcasted_iota(jnp.int32, (KB, KB), 1)
     ).astype(F32).astype(BF16)
     joff = pl.multiple_of(jb * JB, JB)
-
-    def head_body(it, carry):
-        grp = it // HEADS
-        h = lax.rem(it, HEADS)
-        q = qs[grp, h, :, pl.ds(joff, JB)]
-        for kb in range(nk):
-            sl = slice(KB * kb, KB * (kb + 1))
-            rhs = jnp.concatenate([bt[h, sl], q], axis=0)
-            lhs = jnp.concatenate(
-                [jnp.concatenate([eye, km[grp * 4 + r, h, sl]], axis=1) for r in range(4)], axis=0
-            )
-            s4 = jnp.dot(lhs, rhs, preferred_element_type=F32)
-            p4 = jnp.exp2(s4).astype(BF16)
-            for r in range(4):
-                pp[r, sl] = p4[KB * r : KB * (r + 1)]
-        good = None
+    tasks = groups * HEADS
+
+    def of(t):
+        return t // HEADS, lax.rem(t, HEADS)
+
+    def head_slice(h):
+        return pl.ds(pl.multiple_of(HEAD_DIM * h, HEAD_DIM), HEAD_DIM)
+
+    def weights_step(t, kb, pp):
+        grp, h = of(t)
+        sl = slice(KB * kb, KB * (kb + 1))
+        rhs = jnp.concatenate([bt[h, sl], qs[grp, h, :, pl.ds(joff, JB)]], axis=0)
+        lhs = jnp.concatenate(
+            [jnp.concatenate([eye, km[grp * 4 + r, h, sl]], axis=1) for r in range(4)], axis=0
+        )
+        p4 = jnp.exp2(jnp.dot(lhs, rhs, preferred_element_type=F32)).astype(BF16)
         for r in range(4):
-            oe = jnp.dot(vx[grp * 4 + r, h], pp[r], preferred_element_type=F32)
-            den = oe[HEAD_DIM : HEAD_DIM + 1]
-            fine = (den > 2.0**-60) & (den < 2.0**100)
-            good = fine if good is None else good & fine
-            ot[grp * 4 + r, pl.ds(pl.multiple_of(HEAD_DIM * h, HEAD_DIM), HEAD_DIM)] = (
-                oe[:HEAD_DIM] / den
-            )
-
-        @pl.when(jnp.min(good.astype(F32)) < 0.5)
-        def _():
-            def slow_row(r, carry):
-                row = grp * 4 + r
-
-                def scores(kb, carry):
-                    ks = pl.ds(pl.multiple_of(kb * KB, KB), KB)
-                    rhs = jnp.concatenate([bt[h, ks], q], axis=0)
-                    lhs = jnp.concatenate([eye, km[row, h, ks]], axis=1)
-                    s1 = jnp.dot(lhs, rhs, preferred_element_type=F32)
-                    s1 = jnp.where(mcol_ref[ks] > 0.5, s1, -1e30)
-                    ss[ks] = s1
-                    return jnp.maximum(carry, jnp.max(s1, axis=0, keepdims=True))
-
-                top = lax.fori_loop(0, nk, scores, jnp.full((1, JB), -1e30, F32))
-
-                def weights(kb, carry):
-                    ks = pl.ds(pl.multiple_of(kb * KB, KB), KB)
-                    pp[0, ks] = jnp.exp2(ss[ks] - top).astype(BF16)
-                    return carry
-
-                lax.fori_loop(0, nk, weights, 0)
-                oe = jnp.dot(vx[row, h], pp[0], preferred_element_type=F32)
-                ot[row, pl.ds(pl.multiple_of(HEAD_DIM * h, HEAD_DIM), HEAD_DIM)] = (
-                    oe[:HEAD_DIM] / oe[HEAD_DIM : HEAD_DIM + 1]
-                )
-                return carry
-
-            lax.fori_loop(0, 4, slow_row, 0)
-
-        return carry
-
-    lax.fori_loop(0, groups * HEADS, head_body, 0)
-
-    def finish(r, carry):
+            pp[r, sl] = p4[KB * r : KB * (r + 1)]
+
+    def mix_step(t, r, pp):
+        grp, h = of(t)
+        oe = jnp.dot(vx[grp * 4 + r, h], pp[r], preferred_element_type=F32)
+        den = oe[HEAD_DIM : HEAD_DIM + 1]
+        gd[...] = jnp.where((den > 2.0**-60) & (den < 2.0**100), gd[...], 0.0)
+        ot[grp * 4 + r, head_slice(h)] = oe[:HEAD_DIM] / den
+
+    def finish(r):
         gated = (ot[r] * gt[r, :, pl.ds(joff, JB)]).T.astype(BF16)
         z = x_ref[r, pl.ds(joff, JB)].astype(F32) + jnp.dot(
             gated, ow_ref[...], preferred_element_type=F32
@@ -339,30 +306,101 @@
         z = z.astype(BF16)
         if trans:
             zf = z.astype(F32)
-            a = layer_norm(zf, ng_ref[...])
+            a = layer_norm(z, ng_ref[...])
             hid = jnp.dot(a, ti_ref[...], preferred_element_type=F32) + tb_ref[...]
             hid = jnp.maximum(hid, 0.0).astype(BF16)
             z = (zf + jnp.dot(hid, to_ref[...], preferred_element_type=F32)).astype(BF16)
-        o_ref[r] = z
+        zz[r] = z
+
+    def both(t, new, old):
+        for kb in range(nk):
+            weights_step(t, kb, new)
+            if kb % 2:
+                mix_step(t - 1, kb // 2, old)
+
+    for h in range(HEADS):
+        for kb in range(nk):
+            sl = slice(KB * kb, KB * (kb + 1))
+            bt[h, sl] = b_ref[h, :, sl].T
+    gd[...] = jnp.ones_like(gd)
+    for kb in range(nk):
+        weights_step(0, kb, pa)
+
+    def pair(i, carry):
+        both(2 * i + 1, pb, pa)
+        both(2 * i + 2, pa, pb)
         return carry
 
-    lax.fori_loop(0, rows, finish, 0)
-
-
-def attention(x, gain, proj, gate_bias, out_w, mrow, mcol, bias, trans=()):
+    lax.fori_loop(0, tasks // 2 - 1, pair, 0)
+    both(tasks - 1, pb, pa)
+    for r in range(4):
+        mix_step(tasks - 1, r, pb)
+
+    @pl.when(jnp.min(gd[...]) < 0.5)
+    def _():
+        def slow(it, carry):
+            row, h = it // HEADS, lax.rem(it, HEADS)
+            q = qs[row // 4, h, :, pl.ds(joff, JB)]
+
+            def scores(kb, carry):
+                ks = pl.ds(pl.multiple_of(kb * KB, KB), KB)
+                rhs = jnp.concatenate([bt[h, ks], q], axis=0)
+                lhs = jnp.concatenate([eye, km[row, h, ks]], axis=1)
+                s1 = jnp.dot(lhs, rhs, preferred_element_type=F32)
+                s1 = jnp.where(mcol_ref[ks] > 0.5, s1, -1e30)
+                ss[ks] = s1
+                return jnp.maximum(carry, jnp.max(s1, axis=0, keepdims=True))
+
+            top = lax.fori_loop(0, nk, scores, jnp.full((1, JB), -1e30, F32))
+
+            def weights(kb, carry):
+                ks = pl.ds(pl.multiple_of(kb * KB, KB), KB)
+                pa[0, ks] = jnp.exp2(ss[ks] - top).astype(BF16)
+                return carry
+
+            lax.fori_loop(0, nk, weights, 0)
+            oe = jnp.dot(vx[row, h], pa[0], preferred_element_type=F32)
+            ot[row, head_slice(h)] = oe[:HEAD_DIM] / oe[HEAD_DIM : HEAD_DIM + 1]
+            return carry
+
+        lax.fori_loop(0, rows * HEADS, slow, 0)
+
+    def last(i, carry):
+        for r in range(UNROLL):
+            finish(UNROLL * i + r)
+        return carry
+
+    lax.fori_loop(0, rows // UNROLL, last, 0)
+
+    span = JB // rows
+    out_row = lax.broadcasted_iota(jnp.int32, (JB, JB), 0)
+    in_row = lax.broadcasted_iota(jnp.int32, (JB, JB), 1)
+    perm = (in_row == lax.rem(out_row, rows) * span + out_row // rows).astype(F32).astype(BF16)
+    for q in range(rows // 2):
+        cols = [
+            jnp.concatenate([zz[r, span * n : span * (n + 1)] for r in range(rows)], axis=0)
+            for n in (2 * q, 2 * q + 1)
+        ]
+        moved = jnp.dot(perm, jnp.concatenate(cols, axis=1), preferred_element_type=F32).astype(BF16)
+        o_ref[2 * JB * q : 2 * JB * q + JB] = moved[:, :chan]
+        o_ref[2 * JB * q + JB : 2 * JB * (q + 1)] = moved[:, chan:]
+
+
+def attention(x, a, proj, gate_bias, out_w, mrow, mcol, bias, trans=()):
     rows, res, chan = x.shape
+    nj = res // JB
     full = lambda a: pl.BlockSpec(a.shape, lambda j, n=a.ndim: (0,) * n)
-    ins = [x, gain, proj, gate_bias, out_w, mrow, mcol]
+    ins = [x, a, proj, gate_bias, out_w, mrow, mcol]
     specs = [full(a) for a in ins] + [pl.BlockSpec((HEADS, JB, res), lambda j: (0, j, 0))]
     ins.append(bias)
     ins += trans
     specs += [full(a) for a in trans]
     return pl.pallas_call(
         functools.partial(attn_kernel, bool(trans)),
-        grid=(res // JB,),
-        out_shape=jax.ShapeDtypeStruct((rows, res, chan), BF16),
+        grid=(nj,),
+        out_shape=jax.ShapeDtypeStruct((res * rows, chan), BF16),
         in_specs=specs,
-        out_specs=pl.BlockSpec((rows, JB, chan), lambda j: (0, j, 0)),
+        out_specs=pl.BlockSpec((JB * rows, chan), lambda j: (j, 0)),
         scratch_shapes=[
             pltpu.VMEM((rows, HEADS, res, chan), BF16),
             pltpu.VMEM((rows // 4, HEADS, chan, res), BF16),
@@ -370,15 +408,76 @@
             pltpu.VMEM((rows, chan, res), F32),
             pltpu.VMEM((HEADS, res, JB), BF16),
             pltpu.VMEM((4, res, JB), BF16),
+            pltpu.VMEM((4, res, JB), BF16),
             pltpu.VMEM((rows, chan, JB), F32),
             pltpu.VMEM((4, chan, chan), BF16),
             pltpu.VMEM((4, chan, chan), BF16),
             pltpu.VMEM((res, JB), F32),
+            pltpu.VMEM((1, JB), F32),
+            pltpu.VMEM((rows, JB, chan), BF16),
         ],
         compiler_params=pltpu.CompilerParams(
             dimension_semantics=("arbitrary",), vmem_limit_bytes=60 * 1024 * 1024
         ),
     )(*ins)
+
+
+def exchange_kernel(n, z_ref, o_ref, send_sem, recv_sem, own_sem):
+    rows = o_ref.shape[0]
+    gy = n // 16
+    me = lax.axis_index("gx") * gy + lax.axis_index("gy")
+    at = lambda d: {"gx": d // gy, "gy": lax.rem(d, gy)}
+    barrier = pltpu.get_barrier_semaphore()
+
+    def greet(t, carry):
+        pl.semaphore_signal(
+            barrier, inc=1, device_id=at(lax.rem(me + t, n)), device_id_type=pl.DeviceIdType.MESH
+        )
+        return carry
+
+    lax.fori_loop(1, n, greet, 0)
+    mine = pl.ds(pl.multiple_of(rows * me, rows), rows)
+    own = pltpu.make_async_copy(z_ref.at[mine], o_ref.at[:, mine], own_sem)
+    own.start()
+    pl.semaphore_wait(barrier, n - 1)
+
+    def copy(t, to, frm):
+        return pltpu.make_async_remote_copy(
+            src_ref=z_ref.at[pl.ds(pl.multiple_of(rows * to, rows), rows)],
+            dst_ref=o_ref.at[:, pl.ds(pl.multiple_of(rows * frm, rows), rows)],
+            send_sem=send_sem.at[t], recv_sem=recv_sem.at[t],
+            device_id=at(to), device_id_type=pl.DeviceIdType.MESH,
+        )
+
+    def send(t, carry):
+        copy(t, lax.rem(me + t, n), me).start()
+        return carry
+
+    lax.fori_loop(1, n, send, 0)
+    own.wait()
+
+    def land(t, carry):
+        copy(t, lax.rem(me + t, n), lax.rem(me + n - t, n)).wait_recv()
+        copy(t, lax.rem(me + t, n), me).wait_send()
+        return carry
+
+    lax.fori_loop(1, n, land, 0)
+
+
+def exchange(cid, n, z, rows):
+    res = z.shape[0] // rows
+    return pl.pallas_call(
+        functools.partial(exchange_kernel, n),
+        out_shape=jax.ShapeDtypeStruct((rows, res, z.shape[1]), BF16),
+        in_specs=[pl.BlockSpec(memory_space=pl.ANY)],
+        out_specs=pl.BlockSpec(memory_space=pl.ANY),
+        scratch_shapes=[
+            pltpu.SemaphoreType.DMA((n,)),
+            pltpu.SemaphoreType.DMA((n,)),
+            pltpu.SemaphoreType.DMA,
+        ],
+        compiler_params=pltpu.CompilerParams(collective_id=cid, has_side_effects=True),
+    )(z.reshape(res, rows, z.shape[1]))
 
 
 def local(
@@ -400,28 +499,26 @@
     trans_out,
 ):
     rows, res, chan = pair_in.shape
-    axes = ("gx", "gy")
+    n = lax.axis_size(("gx", "gy"))
     row = lambda v: v.reshape(1, -1)
     mine = jnp.pad(residue_mask.astype(F32).reshape(1, rows), ((0, 7), (0, 128 - rows)))
-    bias = pair_bias(pair_in, row(norm_start), bias_w_start)
+    bias, normed = pair_bias(pair_in, row(norm_start), bias_w_start)
     bias, mask = gather(0, bias, mine)
     mask = mask[:, 0, :rows].reshape(res)
     mask = jnp.where(jnp.max(mask) > 0.5, mask, 1.0)
     mrow, mcol = mask.reshape(1, res), mask.reshape(res, 1)
 
     z1 = attention(
-        pair_in, row(norm_start), proj_start, row(gate_bias_start), out_w_start, mrow, mcol, bias
+        pair_in, normed, proj_start, row(gate_bias_start), out_w_start, mrow, mcol, bias
     )
-    cols = lax.all_to_all(z1, axes, split_axis=1, concat_axis=0, tiled=True)
-    cols = jnp.swapaxes(cols, 0, 1)
-    bias = pair_bias(cols, row(norm_end), bias_w_end)
+    cols = exchange(2, n, z1, rows)
+    bias, normed = pair_bias(cols, row(norm_end), bias_w_end)
     bias = gather(1, bias)
     out = attention(
-        cols, row(norm_end), proj_end, row(gate_bias_end), out_w_end, mrow, mcol, bias,
+        cols, normed, proj_end, row(gate_bias_end), out_w_end, mrow, mcol, bias,
         (row(norm_trans), trans_in, row(trans_bias), trans_out),
     )
-    out = lax.all_to_all(jnp.swapaxes(out, 0, 1), axes, split_axis=0, concat_axis=1, tiled=True)
-    return out
+    return exchange(3, n, out, rows)
 
 
 def solution(mesh):

time: 308 us -> 277 us (0.90)
  Pallas kernels: 217 us -> 265 us
  blocking collectives: 35.3 us -> 0 us
  waiting for transfers between devices: 29.8 us -> 0 us
  local copies, waits for them, and re-layouts: 16.2 us -> 9.3 us
  starting transfers between devices: 6.21 us -> 0 us
    pallas_call x4 -> x6, Pallas kernels: 139 us -> 185 us  [the longest x2 105 us: attention(): pl.pallas_call(functools.partial(attn_kernel, bool(trans)), grid=(nj,), o...]
    all_to_all x1 -> x0, blocking collectives: 35.3 us -> none  [local(): lax.all_to_all(jnp.swapaxes(out, 0, 1), axes, split_axis=0, concat_axis=1...]
    all_to_all x1 -> x0, waiting for transfers between devices: 29.8 us -> none  [local(): cols = lax.all_to_all(z1, axes, split_axis=1, concat_axis=0, tiled=True)]
    all_to_all x1 -> x0, starting transfers between devices: 6.21 us -> none  [local(): cols = lax.all_to_all(z1, axes, split_axis=1, concat_axis=0, tiled=True)]
    pallas_call x1 -> x0, local copies, waits for them, and re-layouts: 4.28 us -> none  [attention(): pl.pallas_call(functools.partial(attn_kernel, bool(trans)), grid=(res //...]
    unnamed x4 -> x3, local copies, waits for them, and re-layouts: 0.95 us -> 4.68 us
    all_to_all x2 -> x0, local copies, waits for them, and re-layouts: 3.4 us -> none  [the longest x1 1.7 us: local(): cols = lax.all_to_all(z1, axes, split_axis=1, concat_axis=0, tiled=True)]
  transfers between devices with their start and end apart: 1 -> 0, of which waited for: 1 -> 0; matrix products, arithmetic and copies ran while one was open for 0% -> 0% of each run, Pallas kernels for 0% -> 0%
where the time goes in v3:
time: 277 us
  Pallas kernels  265 us (96%)
  local copies, waits for them, and re-layouts  9.3 us (3%)
    pallas_call x2, Pallas kernels, attention(): pl.pallas_call(functools.partial(attn_kernel, bool(trans)), grid=(nj,), o...  105 us
    pallas_call x2, Pallas kernels, gather(): pl.pallas_call(functools.partial(gather_kernel, n), out_shape=outs, in_sp...  80.2 us
    pallas_call x2, Pallas kernels, exchange(): pl.pallas_call(functools.partial(exchange_kernel, n), out_shape=jax.Shape...  71.7 us
    pallas_call x2, Pallas kernels, pair_bias(): pl.pallas_call(bias_kernel, out_shape=[jax.ShapeDtypeStruct((HEADS, rows,...  8.92 us

profile of v3, /device:TPU:1, one launch (start us, length us, event | category | flops | bytes accessed | tf_op | source)
XLA Modules:
  0.0 276.7 jit_solution(4936379207661999594)
XLA Ops:
  0.0 0.7 convert_bitcast_fusion
  0.7 0.6 pad.12.refs_1_
  1.3 0.8 copy.20
  2.1 0.6 pad.11.bw_ref
  2.7 0.8 copy.23
  3.5 0.6 pad.13.bw_ref
  4.1 4.5 %shard_map.154 = (bf16[4,8,1024]{2,1,0:T(8,128)(2,1)}, bf16[8,1024,128]{2,1,0:T(8,128)(2,1)}) custom-call(bf16[8,1024,128]{2,1,0:T(8,128)(2,1)} %refs_0_.1, f32[1,128]{1,0:T(1,128)} %bitcast.29, bf16[128,128]{1,0:T(8,128)(2,1)} %pad.11.bw_ref), custom_call_target="tpu_custom_call" | custom-call | tf_op jit(solution)/shard_map/pallas_call | solution.py:44
  8.6 42.1 %shard_map.155 = (bf16[4,2,4,2,4,2,8,1024]{7,6,5,4,3,2,1,0:T(8,128)(2,1)}, f32[2,4,2,4,2,8,128]{6,5,4,3,2,1,0:T(8,128)}) custom-call(bf16[4,8,1024]{2,1,0:T(8,128)(2,1)} %get-tuple-element.12.refs_0_, f32[8,128]{1,0:T(8,128)} %pad.12.refs_1_), custom_call_target="tpu_custom_call" | custom-call | tf_op jit(solution)/shard_map/pallas_call | solution.py:206
  50.7 1.1 slice.4
  51.8 0.6 reduce_max.9
  53.1 0.7 select_n.30.refs_5_
  53.8 1.0 select_n.32.refs_6_
  54.8 44.0 %shard_map.156 = bf16[8192,128]{1,0:T(8,128)(2,1)} custom-call(bf16[8,1024,128]{2,1,0:T(8,128)(2,1)} %refs_0_.1, bf16[8,1024,128]{2,1,0:T(8,128)(2,1)} %get-tuple-element.11.refs_1_, bf16[128,512]{1,0:T(8,128)(2,1)} %refs_2_.2, f32[1,128]{1,0:T(1,128)} %bitcast.26, bf16[128,128]{1,0:T(8,128)(2,1)} %refs_4_.2, f32[1,1024]{1,0:T(1,128)} %select_n.30.refs_5_, ...), custom_call_target="tpu_custom_call" | custom-call | tf_op jit(solution)/shard_map/pallas_call | solution.py:398
  98.8 35.4 %shard_map.157.x_ref.refs_0_ = bf16[8,1024,128]{2,1,0:T(8,128)(2,1)} custom-call(bf16[1024,8,128]{2,1,0:T(8,128)(2,1)} %bitcast.21), custom_call_target="tpu_custom_call" | custom-call | tf_op jit(solution)/shard_map/pallas_call | solution.py:469
  134.1 4.5 %shard_map.158 = (bf16[4,8,1024]{2,1,0:T(8,128)(2,1)}, bf16[8,1024,128]{2,1,0:T(8,128)(2,1)}) custom-call(bf16[8,1024,128]{2,1,0:T(8,128)(2,1)} %shard_map.157.x_ref.refs_0_, f32[1,128]{1,0:T(1,128)} %bitcast.30, bf16[128,128]{1,0:T(8,128)(2,1)} %pad.13.bw_ref), custom_call_target="tpu_custom_call" | custom-call | tf_op jit(solution)/shard_map/pallas_call | solution.py:44
  138.6 38.0 %shard_map.159 = bf16[4,2,4,2,4,2,8,1024]{7,6,5,4,3,2,1,0:T(8,128)(2,1)} custom-call(bf16[4,8,1024]{2,1,0:T(8,128)(2,1)} %get-tuple-element.16.refs_0_), custom_call_target="tpu_custom_call" | custom-call | tf_op jit(solution)/shard_map/pallas_call | solution.py:206
  176.6 60.7 %shard_map.160 = bf16[8192,128]{1,0:T(8,128)(2,1)} custom-call(bf16[8,1024,128]{2,1,0:T(8,128)(2,1)} %shard_map.157.x_ref.refs_0_, bf16[8,1024,128]{2,1,0:T(8,128)(2,1)} %get-tuple-element.15.refs_1_, bf16[128,512]{1,0:T(8,128)(2,1)} %refs_2_.3, f32[1,128]{1,0:T(1,128)} %bitcast.27, bf16[128,128]{1,0:T(8,128)(2,1)} %refs_4_.3, f32[1,1024]{1,0:T(1,128)} %select_n.30.refs_5_, ...), custom_call_target="tpu_custom_call" | custom-call | tf_op jit(solution)/shard_map/pallas_call | solution.py:398
  237.3 36.4 %shard_map.161 = bf16[8,1024,128]{2,1,0:T(8,128)(2,1)} custom-call(bf16[1024,8,128]{2,1,0:T(8,128)(2,1)} %bitcast.20), custom_call_target="tpu_custom_call" | custom-call | tf_op jit(solution)/shard_map/pallas_call | solution.py:469
  273.7 3.1 %copy.27 = bf16[8,1024,128]{2,1,0:T(8,128)(2,1)} copy(bf16[8,1024,128]{2,1,0:T(8,128)(2,1)} %shard_map.161) | data formatting | bytes 4194304
  (1 shorter events, 0.0 us)

commit v4 on v3

--- a/solution.py
+++ b/solution.py
@@ -1,4 +1,5 @@
 import functools
+import types
 
 import jax
 import jax.numpy as jnp
@@ -221,205 +222,431 @@
     return (full, got[1].reshape((-1,) + mask[0].shape)) if mask else full
 
 
-def attn_kernel(trans, *refs):
-    (x_ref, a_ref, w_ref, gb_ref, ow_ref, mrow_ref, mcol_ref, b_ref), refs = refs[:8], refs[8:]
-    if trans:
-        (ng_ref, ti_ref, tb_ref, to_ref), refs = refs[:4], refs[4:]
-    o_ref, km, qs, vx, gt, bt, pa, pb, ot, wk, wq, ss, gd, zz = refs
-    rows, res, chan = x_ref.shape
-    jb = pl.program_id(0)
+def stage_tools(trans, m):
+    rows, res, chan = m.x.shape
     groups = rows // 4
     nk = res // KB
-
-    @pl.when(jb == 0)
-    def _():
-        w = w_ref[...].astype(F32)
+    tasks = groups * HEADS
+    t = types.SimpleNamespace()
+
+    def eye():
+        i = lax.broadcasted_iota(jnp.int32, (KB, KB), 0)
+        j = lax.broadcasted_iota(jnp.int32, (KB, KB), 1)
+        return (i == j).astype(F32).astype(BF16)
+
+    def project_all():
+        w = m.w[...].astype(F32)
         wqt = w[:, :chan].T
         for s in range(4):
             cut = chan - 32 * s
-            wk[s] = (pltpu.roll(w[:, chan : 2 * chan], 32 * s, 1) if s else w[:, chan : 2 * chan]).astype(BF16)
-            wq[s] = (jnp.concatenate([wqt[cut:], wqt[:cut]], axis=0) if s else wqt).astype(BF16)
+            wk = w[:, chan : 2 * chan]
+            m.wk[s] = (pltpu.roll(wk, 32 * s, 1) if s else wk).astype(BF16)
+            m.wq[s] = (jnp.concatenate([wqt[cut:], wqt[:cut]], axis=0) if s else wqt).astype(BF16)
         wvt = w[:, 2 * chan : 3 * chan].T.astype(BF16)
         wgt = w[:, 3 * chan :].T.astype(BF16)
-        gb = gb_ref[...].T
-        mrow = mrow_ref[...]
+        gb = m.gb[...].T
+        mrow = m.mrow[...]
         lane = lax.broadcasted_iota(jnp.int32, (1, chan), 1) // HEAD_DIM
 
         def project(r, carry):
             s = lax.rem(r, 4)
             grp = r // 4
-            a = a_ref[r]
-            kk = jnp.dot(a, wk[s], preferred_element_type=F32).astype(BF16)
+            a = m.a[r]
+            kk = jnp.dot(a, m.wk[s], preferred_element_type=F32).astype(BF16)
             qt = (
-                lax.dot_general(wq[s], a, NT, preferred_element_type=F32)
+                lax.dot_general(m.wq[s], a, NT, preferred_element_type=F32)
                 * (HEAD_DIM**-0.5 * LOG2E)
             ).astype(BF16)
             vt = lax.dot_general(wvt, a, NT, preferred_element_type=F32) * mrow
-            gt[r] = jax.nn.sigmoid(lax.dot_general(wgt, a, NT, preferred_element_type=F32) + gb)
+            m.gt[r] = jax.nn.sigmoid(lax.dot_general(wgt, a, NT, preferred_element_type=F32) + gb)
             for h in range(HEADS):
                 slot = lax.rem(h + s, 4)
-                km[r, h] = kk * (lane == slot).astype(F32).astype(BF16)
-                vx[r, h, :HEAD_DIM] = vt[HEAD_DIM * h : HEAD_DIM * (h + 1)].astype(BF16)
-                vx[r, h, HEAD_DIM:] = jnp.broadcast_to(mrow, (16, res)).astype(BF16)
-            for t in range(4):
-                hh = lax.rem(t - s + 4, 4)
-                qs[grp, hh, pl.ds(32 * t, 32)] = qt[32 * t : 32 * (t + 1)]
+                m.km[r, h] = kk * (lane == slot).astype(F32).astype(BF16)
+                m.vx[r, h, :HEAD_DIM] = vt[HEAD_DIM * h : HEAD_DIM * (h + 1)].astype(BF16)
+                m.vx[r, h, HEAD_DIM:] = jnp.broadcast_to(mrow, (16, res)).astype(BF16)
+            for u in range(4):
+                hh = lax.rem(u - s + 4, 4)
+                m.qs[grp, hh, pl.ds(32 * u, 32)] = qt[32 * u : 32 * (u + 1)]
             return carry
 
         lax.fori_loop(0, rows, project, 0)
 
-    eye = (
-        lax.broadcasted_iota(jnp.int32, (KB, KB), 0) == lax.broadcasted_iota(jnp.int32, (KB, KB), 1)
-    ).astype(F32).astype(BF16)
-    joff = pl.multiple_of(jb * JB, JB)
-    tasks = groups * HEADS
-
-    def of(t):
-        return t // HEADS, lax.rem(t, HEADS)
+    def turn_bias(b_ref):
+        for h in range(HEADS):
+            for kb in range(nk):
+                sl = slice(KB * kb, KB * (kb + 1))
+                m.bt[h, sl] = b_ref[h, :, sl].T
 
     def head_slice(h):
         return pl.ds(pl.multiple_of(HEAD_DIM * h, HEAD_DIM), HEAD_DIM)
 
-    def weights_step(t, kb, pp):
-        grp, h = of(t)
-        sl = slice(KB * kb, KB * (kb + 1))
-        rhs = jnp.concatenate([bt[h, sl], qs[grp, h, :, pl.ds(joff, JB)]], axis=0)
-        lhs = jnp.concatenate(
-            [jnp.concatenate([eye, km[grp * 4 + r, h, sl]], axis=1) for r in range(4)], axis=0
-        )
-        p4 = jnp.exp2(jnp.dot(lhs, rhs, preferred_element_type=F32)).astype(BF16)
+    def fast_heads(joff):
+        one = eye()
+
+        def of(k):
+            return k // HEADS, lax.rem(k, HEADS)
+
+        def weights_step(k, kb, pp):
+            grp, h = of(k)
+            sl = slice(KB * kb, KB * (kb + 1))
+            rhs = jnp.concatenate([m.bt[h, sl], m.qs[grp, h, :, pl.ds(joff, JB)]], axis=0)
+            lhs = jnp.concatenate(
+                [jnp.concatenate([one, m.km[grp * 4 + r, h, sl]], axis=1) for r in range(4)], axis=0
+            )
+            p4 = jnp.exp2(jnp.dot(lhs, rhs, preferred_element_type=F32)).astype(BF16)
+            for r in range(4):
+                pp[r, sl] = p4[KB * r : KB * (r + 1)]
+
+        def mix_step(k, r, pp):
+            grp, h = of(k)
+            oe = jnp.dot(m.vx[grp * 4 + r, h], pp[r], preferred_element_type=F32)
+            den = oe[HEAD_DIM : HEAD_DIM + 1]
+            m.gd[...] = jnp.where((den > 2.0**-60) & (den < 2.0**100), m.gd[...], 0.0)
+            m.ot[grp * 4 + r, head_slice(h)] = oe[:HEAD_DIM] / den
+
+        def both(k, new, old):
+            for kb in range(nk):
+                weights_step(k, kb, new)
+                if kb % 2:
+                    mix_step(k - 1, kb // 2, old)
+
+        for kb in range(nk):
+            weights_step(0, kb, m.pa)
+
+        def pair(i, carry):
+            both(2 * i + 1, m.pb, m.pa)
+            both(2 * i + 2, m.pa, m.pb)
+            return carry
+
+        lax.fori_loop(0, tasks // 2 - 1, pair, 0)
+        both(tasks - 1, m.pb, m.pa)
         for r in range(4):
-            pp[r, sl] = p4[KB * r : KB * (r + 1)]
-
-    def mix_step(t, r, pp):
-        grp, h = of(t)
-        oe = jnp.dot(vx[grp * 4 + r, h], pp[r], preferred_element_type=F32)
-        den = oe[HEAD_DIM : HEAD_DIM + 1]
-        gd[...] = jnp.where((den > 2.0**-60) & (den < 2.0**100), gd[...], 0.0)
-        ot[grp * 4 + r, head_slice(h)] = oe[:HEAD_DIM] / den
-
-    def finish(r):
-        gated = (ot[r] * gt[r, :, pl.ds(joff, JB)]).T.astype(BF16)
-        z = x_ref[r, pl.ds(joff, JB)].astype(F32) + jnp.dot(
-            gated, ow_ref[...], preferred_element_type=F32
-        )
-        z = z.astype(BF16)
-        if trans:
-            zf = z.astype(F32)
-            a = layer_norm(z, ng_ref[...])
-            hid = jnp.dot(a, ti_ref[...], preferred_element_type=F32) + tb_ref[...]
-            hid = jnp.maximum(hid, 0.0).astype(BF16)
-            z = (zf + jnp.dot(hid, to_ref[...], preferred_element_type=F32)).astype(BF16)
-        zz[r] = z
-
-    def both(t, new, old):
-        for kb in range(nk):
-            weights_step(t, kb, new)
-            if kb % 2:
-                mix_step(t - 1, kb // 2, old)
-
-    for h in range(HEADS):
-        for kb in range(nk):
-            sl = slice(KB * kb, KB * (kb + 1))
-            bt[h, sl] = b_ref[h, :, sl].T
-    gd[...] = jnp.ones_like(gd)
-    for kb in range(nk):
-        weights_step(0, kb, pa)
-
-    def pair(i, carry):
-        both(2 * i + 1, pb, pa)
-        both(2 * i + 2, pa, pb)
-        return carry
-
-    lax.fori_loop(0, tasks // 2 - 1, pair, 0)
-    both(tasks - 1, pb, pa)
-    for r in range(4):
-        mix_step(tasks - 1, r, pb)
-
-    @pl.when(jnp.min(gd[...]) < 0.5)
-    def _():
-        def slow(it, carry):
+            mix_step(tasks - 1, r, m.pb)
+
+    def safe_heads(joff):
+        one = eye()
+
+        def row_head(it, carry):
             row, h = it // HEADS, lax.rem(it, HEADS)
-            q = qs[row // 4, h, :, pl.ds(joff, JB)]
+            q = m.qs[row // 4, h, :, pl.ds(joff, JB)]
 
             def scores(kb, carry):
                 ks = pl.ds(pl.multiple_of(kb * KB, KB), KB)
-                rhs = jnp.concatenate([bt[h, ks], q], axis=0)
-                lhs = jnp.concatenate([eye, km[row, h, ks]], axis=1)
+                rhs = jnp.concatenate([m.bt[h, ks], q], axis=0)
+                lhs = jnp.concatenate([one, m.km[row, h, ks]], axis=1)
                 s1 = jnp.dot(lhs, rhs, preferred_element_type=F32)
-                s1 = jnp.where(mcol_ref[ks] > 0.5, s1, -1e30)
-                ss[ks] = s1
+                s1 = jnp.where(m.mcol[ks] > 0.5, s1, -1e30)
+                m.ss[ks] = s1
                 return jnp.maximum(carry, jnp.max(s1, axis=0, keepdims=True))
 
             top = lax.fori_loop(0, nk, scores, jnp.full((1, JB), -1e30, F32))
 
             def weights(kb, carry):
                 ks = pl.ds(pl.multiple_of(kb * KB, KB), KB)
-                pa[0, ks] = jnp.exp2(ss[ks] - top).astype(BF16)
+                m.pa[0, ks] = jnp.exp2(m.ss[ks] - top).astype(BF16)
                 return carry
 
             lax.fori_loop(0, nk, weights, 0)
-            oe = jnp.dot(vx[row, h], pa[0], preferred_element_type=F32)
-            ot[row, head_slice(h)] = oe[:HEAD_DIM] / oe[HEAD_DIM : HEAD_DIM + 1]
+            oe = jnp.dot(m.vx[row, h], m.pa[0], preferred_element_type=F32)
+            m.ot[row, head_slice(h)] = oe[:HEAD_DIM] / oe[HEAD_DIM : HEAD_DIM + 1]
             return carry
 
-        lax.fori_loop(0, rows * HEADS, slow, 0)
-
-    def last(i, carry):
-        for r in range(UNROLL):
-            finish(UNROLL * i + r)
-        return carry
-
-    lax.fori_loop(0, rows // UNROLL, last, 0)
-
-    span = JB // rows
-    out_row = lax.broadcasted_iota(jnp.int32, (JB, JB), 0)
-    in_row = lax.broadcasted_iota(jnp.int32, (JB, JB), 1)
-    perm = (in_row == lax.rem(out_row, rows) * span + out_row // rows).astype(F32).astype(BF16)
-    for q in range(rows // 2):
-        cols = [
-            jnp.concatenate([zz[r, span * n : span * (n + 1)] for r in range(rows)], axis=0)
-            for n in (2 * q, 2 * q + 1)
-        ]
-        moved = jnp.dot(perm, jnp.concatenate(cols, axis=1), preferred_element_type=F32).astype(BF16)
-        o_ref[2 * JB * q : 2 * JB * q + JB] = moved[:, :chan]
-        o_ref[2 * JB * q + JB : 2 * JB * (q + 1)] = moved[:, chan:]
-
-
-def attention(x, a, proj, gate_bias, out_w, mrow, mcol, bias, trans=()):
-    rows, res, chan = x.shape
-    nj = res // JB
+        lax.fori_loop(0, rows * HEADS, row_head, 0)
+
+    def finish(joff, store):
+        def row(r):
+            gated = (m.ot[r] * m.gt[r, :, pl.ds(joff, JB)]).T.astype(BF16)
+            z = m.x[r, pl.ds(joff, JB)].astype(F32) + jnp.dot(
+                gated, m.ow[...], preferred_element_type=F32
+            )
+            z = z.astype(BF16)
+            if trans:
+                zf = z.astype(F32)
+                a = layer_norm(z, m.ng[...])
+                hid = jnp.dot(a, m.ti[...], preferred_element_type=F32) + m.tb[...]
+                hid = jnp.maximum(hid, 0.0).astype(BF16)
+                z = (zf + jnp.dot(hid, m.to[...], preferred_element_type=F32)).astype(BF16)
+            m.zz[r] = z
+
+        def some(i, carry):
+            for r in range(UNROLL):
+                row(UNROLL * i + r)
+            return carry
+
+        lax.fori_loop(0, rows // UNROLL, some, 0)
+        span = JB // rows
+        out_row = lax.broadcasted_iota(jnp.int32, (JB, JB), 0)
+        in_row = lax.broadcasted_iota(jnp.int32, (JB, JB), 1)
+        perm = (in_row == lax.rem(out_row, rows) * span + out_row // rows).astype(F32).astype(BF16)
+        for q in range(rows // 2):
+            cols = [
+                jnp.concatenate([m.zz[r, span * n : span * (n + 1)] for r in range(rows)], axis=0)
+                for n in (2 * q, 2 * q + 1)
+            ]
+            moved = jnp.dot(perm, jnp.concatenate(cols, axis=1), preferred_element_type=F32)
+            for n in range(2):
+                part = moved[:, chan * n : chan * (n + 1)]
+                store(span * (2 * q + n), part.reshape(span, rows, chan).astype(BF16))
+
+    return types.SimpleNamespace(
+        project_all=project_all, turn_bias=turn_bias, fast_heads=fast_heads,
+        safe_heads=safe_heads, finish=finish,
+    )
+
+
+def stage_names(trans):
+    names = ["x", "a", "w", "gb", "ow", "mrow", "mcol"]
+    return names + (["ng", "ti", "tb", "to"] if trans else [])
+
+
+def stage_scratch(rows, res, chan):
+    return {
+        "km": pltpu.VMEM((rows, HEADS, res, chan), BF16),
+        "qs": pltpu.VMEM((rows // 4, HEADS, chan, res), BF16),
+        "vx": pltpu.VMEM((rows, HEADS, HEAD_DIM + 16, res), BF16),
+        "gt": pltpu.VMEM((rows, chan, res), F32),
+        "bt": pltpu.VMEM((HEADS, res, JB), BF16),
+        "pa": pltpu.VMEM((4, res, JB), BF16),
+        "pb": pltpu.VMEM((4, res, JB), BF16),
+        "ot": pltpu.VMEM((rows, chan, JB), F32),
+        "wk": pltpu.VMEM((4, chan, chan), BF16),
+        "wq": pltpu.VMEM((4, chan, chan), BF16),
+        "gd": pltpu.VMEM((1, JB), F32),
+        "zz": pltpu.VMEM((rows, JB, chan), BF16),
+        "bs": pltpu.VMEM((HEADS, JB, res), BF16),
+        "ss": pltpu.VMEM((res, JB), F32),
+    }
+
+
+def safe_kernel(trans, names, *refs):
+    m = types.SimpleNamespace(**dict(zip(names, refs)))
+    tools = stage_tools(trans, m)
+
+    @pl.when(pl.program_id(0) == 0)
+    def _():
+        tools.project_all()
+
+    joff = pl.multiple_of(pl.program_id(0) * JB, JB)
+    tools.turn_bias(m.b)
+    tools.safe_heads(joff)
+
+    def store(at, part):
+        m.o[at : at + part.shape[0]] = part
+
+    tools.finish(joff, store)
+
+
+def safe_attention(ins, bias, trans):
+    rows, res, chan = ins[0].shape
+    scratch = stage_scratch(rows, res, chan)
+    names = stage_names(trans) + ["b", "o"] + list(scratch)
     full = lambda a: pl.BlockSpec(a.shape, lambda j, n=a.ndim: (0,) * n)
-    ins = [x, a, proj, gate_bias, out_w, mrow, mcol]
-    specs = [full(a) for a in ins] + [pl.BlockSpec((HEADS, JB, res), lambda j: (0, j, 0))]
-    ins.append(bias)
-    ins += trans
-    specs += [full(a) for a in trans]
     return pl.pallas_call(
-        functools.partial(attn_kernel, bool(trans)),
-        grid=(nj,),
-        out_shape=jax.ShapeDtypeStruct((res * rows, chan), BF16),
-        in_specs=specs,
-        out_specs=pl.BlockSpec((JB * rows, chan), lambda j: (j, 0)),
-        scratch_shapes=[
-            pltpu.VMEM((rows, HEADS, res, chan), BF16),
-            pltpu.VMEM((rows // 4, HEADS, chan, res), BF16),
-            pltpu.VMEM((rows, HEADS, HEAD_DIM + 16, res), BF16),
-            pltpu.VMEM((rows, chan, res), F32),
-            pltpu.VMEM((HEADS, res, JB), BF16),
-            pltpu.VMEM((4, res, JB), BF16),
-            pltpu.VMEM((4, res, JB), BF16),
-            pltpu.VMEM((rows, chan, JB), F32),
-            pltpu.VMEM((4, chan, chan), BF16),
-            pltpu.VMEM((4, chan, chan), BF16),
-            pltpu.VMEM((res, JB), F32),
-            pltpu.VMEM((1, JB), F32),
-            pltpu.VMEM((rows, JB, chan), BF16),
-        ],
+        functools.partial(safe_kernel, trans, names),
+        grid=(res // JB,),
+        out_shape=jax.ShapeDtypeStruct((res, rows, chan), BF16),
+        in_specs=[full(a) for a in ins] + [pl.BlockSpec((HEADS, JB, res), lambda j: (0, j, 0))],
+        out_specs=pl.BlockSpec((JB, rows, chan), lambda j: (j, 0, 0)),
+        scratch_shapes=list(scratch.values()),
         compiler_params=pltpu.CompilerParams(
             dimension_semantics=("arbitrary",), vmem_limit_bytes=60 * 1024 * 1024
         ),
-    )(*ins)
+    )(*ins, bias)
+
+
+def fused_kernel(trans, n, names, *refs):
+    m = types.SimpleNamespace(**dict(zip(names, refs)))
+    tools = stage_tools(trans, m)
+    rows, res, chan = m.x.shape
+    nj = res // JB
+    per = JB // rows
+    gy = n // 16
+    me = lax.axis_index("gx") * gy + lax.axis_index("gy")
+    at = lambda d: {"gx": d // gy, "gy": lax.rem(d, gy)}
+    barrier = pltpu.get_barrier_semaphore()
+
+    def greet(t, carry):
+        pl.semaphore_signal(
+            barrier, inc=1, device_id=at(lax.rem(me + t, n)), device_id_type=pl.DeviceIdType.MESH
+        )
+        return carry
+
+    lax.fori_loop(1, n, greet, 0)
+
+    def block_of(t):
+        return lax.rem(t + me, nj)
+
+    def fetch(t):
+        return pltpu.make_async_copy(
+            m.b.at[:, pl.ds(pl.multiple_of(block_of(t) * JB, JB), JB)], m.bs, m.fetch_sem
+        )
+
+    def copy(t, i, frm):
+        to = block_of(t) * per + i
+        ahead = lax.rem(to - me + n, n)
+        return to, pltpu.make_async_remote_copy(
+            src_ref=m.zs.at[lax.rem(t, 2), pl.ds(pl.multiple_of(i * rows, rows), rows)],
+            dst_ref=m.o.at[:, pl.ds(pl.multiple_of(rows * frm, rows), rows)],
+            send_sem=m.send_sem.at[ahead], recv_sem=m.recv_sem.at[ahead],
+            device_id=at(to), device_id_type=pl.DeviceIdType.MESH,
+        )
+
+    def own(t, i):
+        mine = pl.ds(pl.multiple_of(rows * me, rows), rows)
+        return pltpu.make_async_copy(
+            m.zs.at[lax.rem(t, 2), pl.ds(pl.multiple_of(i * rows, rows), rows)],
+            m.o.at[:, mine], m.own_sem,
+        )
+
+    def send_block(t):
+        def send(i, carry):
+            to, c = copy(t, i, me)
+
+            @pl.when(to != me)
+            def _():
+                c.start()
+
+            @pl.when(to == me)
+            def _():
+                own(t, i).start()
+
+            return carry
+
+        lax.fori_loop(0, per, send, 0)
+
+    def sent_block(t):
+        def sent(i, carry):
+            to, c = copy(t, i, me)
+
+            @pl.when(to != me)
+            def _():
+                c.wait_send()
+
+            @pl.when(to == me)
+            def _():
+                own(t, i).wait()
+
+            return carry
+
+        lax.fori_loop(0, per, sent, 0)
+
+    fetch(0).start()
+    tools.project_all()
+    m.gd[...] = jnp.ones_like(m.gd)
+    pl.semaphore_wait(barrier, n - 1)
+
+    def block(t, carry):
+        joff = pl.multiple_of(block_of(t) * JB, JB)
+        fetch(t).wait()
+        tools.turn_bias(m.bs)
+
+        @pl.when(t > 0)
+        def _():
+            send_block(t - 1)
+
+        @pl.when(t < nj - 1)
+        def _():
+            fetch(t + 1).start()
+
+        tools.fast_heads(joff)
+
+        @pl.when(t > 1)
+        def _():
+            sent_block(t - 2)
+
+        def store(at, part):
+            m.zs[lax.rem(t, 2), at : at + part.shape[0]] = part
+
+        tools.finish(joff, store)
+        return carry
+
+    lax.fori_loop(0, nj, block, 0)
+    good = jnp.min(m.gd[...], axis=1, keepdims=True)
+    if trans:
+        m.good[...] = jnp.minimum(m.before[...], good)
+    else:
+        m.good[...] = jnp.broadcast_to(good, m.good.shape)
+    send_block(nj - 1)
+    if trans:
+        def flag(t, carry):
+            c = pltpu.make_async_remote_copy(
+                src_ref=m.good, dst_ref=m.flags.at[me],
+                send_sem=m.fsend.at[t], recv_sem=m.frecv.at[t],
+                device_id=at(lax.rem(me + t, n)), device_id_type=pl.DeviceIdType.MESH,
+            )
+            c.start()
+            return carry
+
+        lax.fori_loop(1, n, flag, 0)
+        mine = pltpu.make_async_copy(m.good, m.flags.at[me], m.fsend.at[0])
+        mine.start()
+        mine.wait()
+    sent_block(nj - 2)
+    sent_block(nj - 1)
+
+    def land(t, carry):
+        frm = lax.rem(me + n - t, n)
+        pltpu.make_async_remote_copy(
+            src_ref=m.zs.at[0, pl.ds(0, rows)],
+            dst_ref=m.o.at[:, pl.ds(pl.multiple_of(rows * frm, rows), rows)],
+            send_sem=m.send_sem.at[t], recv_sem=m.recv_sem.at[t],
+            device_id=at(frm), device_id_type=pl.DeviceIdType.MESH,
+        ).wait_recv()
+        if trans:
+            c = pltpu.make_async_remote_copy(
+                src_ref=m.good, dst_ref=m.flags.at[frm],
+                send_sem=m.fsend.at[t], recv_sem=m.frecv.at[t],
+                device_id=at(frm), device_id_type=pl.DeviceIdType.MESH,
+            )
+            c.wait_recv()
+            c.wait_send()
+        return carry
+
+    lax.fori_loop(1, n, land, 0)
+
+
+def fused_attention(cid, n, ins, bias, before):
+    trans = before is not None
+    rows, res, chan = ins[0].shape
+    scratch = stage_scratch(rows, res, chan)
+    del scratch["ss"]
+    scratch |= {
+        "zs": pltpu.VMEM((2, JB, rows, chan), BF16),
+        "send_sem": pltpu.SemaphoreType.DMA((n,)),
+        "recv_sem": pltpu.SemaphoreType.DMA((n,)),
+        "fetch_sem": pltpu.SemaphoreType.DMA,
+        "own_sem": pltpu.SemaphoreType.DMA,
+    }
+    anywhere = pl.BlockSpec(memory_space=pl.ANY)
+    outs = {"o": jax.ShapeDtypeStruct((rows, res, chan), BF16)}
+    out_specs = [anywhere]
+    names = stage_names(trans) + ["b"]
+    args = list(ins) + [bias]
+    in_specs = [VMEM] * len(ins) + [anywhere]
+    if trans:
+        names.append("before")
+        args.append(before)
+        in_specs.append(VMEM)
+        outs["flags"] = jax.ShapeDtypeStruct((n, 8, 128), F32)
+        out_specs.append(anywhere)
+        scratch |= {
+            "good": pltpu.VMEM((8, 128), F32),
+            "fsend": pltpu.SemaphoreType.DMA((n,)),
+            "frecv": pltpu.SemaphoreType.DMA((n,)),
+        }
+    else:
+        outs["good"] = jax.ShapeDtypeStruct((8, 128), F32)
+        out_specs.append(VMEM)
+    return pl.pallas_call(
+        functools.partial(fused_kernel, trans, n, names + list(outs) + list(scratch)),
+        out_shape=list(outs.values()),
+        in_specs=in_specs,
+        out_specs=out_specs,
+        scratch_shapes=list(scratch.values()),
+        compiler_params=pltpu.CompilerParams(
+            collective_id=cid, has_side_effects=True, vmem_limit_bytes=60 * 1024 * 1024
+        ),
+    )(*args)
 
 
 def exchange_kernel(n, z_ref, o_ref, send_sem, recv_sem, own_sem):
@@ -465,10 +692,10 @@
 
 
 def exchange(cid, n, z, rows):
-    res = z.shape[0] // rows
+    res, _, chan = z.shape
     return pl.pallas_call(
         functools.partial(exchange_kernel, n),
-        out_shape=jax.ShapeDtypeStruct((rows, res, z.shape[1]), BF16),
+        out_shape=jax.ShapeDtypeStruct((rows, res, chan), BF16),
         in_specs=[pl.BlockSpec(memory_space=pl.ANY)],
         out_specs=pl.BlockSpec(memory_space=pl.ANY),
         scratch_shapes=[
@@ -477,7 +704,7 @@
             pltpu.SemaphoreType.DMA,
         ],
         compiler_params=pltpu.CompilerParams(collective_id=cid, has_side_effects=True),
-    )(z.reshape(res, rows, z.shape[1]))
+    )(z)
 
 
 def local(
@@ -507,18 +734,23 @@
     mask = mask[:, 0, :rows].reshape(res)
     mask = jnp.where(jnp.max(mask) > 0.5, mask, 1.0)
     mrow, mcol = mask.reshape(1, res), mask.reshape(res, 1)
-
-    z1 = attention(
-        pair_in, normed, proj_start, row(gate_bias_start), out_w_start, mrow, mcol, bias
-    )
-    cols = exchange(2, n, z1, rows)
-    bias, normed = pair_bias(cols, row(norm_end), bias_w_end)
-    bias = gather(1, bias)
-    out = attention(
-        cols, normed, proj_end, row(gate_bias_end), out_w_end, mrow, mcol, bias,
-        (row(norm_trans), trans_in, row(trans_bias), trans_out),
-    )
-    return exchange(3, n, out, rows)
+    start = [pair_in, normed, proj_start, row(gate_bias_start), out_w_start, mrow, mcol]
+    ends = [proj_end, row(gate_bias_end), out_w_end, mrow, mcol]
+    ends += [row(norm_trans), trans_in, row(trans_bias), trans_out]
+
+    def end_inputs(cols):
+        bias, normed = pair_bias(cols, row(norm_end), bias_w_end)
+        return [cols, normed] + ends, gather(1, bias)
+
+    def safe(bias):
+        cols = exchange(4, n, safe_attention(start, bias, False), rows)
+        ins, bias = end_inputs(cols)
+        return exchange(5, n, safe_attention(ins, bias, True), rows)
+
+    cols, good = fused_attention(2, n, start, bias, None)
+    ins, end_bias = end_inputs(cols)
+    out, flags = fused_attention(3, n, ins, end_bias, good)
+    return lax.cond(jnp.min(flags) > 0.5, lambda b: out, safe, bias)
 
 
 def solution(mesh):

time: 277 us -> 266 us (0.960)
  Pallas kernels: 265 us -> 252 us
    pallas_call x4 -> x2, Pallas kernels: 176 us -> 166 us  [fused_attention(): pl.pallas_call(functools.partial(fused_kernel, trans, n, names + list(out...]
    pallas_call x2, Pallas kernels: 80.2 us -> 77.2 us  [gather(): pl.pallas_call(functools.partial(gather_kernel, n), out_shape=outs, in_sp...]
where the time goes in v4:
time: 266 us
  Pallas kernels  252 us (95%)
  local copies, waits for them, and re-layouts  8.89 us (3%)
  other arithmetic  3.25 us (1%)
    pallas_call x2, Pallas kernels, fused_attention(): pl.pallas_call(functools.partial(fused_kernel, trans, n, names + list(out...  166 us
    pallas_call x2, Pallas kernels, gather(): pl.pallas_call(functools.partial(gather_kernel, n), out_shape=outs, in_sp...  77.2 us
    pallas_call x2, Pallas kernels, pair_bias(): pl.pallas_call(bias_kernel, out_shape=[jax.ShapeDtypeStruct((HEADS, rows,...  8.94 us

profile of v4, /device:TPU:1, one launch (start us, length us, event | category | flops | bytes accessed | tf_op | source)
XLA Modules:
  0.0 265.5 jit_solution(6040633647998083711)
XLA Ops:
  0.0 0.0 copy-start
  0.0 0.0 copy-start.5
  0.0 0.0 copy-start.1
  0.0 0.0 copy-start.9
  0.0 0.8 convert_bitcast_fusion
  0.8 0.6 pad.15.refs_1_
  1.4 0.8 copy.23
  2.2 0.6 pad.14.bw_ref
  2.8 0.8 copy.26
  3.7 0.6 pad.16.bw_ref
  4.3 4.5 %shard_map.156 = (bf16[4,8,1024]{2,1,0:T(8,128)(2,1)}, bf16[8,1024,128]{2,1,0:T(8,128)(2,1)}) custom-call(bf16[8,1024,128]{2,1,0:T(8,128)(2,1)} %refs_0_.1, f32[1,128]{1,0:T(1,128)} %bitcast.35, bf16[128,128]{1,0:T(8,128)(2,1)} %pad.14.bw_ref), custom_call_target="tpu_custom_call" | custom-call | tf_op jit(solution)/shard_map/pallas_call | solution.py:45
  8.7 42.1 %shard_map.157 = (bf16[4,2,4,2,4,2,8,1024]{7,6,5,4,3,2,1,0:T(8,128)(2,1)}, f32[2,4,2,4,2,8,128]{6,5,4,3,2,1,0:T(8,128)}) custom-call(bf16[4,8,1024]{2,1,0:T(8,128)(2,1)} %get-tuple-element.73.refs_0_, f32[8,128]{1,0:T(8,128)} %pad.15.refs_1_), custom_call_target="tpu_custom_call" | custom-call | tf_op jit(solution)/shard_map/pallas_call | solution.py:207
  50.9 1.1 slice.4
  52.0 0.6 reduce_max.9
  53.2 0.1 select_n.30.refs_5_
  53.3 0.1 select_n.31
  53.4 1.0 copy.25.refs_6_
  54.5 0.0 copy-done
  54.5 0.0 copy-done.5
  54.5 0.0 copy-done.1
  54.5 0.0 copy-done.9
  54.5 0.0 copy-start.12
  54.5 68.2 %shard_map.158 = (bf16[8,1024,128]{2,1,0:T(8,128)(2,1)}, f32[8,128]{1,0:T(8,128)}) custom-call(bf16[8,1024,128]{2,1,0:T(8,128)(2,1)S(1)} %copy-done, bf16[8,1024,128]{2,1,0:T(8,128)(2,1)} %get-tuple-element.72.refs_1_, bf16[128,512]{1,0:T(8,128)(2,1)S(1)} %copy-done.1, f32[1,128]{1,0:T(1,128)S(1)} %bitcast.27, bf16[128,128]{1,0:T(8,128)(2,1)S(1)} %copy-done.5, ...), custom_call_target="tpu_custom_call" | custom-call | tf_op jit(solution)/shard_map/pallas_call | solution.py:640
  122.7 0.0 copy-done.12
  122.7 4.5 %shard_map.159 = (bf16[4,8,1024]{2,1,0:T(8,128)(2,1)}, bf16[8,1024,128]{2,1,0:T(8,128)(2,1)}) custom-call(bf16[8,1024,128]{2,1,0:T(8,128)(2,1)} %get-tuple-element.76.x_ref.refs_0_, f32[1,128]{1,0:T(1,128)S(1)} %bitcast.33, bf16[128,128]{1,0:T(8,128)(2,1)} %pad.16.bw_ref), custom_call_target="tpu_custom_call" | custom-call | tf_op jit(solution)/shard_map/pallas_call | solution.py:45
  127.2 0.0 copy-start.2
  127.2 0.0 copy-start.3
  127.2 0.0 copy-start.4
  127.2 0.0 copy-start.6
  127.2 0.0 copy-start.7
  127.2 0.0 copy-start.10
  127.2 0.0 copy-start.11
  127.2 35.0 %shard_map.160 = bf16[4,2,4,2,4,2,8,1024]{7,6,5,4,3,2,1,0:T(8,128)(2,1)} custom-call(bf16[4,8,1024]{2,1,0:T(8,128)(2,1)} %get-tuple-element.78.refs_0_), custom_call_target="tpu_custom_call" | custom-call | tf_op jit(solution)/shard_map/pallas_call | solution.py:207
  162.3 0.0 copy-done.2
  162.3 0.0 copy-done.3
  162.3 0.0 copy-done.4
  162.3 0.0 copy-done.6
  162.3 0.0 copy-done.7
  162.3 0.0 copy-done.10
  162.3 0.0 copy-done.11
  162.3 0.0 copy-start.8
  162.3 97.7 %shard_map.161 = (bf16[8,1024,128]{2,1,0:T(8,128)(2,1)}, f32[128,8,128]{2,1,0:T(8,128)}) custom-call(bf16[8,1024,128]{2,1,0:T(8,128)(2,1)} %get-tuple-element.76.x_ref.refs_0_, bf16[8,1024,128]{2,1,0:T(8,128)(2,1)} %get-tuple-element.77.refs_1_, bf16[128,512]{1,0:T(8,128)(2,1)S(1)} %copy-done.2, f32[1,128]{1,0:T(1,128)S(1)} %bitcast.29, ...), custom_call_target="tpu_custom_call" | custom-call | tf_op jit(solution)/shard_map/pallas_call | solution.py:640
  260.0 1.8 reduce_min.9
  262.4 0.0 copy-done.8
  262.5 3.1 %copy.34 = bf16[8,1024,128]{2,1,0:T(8,128)(2,1)} copy(bf16[8,1024,128]{2,1,0:T(8,128)(2,1)} %get-tuple-element.82) | data formatting | bytes 4194304
  (2 shorter events, 0.0 us)
Async XLA Ops:
  0.0 54.5 %copy-start = (bf16[8,1024,128]{2,1,0:T(8,128)(2,1)S(1)}, bf16[8,1024,128]{2,1,0:T(8,128)(2,1)}, u32[]{:S(2)}) copy-start(bf16[8,1024,128]{2,1,0:T(8,128)(2,1)} %refs_0_.1) | copy-start | bytes 6291460
  0.0 54.5 %copy-start.5 = (bf16[128,128]{1,0:T(8,128)(2,1)S(1)}, bf16[128,128]{1,0:T(8,128)(2,1)}, u32[]{:S(2)}) copy-start(bf16[128,128]{1,0:T(8,128)(2,1)} %refs_4_.2) | copy-start | bytes 98308
  0.0 54.5 %copy-start.1 = (bf16[128,512]{1,0:T(8,128)(2,1)S(1)}, bf16[128,512]{1,0:T(8,128)(2,1)}, u32[]{:S(2)}) copy-start(bf16[128,512]{1,0:T(8,128)(2,1)} %refs_2_.2) | copy-start | bytes 393220
  0.0 54.5 %copy-start.9 = (f32[128]{0:T(128)S(1)}, f32[128]{0:T(128)}, u32[]{:S(2)}) copy-start(f32[128]{0:T(128)} %param.22) | copy-start | bytes 1540
  54.5 68.2 %copy-start.12 = (f32[128]{0:T(128)S(1)}, f32[128]{0:T(128)}, u32[]{:S(2)}) copy-start(f32[128]{0:T(128)} %param.25) | copy-start | bytes 1540
  127.2 35.1 %copy-start.2 = (bf16[128,512]{1,0:T(8,128)(2,1)S(1)}, bf16[128,512]{1,0:T(8,128)(2,1)}, u32[]{:S(2)}) copy-start(bf16[128,512]{1,0:T(8,128)(2,1)} %refs_2_.3) | copy-start | bytes 393220
  127.2 35.1 %copy-start.3 = (bf16[128,512]{1,0:T(8,128)(2,1)S(1)}, bf16[128,512]{1,0:T(8,128)(2,1)}, u32[]{:S(2)}) copy-start(bf16[128,512]{1,0:T(8,128)(2,1)} %refs_8_.1) | copy-start | bytes 393220
  127.2 35.1 %copy-start.4 = (bf16[512,128]{1,0:T(8,128)(2,1)S(1)}, bf16[512,128]{1,0:T(8,128)(2,1)}, u32[]{:S(2)}) copy-start(bf16[512,128]{1,0:T(8,128)(2,1)} %refs_10_.1) | copy-start | bytes 393220
  127.2 35.1 %copy-start.6 = (bf16[128,128]{1,0:T(8,128)(2,1)S(1)}, bf16[128,128]{1,0:T(8,128)(2,1)}, u32[]{:S(2)}) copy-start(bf16[128,128]{1,0:T(8,128)(2,1)} %refs_4_.3) | copy-start | bytes 98308
  127.2 35.1 %copy-start.7 = (f32[512]{0:T(512)S(1)}, f32[512]{0:T(512)}, u32[]{:S(2)}) copy-start(f32[512]{0:T(512)} %param.32) | copy-start | bytes 6148
  127.2 35.1 %copy-start.10 = (f32[128]{0:T(128)S(1)}, f32[128]{0:T(128)}, u32[]{:S(2)}) copy-start(f32[128]{0:T(128)} %param.27) | copy-start | bytes 1540
  127.2 35.1 %copy-start.11 = (f32[128]{0:T(128)S(1)}, f32[128]{0:T(128)}, u32[]{:S(2)}) copy-start(f32[128]{0:T(128)} %param.30) | copy-start | bytes 1540
  162.3 100.1 %copy-start.8 = (bf16[128,4]{0,1:T(4,128)(2,1)S(1)}, bf16[128,4]{0,1:T(4,128)(2,1)}, u32[]{:S(2)}) copy-start(bf16[128,4]{0,1:T(4,128)(2,1)} %param.28) | copy-start | bytes 3076

commit v5 on v4

--- a/solution.py
+++ b/solution.py
@@ -499,7 +499,8 @@
         )
 
     def send_block(t):
-        def send(i, carry):
+        def send(k, carry):
+            i = lax.rem(k + me // nj, per)
             to, c = copy(t, i, me)
 
             @pl.when(to != me)
@@ -515,7 +516,8 @@
         lax.fori_loop(0, per, send, 0)
 
     def sent_block(t):
-        def sent(i, carry):
+        def sent(k, carry):
+            i = lax.rem(k + me // nj, per)
             to, c = copy(t, i, me)
 
             @pl.when(to != me)
@@ -570,7 +572,7 @@
     if trans:
         def flag(t, carry):
             c = pltpu.make_async_remote_copy(
-                src_ref=m.good, dst_ref=m.flags.at[me],
+                src_ref=m.good.at[pl.ds(0, 1)], dst_ref=m.flags.at[me, pl.ds(0, 1)],
                 send_sem=m.fsend.at[t], recv_sem=m.frecv.at[t],
                 device_id=at(lax.rem(me + t, n)), device_id_type=pl.DeviceIdType.MESH,
             )
@@ -594,7 +596,7 @@
         ).wait_recv()
         if trans:
             c = pltpu.make_async_remote_copy(
-                src_ref=m.good, dst_ref=m.flags.at[frm],
+                src_ref=m.good.at[pl.ds(0, 1)], dst_ref=m.flags.at[frm, pl.ds(0, 1)],
                 send_sem=m.fsend.at[t], recv_sem=m.frecv.at[t],
                 device_id=at(frm), device_id_type=pl.DeviceIdType.MESH,
             )
@@ -750,7 +752,7 @@
     cols, good = fused_attention(2, n, start, bias, None)
     ins, end_bias = end_inputs(cols)
     out, flags = fused_attention(3, n, ins, end_bias, good)
-    return lax.cond(jnp.min(flags) > 0.5, lambda b: out, safe, bias)
+    return lax.cond(jnp.min(flags[:, 0]) > 0.5, lambda b: out, safe, bias)
 
 
 def solution(mesh):

time: 266 us -> 261 us (0.981)
  Pallas kernels: 252 us -> 247 us
    pallas_call x2, Pallas kernels: 166 us -> 160 us  [fused_attention(): pl.pallas_call(functools.partial(fused_kernel, trans, n, names + list(out...]
where the time goes in v5:
time: 261 us
  Pallas kernels  247 us (95%)
  local copies, waits for them, and re-layouts  8.89 us (3%)
  other arithmetic  3.25 us (1%)
    pallas_call x2, Pallas kernels, fused_attention(): pl.pallas_call(functools.partial(fused_kernel, trans, n, names + list(out...  160 us
    pallas_call x2, Pallas kernels, gather(): pl.pallas_call(functools.partial(gather_kernel, n), out_shape=outs, in_sp...  78.4 us
    pallas_call x2, Pallas kernels, pair_bias(): pl.pallas_call(bias_kernel, out_shape=[jax.ShapeDtypeStruct((HEADS, rows,...  8.94 us

profile of v5, /device:TPU:1, one launch (start us, length us, event | category | flops | bytes accessed | tf_op | source)
XLA Modules:
  0.0 260.9 jit_solution(16759500280035031509)
XLA Ops:
  0.0 0.0 copy-start
  0.0 0.0 copy-start.5
  0.0 0.0 copy-start.1
  0.0 0.0 copy-start.9
  0.0 0.8 convert_bitcast_fusion
  0.8 0.6 pad.15.refs_1_
  1.4 0.8 copy.23
  2.2 0.6 pad.14.bw_ref
  2.8 0.8 copy.26
  3.7 0.6 pad.16.bw_ref
  4.3 4.5 %shard_map.156 = (bf16[4,8,1024]{2,1,0:T(8,128)(2,1)}, bf16[8,1024,128]{2,1,0:T(8,128)(2,1)}) custom-call(bf16[8,1024,128]{2,1,0:T(8,128)(2,1)} %refs_0_.1, f32[1,128]{1,0:T(1,128)} %bitcast.35, bf16[128,128]{1,0:T(8,128)(2,1)} %pad.14.bw_ref), custom_call_target="tpu_custom_call" | custom-call | tf_op jit(solution)/shard_map/pallas_call | solution.py:45
  8.7 42.1 %shard_map.157 = (bf16[4,2,4,2,4,2,8,1024]{7,6,5,4,3,2,1,0:T(8,128)(2,1)}, f32[2,4,2,4,2,8,128]{6,5,4,3,2,1,0:T(8,128)}) custom-call(bf16[4,8,1024]{2,1,0:T(8,128)(2,1)} %get-tuple-element.73.refs_0_, f32[8,128]{1,0:T(8,128)} %pad.15.refs_1_), custom_call_target="tpu_custom_call" | custom-call | tf_op jit(solution)/shard_map/pallas_call | solution.py:207
  50.9 1.1 slice.8
  52.0 0.6 reduce_max.9
  53.2 0.1 select_n.30.refs_5_
  53.3 0.1 select_n.31
  53.4 1.0 copy.25.refs_6_
  54.5 0.0 copy-done
  54.5 0.0 copy-done.5
  54.5 0.0 copy-done.1
  54.5 0.0 copy-done.9
  54.5 0.0 copy-start.12
  54.5 69.1 %shard_map.158 = (bf16[8,1024,128]{2,1,0:T(8,128)(2,1)}, f32[8,128]{1,0:T(8,128)}) custom-call(bf16[8,1024,128]{2,1,0:T(8,128)(2,1)S(1)} %copy-done, bf16[8,1024,128]{2,1,0:T(8,128)(2,1)} %get-tuple-element.72.refs_1_, bf16[128,512]{1,0:T(8,128)(2,1)S(1)} %copy-done.1, f32[1,128]{1,0:T(1,128)S(1)} %bitcast.27, bf16[128,128]{1,0:T(8,128)(2,1)S(1)} %copy-done.5, ...), custom_call_target="tpu_custom_call" | custom-call | tf_op jit(solution)/shard_map/pallas_call | solution.py:642
  123.6 0.0 copy-done.12
  123.6 4.5 %shard_map.159 = (bf16[4,8,1024]{2,1,0:T(8,128)(2,1)}, bf16[8,1024,128]{2,1,0:T(8,128)(2,1)}) custom-call(bf16[8,1024,128]{2,1,0:T(8,128)(2,1)} %get-tuple-element.76.x_ref.refs_0_, f32[1,128]{1,0:T(1,128)S(1)} %bitcast.33, bf16[128,128]{1,0:T(8,128)(2,1)} %pad.16.bw_ref), custom_call_target="tpu_custom_call" | custom-call | tf_op jit(solution)/shard_map/pallas_call | solution.py:45
  128.1 0.0 copy-start.2
  128.1 0.0 copy-start.3
  128.1 0.0 copy-start.4
  128.1 0.0 copy-start.6
  128.2 0.0 copy-start.7
  128.2 0.0 copy-start.10
  128.2 0.0 copy-start.11
  128.2 36.2 %shard_map.160 = bf16[4,2,4,2,4,2,8,1024]{7,6,5,4,3,2,1,0:T(8,128)(2,1)} custom-call(bf16[4,8,1024]{2,1,0:T(8,128)(2,1)} %get-tuple-element.78.refs_0_), custom_call_target="tpu_custom_call" | custom-call | tf_op jit(solution)/shard_map/pallas_call | solution.py:207
  164.4 0.0 copy-done.2
  164.4 0.0 copy-done.3
  164.4 0.0 copy-done.4
  164.4 0.0 copy-done.6
  164.4 0.0 copy-done.7
  164.5 0.0 copy-done.10
  164.5 0.0 copy-done.11
  164.5 0.0 copy-start.8
  164.5 90.9 %shard_map.161 = (bf16[8,1024,128]{2,1,0:T(8,128)(2,1)}, f32[128,8,128]{2,1,0:T(8,128)}) custom-call(bf16[8,1024,128]{2,1,0:T(8,128)(2,1)} %get-tuple-element.76.x_ref.refs_0_, bf16[8,1024,128]{2,1,0:T(8,128)(2,1)} %get-tuple-element.77.refs_1_, bf16[128,512]{1,0:T(8,128)(2,1)S(1)} %copy-done.2, f32[1,128]{1,0:T(1,128)S(1)} %bitcast.29, ...), custom_call_target="tpu_custom_call" | custom-call | tf_op jit(solution)/shard_map/pallas_call | solution.py:642
  255.3 1.8 slice_reduce_fusion
  257.8 0.0 copy-done.8
  257.8 3.1 %copy.34 = bf16[8,1024,128]{2,1,0:T(8,128)(2,1)} copy(bf16[8,1024,128]{2,1,0:T(8,128)(2,1)} %get-tuple-element.82) | data formatting | bytes 4194304
  (2 shorter events, 0.0 us)
Async XLA Ops:
  0.0 54.5 %copy-start = (bf16[8,1024,128]{2,1,0:T(8,128)(2,1)S(1)}, bf16[8,1024,128]{2,1,0:T(8,128)(2,1)}, u32[]{:S(2)}) copy-start(bf16[8,1024,128]{2,1,0:T(8,128)(2,1)} %refs_0_.1) | copy-start | bytes 6291460
  0.0 54.5 %copy-start.5 = (bf16[128,128]{1,0:T(8,128)(2,1)S(1)}, bf16[128,128]{1,0:T(8,128)(2,1)}, u32[]{:S(2)}) copy-start(bf16[128,128]{1,0:T(8,128)(2,1)} %refs_4_.2) | copy-start | bytes 98308
  0.0 54.5 %copy-start.1 = (bf16[128,512]{1,0:T(8,128)(2,1)S(1)}, bf16[128,512]{1,0:T(8,128)(2,1)}, u32[]{:S(2)}) copy-start(bf16[128,512]{1,0:T(8,128)(2,1)} %refs_2_.2) | copy-start | bytes 393220
  0.0 54.5 %copy-start.9 = (f32[128]{0:T(128)S(1)}, f32[128]{0:T(128)}, u32[]{:S(2)}) copy-start(f32[128]{0:T(128)} %param.22) | copy-start | bytes 1540
  54.5 69.1 %copy-start.12 = (f32[128]{0:T(128)S(1)}, f32[128]{0:T(128)}, u32[]{:S(2)}) copy-start(f32[128]{0:T(128)} %param.25) | copy-start | bytes 1540
  128.1 36.3 %copy-start.2 = (bf16[128,512]{1,0:T(8,128)(2,1)S(1)}, bf16[128,512]{1,0:T(8,128)(2,1)}, u32[]{:S(2)}) copy-start(bf16[128,512]{1,0:T(8,128)(2,1)} %refs_2_.3) | copy-start | bytes 393220
  128.1 36.3 %copy-start.3 = (bf16[128,512]{1,0:T(8,128)(2,1)S(1)}, bf16[128,512]{1,0:T(8,128)(2,1)}, u32[]{:S(2)}) copy-start(bf16[128,512]{1,0:T(8,128)(2,1)} %refs_8_.1) | copy-start | bytes 393220
  128.1 36.3 %copy-start.4 = (bf16[512,128]{1,0:T(8,128)(2,1)S(1)}, bf16[512,128]{1,0:T(8,128)(2,1)}, u32[]{:S(2)}) copy-start(bf16[512,128]{1,0:T(8,128)(2,1)} %refs_10_.1) | copy-start | bytes 393220
  128.1 36.3 %copy-start.6 = (bf16[128,128]{1,0:T(8,128)(2,1)S(1)}, bf16[128,128]{1,0:T(8,128)(2,1)}, u32[]{:S(2)}) copy-start(bf16[128,128]{1,0:T(8,128)(2,1)} %refs_4_.3) | copy-start | bytes 98308
  128.2 36.3 %copy-start.7 = (f32[512]{0:T(512)S(1)}, f32[512]{0:T(512)}, u32[]{:S(2)}) copy-start(f32[512]{0:T(512)} %param.32) | copy-start | bytes 6148
  128.2 36.3 %copy-start.10 = (f32[128]{0:T(128)S(1)}, f32[128]{0:T(128)}, u32[]{:S(2)}) copy-start(f32[128]{0:T(128)} %param.27) | copy-start | bytes 1540
  128.2 36.3 %copy-start.11 = (f32[128]{0:T(128)S(1)}, f32[128]{0:T(128)}, u32[]{:S(2)}) copy-start(f32[128]{0:T(128)} %param.30) | copy-start | bytes 1540
  164.5 93.3 %copy-start.8 = (bf16[128,4]{0,1:T(4,128)(2,1)S(1)}, bf16[128,4]{0,1:T(4,128)(2,1)}, u32[]{:S(2)}) copy-start(bf16[128,4]{0,1:T(4,128)(2,1)} %param.28) | copy-start | bytes 3076

commit v6 on v5

--- a/solution.py
+++ b/solution.py
@@ -253,12 +253,13 @@
             grp = r // 4
             a = m.a[r]
             kk = jnp.dot(a, m.wk[s], preferred_element_type=F32).astype(BF16)
+            aq = m.aq[r]
             qt = (
-                lax.dot_general(m.wq[s], a, NT, preferred_element_type=F32)
+                lax.dot_general(m.wq[s], aq, NT, preferred_element_type=F32)
                 * (HEAD_DIM**-0.5 * LOG2E)
             ).astype(BF16)
             vt = lax.dot_general(wvt, a, NT, preferred_element_type=F32) * mrow
-            m.gt[r] = jax.nn.sigmoid(lax.dot_general(wgt, a, NT, preferred_element_type=F32) + gb)
+            m.gt[r] = jax.nn.sigmoid(lax.dot_general(wgt, aq, NT, preferred_element_type=F32) + gb)
             for h in range(HEADS):
                 slot = lax.rem(h + s, 4)
                 m.km[r, h] = kk * (lane == slot).astype(F32).astype(BF16)
@@ -420,6 +421,7 @@
 
 def safe_kernel(trans, names, *refs):
     m = types.SimpleNamespace(**dict(zip(names, refs)))
+    m.aq = m.a
     tools = stage_tools(trans, m)
 
     @pl.when(pl.program_id(0) == 0)
@@ -460,9 +462,10 @@
     rows, res, chan = m.x.shape
     nj = res // JB
     per = JB // rows
-    gy = n // 16
-    me = lax.axis_index("gx") * gy + lax.axis_index("gy")
-    at = lambda d: {"gx": d // gy, "gy": lax.rem(d, gy)}
+    gx, gy = lax.axis_index("gx"), lax.axis_index("gy")
+    ny = n // 16
+    me = gx * ny + gy
+    at = lambda d: {"gx": d // ny, "gy": lax.rem(d, ny)}
     barrier = pltpu.get_barrier_semaphore()
 
     def greet(t, carry):
@@ -473,16 +476,42 @@
 
     lax.fori_loop(1, n, greet, 0)
 
+    def owner(c, i):
+        x, z_lo, core = i // 8, lax.rem(i // 4, 2), lax.rem(i // 2, 2)
+        y = lax.rem(c - x + 4, 4)
+        return ((z_lo * 4 + x) * 2 + core) * ny + y * 2 + lax.rem(i, 2)
+
     def block_of(t):
-        return lax.rem(t + me, nj)
+        return lax.rem(t + lax.rem(gx // 2, 4), nj)
+
+    def chunk(c, u):
+        return pl.ds(pl.multiple_of(owner(c, 2 * u) * rows, 2 * rows), 2 * rows)
+
+    def slot(c, u):
+        return pl.ds(pl.multiple_of(c * JB + u * 2 * rows, 2 * rows), 2 * rows)
 
     def fetch(t):
-        return pltpu.make_async_copy(
-            m.b.at[:, pl.ds(pl.multiple_of(block_of(t) * JB, JB), JB)], m.bs, m.fetch_sem
-        )
+        c = block_of(t)
+
+        def one(u, carry):
+            pltpu.make_async_copy(m.b.at[:, chunk(c, u)], m.bs.at[:, slot(0, u)], m.fetch_sem).start()
+            return carry
+
+        lax.fori_loop(0, per // 2, one, 0)
+
+    def fetched():
+        pltpu.make_async_copy(m.b.at[:, pl.ds(0, JB)], m.bs, m.fetch_sem).wait()
+
+    def sort_rows(src, dst, sem):
+        def one(k, carry):
+            c, u = k // (per // 2), lax.rem(k, per // 2)
+            pltpu.make_async_copy(src.at[:, chunk(c, u)], dst.at[:, slot(c, u)], sem).start()
+            return carry
+
+        lax.fori_loop(0, nj * per // 2, one, 0)
 
     def copy(t, i, frm):
-        to = block_of(t) * per + i
+        to = owner(block_of(t), i)
         ahead = lax.rem(to - me + n, n)
         return to, pltpu.make_async_remote_copy(
             src_ref=m.zs.at[lax.rem(t, 2), pl.ds(pl.multiple_of(i * rows, rows), rows)],
@@ -498,9 +527,11 @@
             m.o.at[:, mine], m.own_sem,
         )
 
+    first = ((gx // 8) * 2 + lax.rem(gx, 2)) * ny + gy
+
     def send_block(t):
         def send(k, carry):
-            i = lax.rem(k + me // nj, per)
+            i = lax.rem(k + first, per)
             to, c = copy(t, i, me)
 
             @pl.when(to != me)
@@ -517,7 +548,7 @@
 
     def sent_block(t):
         def sent(k, carry):
-            i = lax.rem(k + me // nj, per)
+            i = lax.rem(k + first, per)
             to, c = copy(t, i, me)
 
             @pl.when(to != me)
@@ -532,14 +563,18 @@
 
         lax.fori_loop(0, per, sent, 0)
 
-    fetch(0).start()
+    sort_rows(m.ah, m.aq, m.sort_sem.at[0])
+    sort_rows(m.xh, m.x, m.sort_sem.at[1])
+    fetch(0)
+    pltpu.make_async_copy(m.ah, m.aq, m.sort_sem.at[0]).wait()
     tools.project_all()
+    pltpu.make_async_copy(m.xh, m.x, m.sort_sem.at[1]).wait()
     m.gd[...] = jnp.ones_like(m.gd)
     pl.semaphore_wait(barrier, n - 1)
 
     def block(t, carry):
         joff = pl.multiple_of(block_of(t) * JB, JB)
-        fetch(t).wait()
+        fetched()
         tools.turn_bias(m.bs)
 
         @pl.when(t > 0)
@@ -548,7 +583,7 @@
 
         @pl.when(t < nj - 1)
         def _():
-            fetch(t + 1).start()
+            fetch(t + 1)
 
         tools.fast_heads(joff)
 
@@ -616,15 +651,18 @@
         "zs": pltpu.VMEM((2, JB, rows, chan), BF16),
         "send_sem": pltpu.SemaphoreType.DMA((n,)),
         "recv_sem": pltpu.SemaphoreType.DMA((n,)),
+        "x": pltpu.VMEM((rows, res, chan), BF16),
+        "aq": pltpu.VMEM((rows, res, chan), BF16),
+        "sort_sem": pltpu.SemaphoreType.DMA((2,)),
         "fetch_sem": pltpu.SemaphoreType.DMA,
         "own_sem": pltpu.SemaphoreType.DMA,
     }
     anywhere = pl.BlockSpec(memory_space=pl.ANY)
     outs = {"o": jax.ShapeDtypeStruct((rows, res, chan), BF16)}
     out_specs = [anywhere]
-    names = stage_names(trans) + ["b"]
-    args = list(ins) + [bias]
-    in_specs = [VMEM] * len(ins) + [anywhere]
+    names = ["xh"] + stage_names(trans)[1:] + ["ah", "b"]
+    args = list(ins) + [ins[1], bias]
+    in_specs = [anywhere] + [VMEM] * (len(ins) - 1) + [anywhere] * 2
     if trans:
         names.append("before")
         args.append(before)

time: 261 us -> 267 us (1.023)
  Pallas kernels: 247 us -> 253 us
    pallas_call x2, Pallas kernels: 160 us -> 164 us  [fused_attention(): pl.pallas_call(functools.partial(fused_kernel, trans, n, names + list(out...]
where the time goes in v6:
time: 267 us; the launch traced here: 266 us
  Pallas kernels  253 us (95%)
  local copies, waits for them, and re-layouts  8.89 us (3%)
  other arithmetic  3.1 us (1%)
    pallas_call x2, Pallas kernels, fused_attention(): pl.pallas_call(functools.partial(fused_kernel, trans, n, names + list(out...  164 us
    pallas_call x2, Pallas kernels, gather(): pl.pallas_call(functools.partial(gather_kernel, n), out_shape=outs, in_sp...  80.2 us
    pallas_call x2, Pallas kernels, pair_bias(): pl.pallas_call(bias_kernel, out_shape=[jax.ShapeDtypeStruct((HEADS, rows,...  8.35 us

profile of v6, /device:TPU:1, one launch (start us, length us, event | category | flops | bytes accessed | tf_op | source)
XLA Modules:
  0.0 266.5 jit_solution(8391677604702377957)
XLA Ops:
  0.0 0.0 copy-start.4
  0.0 0.0 copy-start
  0.0 0.0 copy-start.8
  0.0 0.7 convert_bitcast_fusion
  0.7 0.6 pad.15.refs_1_
  1.3 0.8 copy.23
  2.1 0.6 pad.14.bw_ref
  2.7 0.8 copy.26
  3.5 0.6 pad.16.bw_ref
  4.2 3.9 %shard_map.156 = (bf16[4,8,1024]{2,1,0:T(8,128)(2,1)}, bf16[8,1024,128]{2,1,0:T(8,128)(2,1)S(1)}) custom-call(bf16[8,1024,128]{2,1,0:T(8,128)(2,1)} %refs_0_.1, f32[1,128]{1,0:T(1,128)} %bitcast.35, bf16[128,128]{1,0:T(8,128)(2,1)} %pad.14.bw_ref), custom_call_target="tpu_custom_call" | custom-call | tf_op jit(solution)/shard_map/pallas_call | solution.py:45
  8.1 42.1 %shard_map.157 = (bf16[4,2,4,2,4,2,8,1024]{7,6,5,4,3,2,1,0:T(8,128)(2,1)}, f32[2,4,2,4,2,8,128]{6,5,4,3,2,1,0:T(8,128)}) custom-call(bf16[4,8,1024]{2,1,0:T(8,128)(2,1)} %get-tuple-element.73.refs_0_, f32[8,128]{1,0:T(8,128)} %pad.15.refs_1_), custom_call_target="tpu_custom_call" | custom-call | tf_op jit(solution)/shard_map/pallas_call | solution.py:207
  50.2 1.1 slice.8
  51.3 0.6 reduce_max.9
  52.6 0.1 select_n.30.refs_5_
  52.7 0.1 select_n.31
  52.8 1.0 copy.25.refs_6_
  53.8 0.0 copy-done.4
  53.8 0.0 copy-done
  53.8 0.0 copy-done.8
  53.8 0.0 copy-start.11
  53.8 70.1 %shard_map.158 = (bf16[8,1024,128]{2,1,0:T(8,128)(2,1)}, f32[8,128]{1,0:T(8,128)}) custom-call(bf16[8,1024,128]{2,1,0:T(8,128)(2,1)} %refs_0_.1, bf16[8,1024,128]{2,1,0:T(8,128)(2,1)S(1)} %get-tuple-element.72.refs_1_.refs_7_, bf16[128,512]{1,0:T(8,128)(2,1)S(1)} %copy-done, f32[1,128]{1,0:T(1,128)S(1)} %bitcast.27, bf16[128,128]{1,0:T(8,128)(2,1)S(1)} %copy-done.4, ...), custom_call_target="tpu_custom_call" | custom-call | tf_op jit(solution)/shard_map/pallas_call | solution.py:680
  123.9 0.0 copy-done.11
  123.9 4.4 %shard_map.159 = (bf16[4,8,1024]{2,1,0:T(8,128)(2,1)}, bf16[8,1024,128]{2,1,0:T(8,128)(2,1)}) custom-call(bf16[8,1024,128]{2,1,0:T(8,128)(2,1)} %get-tuple-element.76.x_ref.refs_0_, f32[1,128]{1,0:T(1,128)S(1)} %bitcast.33, bf16[128,128]{1,0:T(8,128)(2,1)} %pad.16.bw_ref), custom_call_target="tpu_custom_call" | custom-call | tf_op jit(solution)/shard_map/pallas_call | solution.py:45
  128.3 0.0 copy-start.1
  128.4 0.0 copy-start.2
  128.4 0.0 copy-start.3
  128.4 0.0 copy-start.5
  128.4 0.0 copy-start.6
  128.4 0.0 copy-start.9
  128.4 0.0 copy-start.10
  128.4 38.0 %shard_map.160 = bf16[4,2,4,2,4,2,8,1024]{7,6,5,4,3,2,1,0:T(8,128)(2,1)} custom-call(bf16[4,8,1024]{2,1,0:T(8,128)(2,1)} %get-tuple-element.78.refs_0_), custom_call_target="tpu_custom_call" | custom-call | tf_op jit(solution)/shard_map/pallas_call | solution.py:207
  166.4 0.0 copy-done.1
  166.5 0.0 copy-done.2
  166.5 0.0 copy-done.3
  166.5 0.0 copy-done.5
  166.5 0.0 copy-done.6
  166.5 0.0 copy-done.9
  166.5 0.0 copy-done.10
  166.5 0.0 copy-start.7
  166.5 94.4 %shard_map.161 = (bf16[8,1024,128]{2,1,0:T(8,128)(2,1)}, f32[128,8,128]{2,1,0:T(8,128)}) custom-call(bf16[8,1024,128]{2,1,0:T(8,128)(2,1)} %get-tuple-element.76.x_ref.refs_0_, bf16[8,1024,128]{2,1,0:T(8,128)(2,1)} %get-tuple-element.77.refs_1_.refs_11_, bf16[128,512]{1,0:T(8,128)(2,1)S(1)} %copy-done.1, f32[1,128]{1,0:T(1,128)S(1)} %bitcast.29, ...), custom_call_target="tpu_custom_call" | custom-call | tf_op jit(solution)/shard_map/pallas_call | solution.py:680
  261.0 1.8 slice_reduce_fusion
  263.4 0.0 copy-done.7
  263.4 3.1 %copy.34 = bf16[8,1024,128]{2,1,0:T(8,128)(2,1)} copy(bf16[8,1024,128]{2,1,0:T(8,128)(2,1)} %get-tuple-element.82) | data formatting | bytes 4194304
  (2 shorter events, 0.0 us)
Async XLA Ops:
  0.0 53.8 %copy-start.4 = (bf16[128,128]{1,0:T(8,128)(2,1)S(1)}, bf16[128,128]{1,0:T(8,128)(2,1)}, u32[]{:S(2)}) copy-start(bf16[128,128]{1,0:T(8,128)(2,1)} %refs_4_.2) | copy-start | bytes 98308
  0.0 53.8 %copy-start = (bf16[128,512]{1,0:T(8,128)(2,1)S(1)}, bf16[128,512]{1,0:T(8,128)(2,1)}, u32[]{:S(2)}) copy-start(bf16[128,512]{1,0:T(8,128)(2,1)} %refs_2_.2) | copy-start | bytes 393220
  0.0 53.8 %copy-start.8 = (f32[128]{0:T(128)S(1)}, f32[128]{0:T(128)}, u32[]{:S(2)}) copy-start(f32[128]{0:T(128)} %param.22) | copy-start | bytes 1540
  53.8 70.1 %copy-start.11 = (f32[128]{0:T(128)S(1)}, f32[128]{0:T(128)}, u32[]{:S(2)}) copy-start(f32[128]{0:T(128)} %param.25) | copy-start | bytes 1540
  128.3 38.1 %copy-start.1 = (bf16[128,512]{1,0:T(8,128)(2,1)S(1)}, bf16[128,512]{1,0:T(8,128)(2,1)}, u32[]{:S(2)}) copy-start(bf16[128,512]{1,0:T(8,128)(2,1)} %refs_2_.3) | copy-start | bytes 393220
  128.4 38.1 %copy-start.2 = (bf16[128,512]{1,0:T(8,128)(2,1)S(1)}, bf16[128,512]{1,0:T(8,128)(2,1)}, u32[]{:S(2)}) copy-start(bf16[128,512]{1,0:T(8,128)(2,1)} %refs_8_.1) | copy-start | bytes 393220
  128.4 38.1 %copy-start.3 = (bf16[512,128]{1,0:T(8,128)(2,1)S(1)}, bf16[512,128]{1,0:T(8,128)(2,1)}, u32[]{:S(2)}) copy-start(bf16[512,128]{1,0:T(8,128)(2,1)} %refs_10_.1) | copy-start | bytes 393220
  128.4 38.1 %copy-start.5 = (bf16[128,128]{1,0:T(8,128)(2,1)S(1)}, bf16[128,128]{1,0:T(8,128)(2,1)}, u32[]{:S(2)}) copy-start(bf16[128,128]{1,0:T(8,128)(2,1)} %refs_4_.3) | copy-start | bytes 98308
  128.4 38.1 %copy-start.6 = (f32[512]{0:T(512)S(1)}, f32[512]{0:T(512)}, u32[]{:S(2)}) copy-start(f32[512]{0:T(512)} %param.32) | copy-start | bytes 6148
  128.4 38.1 %copy-start.9 = (f32[128]{0:T(128)S(1)}, f32[128]{0:T(128)}, u32[]{:S(2)}) copy-start(f32[128]{0:T(128)} %param.27) | copy-start | bytes 1540
  128.4 38.1 %copy-start.10 = (f32[128]{0:T(128)S(1)}, f32[128]{0:T(128)}, u32[]{:S(2)}) copy-start(f32[128]{0:T(128)} %param.30) | copy-start | bytes 1540
  166.5 96.9 %copy-start.7 = (bf16[128,4]{0,1:T(4,128)(2,1)S(1)}, bf16[128,4]{0,1:T(4,128)(2,1)}, u32[]{:S(2)}) copy-start(bf16[128,4]{0,1:T(4,128)(2,1)} %param.28) | copy-start | bytes 3076

commit v7 on v5

--- a/solution.py
+++ b/solution.py
@@ -87,24 +87,25 @@
 
 
 def gather_kernel(n_out, *refs):
-    ins, outs = refs[:n_out], refs[n_out : 2 * n_out]
-    ring_send, ring_recv, pair_send, pair_recv, own_sem = refs[2 * n_out :]
+    ins, outs, held = refs[:n_out], refs[n_out : 2 * n_out], refs[2 * n_out : 3 * n_out]
+    ring_send, ring_recv, pair_send, pair_recv, own_sem, out_sem = refs[3 * n_out :]
     me = place()
     barrier = pltpu.get_barrier_semaphore()
     sib = {**me, "c": 1 - me["c"]}
     partners = [shift(me, d, by) for d in "xyz" for by in (1, -1)] + [sib]
     for at in partners:
         pl.semaphore_signal(barrier, inc=1, device_id=device(at), device_id_type=pl.DeviceIdType.MESH)
-    pl.semaphore_wait(barrier, len(partners))
-
-    def items(core):
-        half = outs[0].shape[-1] // 2
-        got = []
-        for h in range(HEADS):
-            got.append((h, ins[0].at[h], functools.partial(part, outs[0], (h,)), half))
-        if n_out == 2:
-            got.append((HEADS, ins[1], functools.partial(part, outs[1], ()), 0))
-        return got
+
+    todo = []
+    for h in range(HEADS):
+        todo.append((
+            h, ins[0].at[h], functools.partial(part, held[0], (h,)),
+            functools.partial(part, outs[0], (h,)), outs[0].shape[-1] // 2,
+        ))
+    if n_out == 2:
+        todo.append((
+            HEADS, ins[1], functools.partial(part, held[1], ()), functools.partial(part, outs[1], ()), 0
+        ))
 
     def copy(src, dst, sems, idx, to):
         return pltpu.make_async_remote_copy(
@@ -117,81 +118,117 @@
     def run(core):
         at = {**me, "c": core}
         other = {**me, "c": 1 - core}
-        todo = items(core)
-        sends = []
-
-        def step0(p, idx, own, sets, half):
-            d, free = ORDERS[core][idx][p], ORDERS[core][idx][:p]
-            src = sets(at, free)
+        sends, writes = [], []
+
+        def pieces(p, item):
+            order = ORDERS[core][item[0]]
+            if p == 2 and item[4]:
+                return [(v, {order[0]: v}, order[1]) for v in range(4)]
+            return [(0, {}, order[:p])]
+
+        def step0(p, item):
+            idx, own, sets, _, half = item
+            d = ORDERS[core][idx][p]
+            for v, fix, free in pieces(p, item):
+                src = sets({**at, **fix}, free)
+                for k, by in enumerate((1, -1)):
+                    c = copy(own if p == 0 else src, src, ring, (idx, p, v, k), shift(at, d, by))
+                    c.start()
+                    sends.append(c)
+
+        def step1(p, item, piece):
+            idx, own, sets, _, half = item
+            d = ORDERS[core][idx][p]
+            v, fix, free = piece
             for k, by in enumerate((1, -1)):
-                c = copy(own if p == 0 else src, src, ring, (idx, p, k), shift(at, d, by))
+                frm = {**shift(at, d, -by), **fix}
+                got = sets(frm, free)
+                copy(got, got, ring, (idx, p, v, k), shift(at, d, by)).wait_recv()
+                if half:
+                    got = sets(frm, free, (slice(None), pl.ds(k * half, half)))
+                elif k == 1:
+                    continue
+                c = copy(got, got, ring, (idx, p, v, 2 + k), shift(at, d, by))
                 c.start()
                 sends.append(c)
 
-        def step1(p, idx, own, sets, half):
-            d, free = ORDERS[core][idx][p], ORDERS[core][idx][:p]
+        def step2(p, item, piece):
+            idx, own, sets, _, half = item
+            d = ORDERS[core][idx][p]
+            v, fix, free = piece
             for k, by in enumerate((1, -1)):
-                got = sets(shift(at, d, -by), free)
-                copy(got, got, ring, (idx, p, k), shift(at, d, by)).wait_recv()
+                frm = {**shift(at, d, 2), **fix}
                 if half:
-                    tail = (slice(None), pl.ds(k * half, half))
-                    piece = sets(shift(at, d, -by), free, tail)
+                    got = sets(frm, free, (slice(None), pl.ds(k * half, half)))
                 elif k == 0:
-                    piece = got
+                    got = sets(frm, free)
                 else:
                     continue
-                c = copy(piece, piece, ring, (idx, p, 2 + k), shift(at, d, by))
-                c.start()
-                sends.append(c)
-
-        def step2(p, idx, own, sets, half):
-            d, free = ORDERS[core][idx][p], ORDERS[core][idx][:p]
-            for k, by in enumerate((1, -1)):
-                if half:
-                    tail = (slice(None), pl.ds(k * half, half))
-                    piece = sets(shift(at, d, 2), free, tail)
-                elif k == 0:
-                    piece = sets(shift(at, d, 2), free)
-                else:
-                    continue
-                copy(piece, piece, ring, (idx, p, 2 + k), shift(at, d, by)).wait_recv()
-
-        def across(idx, sets, hop):
+                copy(got, got, ring, (idx, p, v, 2 + k), shift(at, d, by)).wait_recv()
+
+        def write(item, where, free, number):
+            c = pltpu.make_async_copy(
+                item[2](where, free), item[3](where, free), out_sem.at[item[0], number]
+            )
+            c.start()
+            writes.append(c)
+
+        def across(item, hop):
+            idx, own, sets, _, half = item
             d, free = ORDERS[core][idx][2], ORDERS[core][idx][:2]
-            piece = sets(shift(at, d, hop), free)
-            c = copy(piece, piece, pair, (idx, hop), other)
+            where = shift(at, d, hop)
+            c = copy(sets(where, free), sets(where, free), pair, (idx, hop), other)
             c.start()
             sends.append(c)
+            write(item, where, free, hop)
 
         own_copies = []
-        for idx, own, sets, half in todo:
-            step0(0, idx, own, sets, half)
-            mine = pltpu.make_async_copy(own, sets(at, ""), own_sem.at[idx])
+        for item in todo:
+            mine = pltpu.make_async_copy(item[1], item[3](at, ""), own_sem.at[item[0]])
             mine.start()
             own_copies.append(mine)
+        pl.semaphore_wait(barrier, len(partners))
+        for item in todo:
+            step0(0, item)
+        for item, mine in zip(todo, own_copies):
+            mine.wait()
+            back = pltpu.make_async_copy(item[3](at, ""), item[2](at, ""), own_sem.at[item[0]])
+            back.start()
+            own_copies[item[0]] = back
         for p in range(3):
-            for t in todo:
-                step1(p, *t)
+            if p < 2:
+                for item in todo:
+                    step1(p, item, pieces(p, item)[0])
+            else:
+                for v in range(4):
+                    for item in todo:
+                        if v < len(pieces(p, item)):
+                            step1(p, item, pieces(p, item)[v])
+                for item in todo:
+                    for hop in (1, 3):
+                        across(item, hop)
+            for item in todo:
+                if p == 0:
+                    own_copies[item[0]].wait()
+                for piece in pieces(p, item):
+                    step2(p, item, piece)
+                if p < 2:
+                    step0(p + 1, item)
+                if p == 1:
+                    across(item, 0)
                 if p == 2:
-                    for hop in (1, 3):
-                        across(t[0], t[2], hop)
-            for i, t in enumerate(todo):
-                if p == 0:
-                    own_copies[i].wait()
-                step2(p, *t)
-                if p < 2:
-                    step0(p + 1, *t)
-                if p == 1:
-                    across(t[0], t[2], 0)
-                if p == 2:
-                    across(t[0], t[2], 2)
-        for idx, own, sets, half in todo:
-            d, free = ORDERS[1 - core][idx][2], ORDERS[1 - core][idx][:2]
-            for hop in range(4):
-                piece = sets(shift(other, d, hop), free)
-                copy(piece, piece, pair, (idx, hop), other).wait_recv()
+                    across(item, 2)
+        for hop in (0, 1, 3, 2):
+            for item in todo:
+                idx, own, sets, _, half = item
+                d, free = ORDERS[1 - core][idx][2], ORDERS[1 - core][idx][:2]
+                where = shift(other, d, hop)
+                copy(sets(where, free), sets(where, free), pair, (idx, hop), other).wait_recv()
+                write(item, where, free, 4 + hop)
         for c in sends:
             c.wait_send()
+        for c in writes:
+            c.wait()
 
     for core in range(2):
         pl.when(me["c"] == core)(functools.partial(run, core))
@@ -209,14 +246,18 @@
         out_shape=outs,
         in_specs=[VMEM] * n,
         out_specs=[pl.BlockSpec(memory_space=pl.ANY)] * n,
-        scratch_shapes=[
-            pltpu.SemaphoreType.DMA((5, 3, 4)),
-            pltpu.SemaphoreType.DMA((5, 3, 4)),
+        scratch_shapes=[pltpu.VMEM(o.shape, o.dtype) for o in outs]
+        + [
+            pltpu.SemaphoreType.DMA((5, 3, 4, 4)),
+            pltpu.SemaphoreType.DMA((5, 3, 4, 4)),
             pltpu.SemaphoreType.DMA((5, 4)),
             pltpu.SemaphoreType.DMA((5, 4)),
             pltpu.SemaphoreType.DMA((5,)),
+            pltpu.SemaphoreType.DMA((5, 8)),
         ],
-        compiler_params=pltpu.CompilerParams(collective_id=cid, has_side_effects=True),
+        compiler_params=pltpu.CompilerParams(
+            collective_id=cid, has_side_effects=True, vmem_limit_bytes=60 * 1024 * 1024
+        ),
     )(bias, *mask)
     full = got[0].reshape(heads, -1, res)
     return (full, got[1].reshape((-1,) + mask[0].shape)) if mask else full
@@ -651,8 +692,9 @@
     )(*args)
 
 
-def exchange_kernel(n, z_ref, o_ref, send_sem, recv_sem, own_sem):
-    rows = o_ref.shape[0]
+def exchange_kernel(n, whole, z_ref, o_ref, send_sem, recv_sem, own_sem):
+    rows = z_ref.shape[1]
+    cut = lambda d: z_ref if whole else z_ref.at[pl.ds(pl.multiple_of(rows * d, rows), rows)]
     gy = n // 16
     me = lax.axis_index("gx") * gy + lax.axis_index("gy")
     at = lambda d: {"gx": d // gy, "gy": lax.rem(d, gy)}
@@ -666,13 +708,13 @@
 
     lax.fori_loop(1, n, greet, 0)
     mine = pl.ds(pl.multiple_of(rows * me, rows), rows)
-    own = pltpu.make_async_copy(z_ref.at[mine], o_ref.at[:, mine], own_sem)
+    own = pltpu.make_async_copy(cut(me), o_ref.at[:, mine], own_sem)
     own.start()
     pl.semaphore_wait(barrier, n - 1)
 
     def copy(t, to, frm):
         return pltpu.make_async_remote_copy(
-            src_ref=z_ref.at[pl.ds(pl.multiple_of(rows * to, rows), rows)],
+            src_ref=cut(to),
             dst_ref=o_ref.at[:, pl.ds(pl.multiple_of(rows * frm, rows), rows)],
             send_sem=send_sem.at[t], recv_sem=recv_sem.at[t],
             device_id=at(to), device_id_type=pl.DeviceIdType.MESH,
@@ -693,11 +735,12 @@
     lax.fori_loop(1, n, land, 0)
 
 
-def exchange(cid, n, z, rows):
-    res, _, chan = z.shape
+def exchange(cid, n, z, whole=False):
+    lead, rows, width = z.shape
+    shape = (lead, n * rows, width) if whole else (rows, lead, width)
     return pl.pallas_call(
-        functools.partial(exchange_kernel, n),
-        out_shape=jax.ShapeDtypeStruct((rows, res, chan), BF16),
+        functools.partial(exchange_kernel, n, whole),
+        out_shape=jax.ShapeDtypeStruct(shape, BF16),
         in_specs=[pl.BlockSpec(memory_space=pl.ANY)],
         out_specs=pl.BlockSpec(memory_space=pl.ANY),
         scratch_shapes=[
@@ -742,16 +785,16 @@
 
     def end_inputs(cols):
         bias, normed = pair_bias(cols, row(norm_end), bias_w_end)
-        return [cols, normed] + ends, gather(1, bias)
+        return [cols, normed] + ends, bias
 
     def safe(bias):
-        cols = exchange(4, n, safe_attention(start, bias, False), rows)
+        cols = exchange(4, n, safe_attention(start, bias, False))
         ins, bias = end_inputs(cols)
-        return exchange(5, n, safe_attention(ins, bias, True), rows)
+        return exchange(5, n, safe_attention(ins, exchange(6, n, bias, True), True))
 
     cols, good = fused_attention(2, n, start, bias, None)
     ins, end_bias = end_inputs(cols)
-    out, flags = fused_attention(3, n, ins, end_bias, good)
+    out, flags = fused_attention(3, n, ins, gather(1, end_bias), good)
     return lax.cond(jnp.min(flags[:, 0]) > 0.5, lambda b: out, safe, bias)
 
 

time: 261 us -> 269 us (1.031)
  Pallas kernels: 247 us -> 255 us
    pallas_call x2, Pallas kernels: 78.4 us -> 85.6 us  [gather(): pl.pallas_call(functools.partial(gather_kernel, n), out_shape=outs, in_sp...]
where the time goes in v7:
time: 269 us; the launch traced here: 268 us
  Pallas kernels  255 us (95%)
  local copies, waits for them, and re-layouts  8.89 us (3%)
  other arithmetic  3.25 us (1%)
    pallas_call x2, Pallas kernels, fused_attention(): pl.pallas_call(functools.partial(fused_kernel, trans, n, names + list(out...  160 us
    pallas_call x2, Pallas kernels, gather(): pl.pallas_call(functools.partial(gather_kernel, n), out_shape=outs, in_sp...  85.6 us
    pallas_call x2, Pallas kernels, pair_bias(): pl.pallas_call(bias_kernel, out_shape=[jax.ShapeDtypeStruct((HEADS, rows,...  8.94 us

profile of v7, /device:TPU:1, one launch (start us, length us, event | category | flops | bytes accessed | tf_op | source)
XLA Modules:
  0.0 268.4 jit_solution(9531978068169009581)
XLA Ops:
  0.0 0.0 copy-start
  0.0 0.0 copy-start.5
  0.0 0.0 copy-start.1
  0.0 0.0 copy-start.9
  0.0 0.8 convert_bitcast_fusion
  0.8 0.6 pad.15.refs_1_
  1.4 0.8 copy.23
  2.2 0.6 pad.14.bw_ref
  2.8 0.8 copy.26
  3.7 0.6 pad.16.bw_ref
  4.3 4.5 %shard_map.156 = (bf16[4,8,1024]{2,1,0:T(8,128)(2,1)}, bf16[8,1024,128]{2,1,0:T(8,128)(2,1)}) custom-call(bf16[8,1024,128]{2,1,0:T(8,128)(2,1)} %refs_0_.1, f32[1,128]{1,0:T(1,128)} %bitcast.33, bf16[128,128]{1,0:T(8,128)(2,1)} %pad.14.bw_ref), custom_call_target="tpu_custom_call" | custom-call | tf_op jit(solution)/shard_map/pallas_call | solution.py:45
  8.7 46.3 %shard_map.157 = (bf16[4,2,4,2,4,2,8,1024]{7,6,5,4,3,2,1,0:T(8,128)(2,1)}, f32[2,4,2,4,2,8,128]{6,5,4,3,2,1,0:T(8,128)}) custom-call(bf16[4,8,1024]{2,1,0:T(8,128)(2,1)} %get-tuple-element.73.refs_0_, f32[8,128]{1,0:T(8,128)} %pad.15.refs_1_), custom_call_target="tpu_custom_call" | custom-call | tf_op jit(solution)/shard_map/pallas_call | solution.py:244
  55.0 1.1 slice.8
  56.1 0.6 reduce_max.9
  57.4 0.1 select_n.30.refs_5_
  57.5 0.1 select_n.31
  57.6 1.0 copy.25.refs_6_
  58.6 0.0 copy-done
  58.6 0.0 copy-done.5
  58.6 0.0 copy-done.1
  58.6 0.0 copy-done.9
  58.6 0.0 copy-start.12
  58.7 67.7 %shard_map.158 = (bf16[8,1024,128]{2,1,0:T(8,128)(2,1)}, f32[8,128]{1,0:T(8,128)}) custom-call(bf16[8,1024,128]{2,1,0:T(8,128)(2,1)S(1)} %copy-done, bf16[8,1024,128]{2,1,0:T(8,128)(2,1)} %get-tuple-element.72.refs_1_, bf16[128,512]{1,0:T(8,128)(2,1)S(1)} %copy-done.1, f32[1,128]{1,0:T(1,128)S(1)} %bitcast.25, bf16[128,128]{1,0:T(8,128)(2,1)S(1)} %copy-done.5, ...), custom_call_target="tpu_custom_call" | custom-call | tf_op jit(solution)/shard_map/pallas_call | solution.py:683
  126.4 0.0 copy-done.12
  126.4 4.5 %shard_map.159 = (bf16[4,8,1024]{2,1,0:T(8,128)(2,1)}, bf16[8,1024,128]{2,1,0:T(8,128)(2,1)}) custom-call(bf16[8,1024,128]{2,1,0:T(8,128)(2,1)} %get-tuple-element.76.x_ref.refs_0_, f32[1,128]{1,0:T(1,128)S(1)} %bitcast.31, bf16[128,128]{1,0:T(8,128)(2,1)} %pad.16.bw_ref), custom_call_target="tpu_custom_call" | custom-call | tf_op jit(solution)/shard_map/pallas_call | solution.py:45
  130.9 0.0 copy-start.2
  130.9 0.0 copy-start.3
  130.9 0.0 copy-start.4
  130.9 0.0 copy-start.6
  130.9 0.0 copy-start.7
  130.9 0.0 copy-start.10
  130.9 0.0 copy-start.11
  131.0 39.3 %shard_map.160 = bf16[4,2,4,2,4,2,8,1024]{7,6,5,4,3,2,1,0:T(8,128)(2,1)} custom-call(bf16[4,8,1024]{2,1,0:T(8,128)(2,1)} %get-tuple-element.78.refs_0_), custom_call_target="tpu_custom_call" | custom-call | tf_op jit(solution)/shard_map/pallas_call | solution.py:244
  170.2 0.0 copy-done.2
  170.2 0.0 copy-done.3
  170.3 0.0 copy-done.4
  170.3 0.0 copy-done.6
  170.3 0.0 copy-done.7
  170.3 0.0 copy-done.10
  170.3 0.0 copy-done.11
  170.3 0.0 copy-start.8
  170.3 92.3 %shard_map.161 = (bf16[8,1024,128]{2,1,0:T(8,128)(2,1)}, f32[128,8,128]{2,1,0:T(8,128)}) custom-call(bf16[8,1024,128]{2,1,0:T(8,128)(2,1)} %get-tuple-element.76.x_ref.refs_0_, bf16[8,1024,128]{2,1,0:T(8,128)(2,1)} %get-tuple-element.77.refs_1_, bf16[128,512]{1,0:T(8,128)(2,1)S(1)} %copy-done.2, f32[1,128]{1,0:T(1,128)S(1)} %bitcast.27, ...), custom_call_target="tpu_custom_call" | custom-call | tf_op jit(solution)/shard_map/pallas_call | solution.py:683
  262.7 1.8 slice_reduce_fusion
  265.1 0.0 copy-done.8
  265.1 0.3 conditional.1
  265.4 3.1 %copy.34 = bf16[8,1024,128]{2,1,0:T(8,128)(2,1)} copy(bf16[8,1024,128]{2,1,0:T(8,128)(2,1)} %get-tuple-element.82) | data formatting | bytes 4194304
  (1 shorter events, 0.0 us)
Async XLA Ops:
  0.0 58.6 %copy-start = (bf16[8,1024,128]{2,1,0:T(8,128)(2,1)S(1)}, bf16[8,1024,128]{2,1,0:T(8,128)(2,1)}, u32[]{:S(2)}) copy-start(bf16[8,1024,128]{2,1,0:T(8,128)(2,1)} %refs_0_.1) | copy-start | bytes 6291460
  0.0 58.6 %copy-start.5 = (bf16[128,128]{1,0:T(8,128)(2,1)S(1)}, bf16[128,128]{1,0:T(8,128)(2,1)}, u32[]{:S(2)}) copy-start(bf16[128,128]{1,0:T(8,128)(2,1)} %refs_4_.2) | copy-start | bytes 98308
  0.0 58.6 %copy-start.1 = (bf16[128,512]{1,0:T(8,128)(2,1)S(1)}, bf16[128,512]{1,0:T(8,128)(2,1)}, u32[]{:S(2)}) copy-start(bf16[128,512]{1,0:T(8,128)(2,1)} %refs_2_.2) | copy-start | bytes 393220
  0.0 58.6 %copy-start.9 = (f32[128]{0:T(128)S(1)}, f32[128]{0:T(128)}, u32[]{:S(2)}) copy-start(f32[128]{0:T(128)} %param.22) | copy-start | bytes 1540
  58.6 67.8 %copy-start.12 = (f32[128]{0:T(128)S(1)}, f32[128]{0:T(128)}, u32[]{:S(2)}) copy-start(f32[128]{0:T(128)} %param.25) | copy-start | bytes 1540
  130.9 39.3 %copy-start.2 = (bf16[128,512]{1,0:T(8,128)(2,1)S(1)}, bf16[128,512]{1,0:T(8,128)(2,1)}, u32[]{:S(2)}) copy-start(bf16[128,512]{1,0:T(8,128)(2,1)} %refs_2_.3) | copy-start | bytes 393220
  130.9 39.3 %copy-start.3 = (bf16[128,512]{1,0:T(8,128)(2,1)S(1)}, bf16[128,512]{1,0:T(8,128)(2,1)}, u32[]{:S(2)}) copy-start(bf16[128,512]{1,0:T(8,128)(2,1)} %refs_8_.1) | copy-start | bytes 393220
  130.9 39.4 %copy-start.4 = (bf16[512,128]{1,0:T(8,128)(2,1)S(1)}, bf16[512,128]{1,0:T(8,128)(2,1)}, u32[]{:S(2)}) copy-start(bf16[512,128]{1,0:T(8,128)(2,1)} %refs_10_.1) | copy-start | bytes 393220
  130.9 39.4 %copy-start.6 = (bf16[128,128]{1,0:T(8,128)(2,1)S(1)}, bf16[128,128]{1,0:T(8,128)(2,1)}, u32[]{:S(2)}) copy-start(bf16[128,128]{1,0:T(8,128)(2,1)} %refs_4_.3) | copy-start | bytes 98308
  130.9 39.4 %copy-start.7 = (f32[512]{0:T(512)S(1)}, f32[512]{0:T(512)}, u32[]{:S(2)}) copy-start(f32[512]{0:T(512)} %param.32) | copy-start | bytes 6148
  130.9 39.4 %copy-start.10 = (f32[128]{0:T(128)S(1)}, f32[128]{0:T(128)}, u32[]{:S(2)}) copy-start(f32[128]{0:T(128)} %param.27) | copy-start | bytes 1540
  130.9 39.4 %copy-start.11 = (f32[128]{0:T(128)S(1)}, f32[128]{0:T(128)}, u32[]{:S(2)}) copy-start(f32[128]{0:T(128)} %param.30) | copy-start | bytes 1540
  170.3 94.8 %copy-start.8 = (bf16[128,4]{0,1:T(4,128)(2,1)S(1)}, bf16[128,4]{0,1:T(4,128)(2,1)}, u32[]{:S(2)}) copy-start(bf16[128,4]{0,1:T(4,128)(2,1)} %param.28) | copy-start | bytes 3076

commit v8 on v6

--- a/solution.py
+++ b/solution.py
@@ -29,12 +29,22 @@
     return (cent * lax.rsqrt(var + 1e-05) * gain).astype(BF16)
 
 
-def bias_kernel(x_ref, g_ref, bw_ref, o_ref, a_ref):
+def owner(c, i):
+    x, z_lo, core, z_hi = i // 8, (i // 4) % 2, (i // 2) % 2, i % 2
+    y = (c - x + 4) % 4
+    return ((z_lo * 4 + x) * 2 + core) * 8 + y * 2 + z_hi
+
+
+def bias_kernel(x_ref, g_ref, bw_ref, o_ref, a_ref, xq_ref, aq_ref):
     bwt = bw_ref[...].astype(F32).T.astype(BF16)
     gain = g_ref[...]
     for r in range(x_ref.shape[0]):
         a = layer_norm(x_ref[r], gain)
         a_ref[r] = a
+        for p in range(x_ref.shape[1] // 16):
+            at = owner(p // 16, 2 * (p % 16)) * 8
+            aq_ref[r, 16 * p : 16 * p + 16] = a[at : at + 16]
+            xq_ref[r, 16 * p : 16 * p + 16] = x_ref[r, at : at + 16]
         b = lax.dot_general(bwt, a, NT, preferred_element_type=F32) * LOG2E
         o_ref[:, r, :] = b[:HEADS].astype(BF16)
 
@@ -47,9 +57,11 @@
         out_shape=[
             jax.ShapeDtypeStruct((HEADS, rows, res), BF16),
             jax.ShapeDtypeStruct(x.shape, BF16),
+            jax.ShapeDtypeStruct(x.shape, BF16),
+            jax.ShapeDtypeStruct(x.shape, BF16),
         ],
         in_specs=[VMEM] * 3,
-        out_specs=[VMEM] * 2,
+        out_specs=[VMEM] * 4,
     )(x, gain, bw)
 
 
@@ -476,13 +488,8 @@
 
     lax.fori_loop(1, n, greet, 0)
 
-    def owner(c, i):
-        x, z_lo, core = i // 8, lax.rem(i // 4, 2), lax.rem(i // 2, 2)
-        y = lax.rem(c - x + 4, 4)
-        return ((z_lo * 4 + x) * 2 + core) * ny + y * 2 + lax.rem(i, 2)
-
     def block_of(t):
-        return lax.rem(t + lax.rem(gx // 2, 4), nj)
+        return lax.rem(t + lax.rem(gx // 2, 4) + gy // 2 + 2 * lax.rem(gy, 2) + gx // 8, nj)
 
     def chunk(c, u):
         return pl.ds(pl.multiple_of(owner(c, 2 * u) * rows, 2 * rows), 2 * rows)
@@ -501,14 +508,6 @@
 
     def fetched():
         pltpu.make_async_copy(m.b.at[:, pl.ds(0, JB)], m.bs, m.fetch_sem).wait()
-
-    def sort_rows(src, dst, sem):
-        def one(k, carry):
-            c, u = k // (per // 2), lax.rem(k, per // 2)
-            pltpu.make_async_copy(src.at[:, chunk(c, u)], dst.at[:, slot(c, u)], sem).start()
-            return carry
-
-        lax.fori_loop(0, nj * per // 2, one, 0)
 
     def copy(t, i, frm):
         to = owner(block_of(t), i)
@@ -563,12 +562,8 @@
 
         lax.fori_loop(0, per, sent, 0)
 
-    sort_rows(m.ah, m.aq, m.sort_sem.at[0])
-    sort_rows(m.xh, m.x, m.sort_sem.at[1])
     fetch(0)
-    pltpu.make_async_copy(m.ah, m.aq, m.sort_sem.at[0]).wait()
     tools.project_all()
-    pltpu.make_async_copy(m.xh, m.x, m.sort_sem.at[1]).wait()
     m.gd[...] = jnp.ones_like(m.gd)
     pl.semaphore_wait(barrier, n - 1)
 
@@ -651,18 +646,15 @@
         "zs": pltpu.VMEM((2, JB, rows, chan), BF16),
         "send_sem": pltpu.SemaphoreType.DMA((n,)),
         "recv_sem": pltpu.SemaphoreType.DMA((n,)),
-        "x": pltpu.VMEM((rows, res, chan), BF16),
-        "aq": pltpu.VMEM((rows, res, chan), BF16),
-        "sort_sem": pltpu.SemaphoreType.DMA((2,)),
         "fetch_sem": pltpu.SemaphoreType.DMA,
         "own_sem": pltpu.SemaphoreType.DMA,
     }
     anywhere = pl.BlockSpec(memory_space=pl.ANY)
     outs = {"o": jax.ShapeDtypeStruct((rows, res, chan), BF16)}
     out_specs = [anywhere]
-    names = ["xh"] + stage_names(trans)[1:] + ["ah", "b"]
-    args = list(ins) + [ins[1], bias]
-    in_specs = [anywhere] + [VMEM] * (len(ins) - 1) + [anywhere] * 2
+    names = stage_names(trans) + ["aq", "b"]
+    args = list(ins) + [bias]
+    in_specs = [VMEM] * len(ins) + [anywhere]
     if trans:
         names.append("before")
         args.append(before)
@@ -689,8 +681,9 @@
     )(*args)
 
 
-def exchange_kernel(n, z_ref, o_ref, send_sem, recv_sem, own_sem):
-    rows = o_ref.shape[0]
+def exchange_kernel(n, whole, z_ref, o_ref, send_sem, recv_sem, own_sem):
+    rows = z_ref.shape[1]
+    cut = lambda d: z_ref if whole else z_ref.at[pl.ds(pl.multiple_of(rows * d, rows), rows)]
     gy = n // 16
     me = lax.axis_index("gx") * gy + lax.axis_index("gy")
     at = lambda d: {"gx": d // gy, "gy": lax.rem(d, gy)}
@@ -704,13 +697,13 @@
 
     lax.fori_loop(1, n, greet, 0)
     mine = pl.ds(pl.multiple_of(rows * me, rows), rows)
-    own = pltpu.make_async_copy(z_ref.at[mine], o_ref.at[:, mine], own_sem)
+    own = pltpu.make_async_copy(cut(me), o_ref.at[:, mine], own_sem)
     own.start()
     pl.semaphore_wait(barrier, n - 1)
 
     def copy(t, to, frm):
         return pltpu.make_async_remote_copy(
-            src_ref=z_ref.at[pl.ds(pl.multiple_of(rows * to, rows), rows)],
+            src_ref=cut(to),
             dst_ref=o_ref.at[:, pl.ds(pl.multiple_of(rows * frm, rows), rows)],
             send_sem=send_sem.at[t], recv_sem=recv_sem.at[t],
             device_id=at(to), device_id_type=pl.DeviceIdType.MESH,
@@ -731,11 +724,12 @@
     lax.fori_loop(1, n, land, 0)
 
 
-def exchange(cid, n, z, rows):
-    res, _, chan = z.shape
+def exchange(cid, n, z, whole=False):
+    lead, rows, width = z.shape
+    shape = (lead, n * rows, width) if whole else (rows, lead, width)
     return pl.pallas_call(
-        functools.partial(exchange_kernel, n),
-        out_shape=jax.ShapeDtypeStruct((rows, res, chan), BF16),
+        functools.partial(exchange_kernel, n, whole),
+        out_shape=jax.ShapeDtypeStruct(shape, BF16),
         in_specs=[pl.BlockSpec(memory_space=pl.ANY)],
         out_specs=pl.BlockSpec(memory_space=pl.ANY),
         scratch_shapes=[
@@ -769,7 +763,7 @@
     n = lax.axis_size(("gx", "gy"))
     row = lambda v: v.reshape(1, -1)
     mine = jnp.pad(residue_mask.astype(F32).reshape(1, rows), ((0, 7), (0, 128 - rows)))
-    bias, normed = pair_bias(pair_in, row(norm_start), bias_w_start)
+    bias, normed, turned, turned_a = pair_bias(pair_in, row(norm_start), bias_w_start)
     bias, mask = gather(0, bias, mine)
     mask = mask[:, 0, :rows].reshape(res)
     mask = jnp.where(jnp.max(mask) > 0.5, mask, 1.0)
@@ -779,17 +773,17 @@
     ends += [row(norm_trans), trans_in, row(trans_bias), trans_out]
 
     def end_inputs(cols):
-        bias, normed = pair_bias(cols, row(norm_end), bias_w_end)
-        return [cols, normed] + ends, gather(1, bias)
+        bias, normed, turned, turned_a = pair_bias(cols, row(norm_end), bias_w_end)
+        return [cols, normed] + ends, [turned, normed] + ends + [turned_a], bias
 
     def safe(bias):
-        cols = exchange(4, n, safe_attention(start, bias, False), rows)
-        ins, bias = end_inputs(cols)
-        return exchange(5, n, safe_attention(ins, bias, True), rows)
-
-    cols, good = fused_attention(2, n, start, bias, None)
-    ins, end_bias = end_inputs(cols)
-    out, flags = fused_attention(3, n, ins, end_bias, good)
+        cols = exchange(4, n, safe_attention(start, bias, False))
+        ins, _, bias = end_inputs(cols)
+        return exchange(5, n, safe_attention(ins, exchange(6, n, bias, True), True))
+
+    cols, good = fused_attention(2, n, [turned] + start[1:] + [turned_a], bias, None)
+    _, ins, end_bias = end_inputs(cols)
+    out, flags = fused_attention(3, n, ins, gather(1, end_bias), good)
     return lax.cond(jnp.min(flags[:, 0]) > 0.5, lambda b: out, safe, bias)
 
 

time: 267 us -> 264 us (0.989)
    pallas_call x2, Pallas kernels: 164 us -> 160 us  [fused_attention(): pl.pallas_call(functools.partial(fused_kernel, trans, n, names + list(out...]
    pallas_call x2, Pallas kernels: 8.35 us -> 11.3 us  [pair_bias(): pl.pallas_call(bias_kernel, out_shape=[jax.ShapeDtypeStruct((HEADS, rows,...]
where the time goes in v8:
time: 264 us
  Pallas kernels  251 us (95%)
  local copies, waits for them, and re-layouts  8.27 us (3%)
    pallas_call x2, Pallas kernels, fused_attention(): pl.pallas_call(functools.partial(fused_kernel, trans, n, names + list(out...  160 us
    pallas_call x2, Pallas kernels, gather(): pl.pallas_call(functools.partial(gather_kernel, n), out_shape=outs, in_sp...  80.1 us
    pallas_call x2, Pallas kernels, pair_bias(): pl.pallas_call(bias_kernel, out_shape=[jax.ShapeDtypeStruct((HEADS, rows,...  11.3 us

profile of v8, /device:TPU:1, one launch (start us, length us, event | category | flops | bytes accessed | tf_op | source)
XLA Modules:
  0.0 263.8 jit_solution(11102221372540035299)
XLA Ops:
  0.0 0.0 copy-start.12
  0.0 0.0 copy-start.8
  0.0 0.0 copy-start
  0.0 0.0 copy-start.4
  0.0 0.9 copy.23
  0.9 0.6 pad.14.bw_ref
  1.5 5.4 %shard_map.156 = (bf16[4,8,1024]{2,1,0:T(8,128)(2,1)}, bf16[8,1024,128]{2,1,0:T(8,128)(2,1)S(1)}, bf16[8,1024,128]{2,1,0:T(8,128)(2,1)}, bf16[8,1024,128]{2,1,0:T(8,128)(2,1)}) custom-call(bf16[8,1024,128]{2,1,0:T(8,128)(2,1)} %x_ref.1, f32[1,128]{1,0:T(1,128)} %bitcast.33, bf16[128,128]{1,0:T(8,128)(2,1)} %pad.14.bw_ref), custom_call_target="tpu_custom_call" | custom-call | tf_op jit(solution)/shard_map/pallas_call | solution.py:55
  6.9 0.0 copy-done.12
  6.9 0.6 pad.15.refs_1_
  7.5 42.1 %shard_map.157 = (bf16[4,2,4,2,4,2,8,1024]{7,6,5,4,3,2,1,0:T(8,128)(2,1)}, f32[2,4,2,4,2,8,128]{6,5,4,3,2,1,0:T(8,128)}) custom-call(bf16[4,8,1024]{2,1,0:T(8,128)(2,1)} %get-tuple-element.78.refs_0_, f32[8,128]{1,0:T(8,128)} %pad.15.refs_1_), custom_call_target="tpu_custom_call" | custom-call | tf_op jit(solution)/shard_map/pallas_call | solution.py:219
  49.7 1.1 slice.8
  50.7 0.7 reduce_max.9
  52.0 0.1 select_n.31
  52.1 1.0 copy.25.refs_6_
  53.2 0.1 select_n.30.refs_5_
  53.3 0.0 copy-done.8
  53.3 0.0 copy-done
  53.3 0.0 copy-done.4
  53.3 0.0 copy-start.7
  53.3 0.0 copy-start.11
  53.3 68.0 %shard_map.158 = (bf16[8,1024,128]{2,1,0:T(8,128)(2,1)}, f32[8,128]{1,0:T(8,128)}) custom-call(bf16[8,1024,128]{2,1,0:T(8,128)(2,1)} %get-tuple-element.76.refs_0_, bf16[8,1024,128]{2,1,0:T(8,128)(2,1)S(1)} %get-tuple-element.77.refs_1_, bf16[128,512]{1,0:T(8,128)(2,1)S(1)} %copy-done, f32[1,128]{1,0:T(1,128)S(1)} %bitcast.25, ...), custom_call_target="tpu_custom_call" | custom-call | tf_op jit(solution)/shard_map/pallas_call | solution.py:672
  121.3 0.0 copy-done.7
  121.4 0.1 copy.26
  121.5 0.6 pad.16.bw_ref
  122.1 0.0 copy-done.11
  122.1 5.9 %shard_map.159 = (bf16[4,8,1024]{2,1,0:T(8,128)(2,1)}, bf16[8,1024,128]{2,1,0:T(8,128)(2,1)}, bf16[8,1024,128]{2,1,0:T(8,128)(2,1)}, bf16[8,1024,128]{2,1,0:T(8,128)(2,1)}) custom-call(bf16[8,1024,128]{2,1,0:T(8,128)(2,1)} %get-tuple-element.82.x_ref, f32[1,128]{1,0:T(1,128)S(1)} %bitcast.31, bf16[128,128]{1,0:T(8,128)(2,1)} %pad.16.bw_ref), custom_call_target="tpu_custom_call" | custom-call | tf_op jit(solution)/shard_map/pallas_call | solution.py:55
  128.0 0.0 copy-start.1
  128.0 0.0 copy-start.2
  128.0 0.0 copy-start.3
  128.0 0.0 copy-start.5
  128.0 0.0 copy-start.6
  128.0 0.0 copy-start.9
  128.0 0.0 copy-start.10
  128.0 37.9 %shard_map.160 = bf16[4,2,4,2,4,2,8,1024]{7,6,5,4,3,2,1,0:T(8,128)(2,1)} custom-call(bf16[4,8,1024]{2,1,0:T(8,128)(2,1)} %get-tuple-element.86.refs_0_), custom_call_target="tpu_custom_call" | custom-call | tf_op jit(solution)/shard_map/pallas_call | solution.py:219
  166.0 0.0 copy-done.1
  166.0 0.0 copy-done.2
  166.0 0.0 copy-done.3
  166.0 0.0 copy-done.5
  166.0 0.0 copy-done.6
  166.0 0.0 copy-done.9
  166.0 0.0 copy-done.10
  166.0 92.0 %shard_map.161 = (bf16[8,1024,128]{2,1,0:T(8,128)(2,1)}, f32[128,8,128]{2,1,0:T(8,128)}) custom-call(bf16[8,1024,128]{2,1,0:T(8,128)(2,1)} %get-tuple-element.83.refs_0_, bf16[8,1024,128]{2,1,0:T(8,128)(2,1)} %get-tuple-element.84.refs_1_, bf16[128,512]{1,0:T(8,128)(2,1)S(1)} %copy-done.1, f32[1,128]{1,0:T(1,128)S(1)} %bitcast.27, ...), custom_call_target="tpu_custom_call" | custom-call | tf_op jit(solution)/shard_map/pallas_call | solution.py:672
  258.0 1.8 slice_reduce_fusion
  260.5 0.3 conditional.1
  260.7 3.1 %copy.34 = bf16[8,1024,128]{2,1,0:T(8,128)(2,1)} copy(bf16[8,1024,128]{2,1,0:T(8,128)(2,1)} %get-tuple-element.90) | data formatting | bytes 4194304
  (2 shorter events, 0.0 us)
Async XLA Ops:
  0.0 6.9 %copy-start.12 = (s32[8]{0:T(128)S(1)}, s32[8]{0:T(128)}, u32[]{:S(2)}) copy-start(s32[8]{0:T(128)} %param.19) | copy-start | bytes 100
  0.0 53.3 %copy-start.8 = (f32[128]{0:T(128)S(1)}, f32[128]{0:T(128)}, u32[]{:S(2)}) copy-start(f32[128]{0:T(128)} %param.22) | copy-start | bytes 1540
  0.0 53.3 %copy-start = (bf16[128,512]{1,0:T(8,128)(2,1)S(1)}, bf16[128,512]{1,0:T(8,128)(2,1)}, u32[]{:S(2)}) copy-start(bf16[128,512]{1,0:T(8,128)(2,1)} %refs_2_.2) | copy-start | bytes 393220
  0.0 53.3 %copy-start.4 = (bf16[128,128]{1,0:T(8,128)(2,1)S(1)}, bf16[128,128]{1,0:T(8,128)(2,1)}, u32[]{:S(2)}) copy-start(bf16[128,128]{1,0:T(8,128)(2,1)} %refs_4_.2) | copy-start | bytes 98308
  53.3 68.0 %copy-start.7 = (bf16[128,4]{0,1:T(4,128)(2,1)S(1)}, bf16[128,4]{0,1:T(4,128)(2,1)}, u32[]{:S(2)}) copy-start(bf16[128,4]{0,1:T(4,128)(2,1)} %param.28) | copy-start | bytes 3076
  53.3 68.8 %copy-start.11 = (f32[128]{0:T(128)S(1)}, f32[128]{0:T(128)}, u32[]{:S(2)}) copy-start(f32[128]{0:T(128)} %param.25) | copy-start | bytes 1540
  128.0 38.0 %copy-start.1 = (bf16[128,512]{1,0:T(8,128)(2,1)S(1)}, bf16[128,512]{1,0:T(8,128)(2,1)}, u32[]{:S(2)}) copy-start(bf16[128,512]{1,0:T(8,128)(2,1)} %refs_2_.3) | copy-start | bytes 393220
  128.0 38.0 %copy-start.2 = (bf16[128,512]{1,0:T(8,128)(2,1)S(1)}, bf16[128,512]{1,0:T(8,128)(2,1)}, u32[]{:S(2)}) copy-start(bf16[128,512]{1,0:T(8,128)(2,1)} %refs_8_.1) | copy-start | bytes 393220
  128.0 38.0 %copy-start.3 = (bf16[512,128]{1,0:T(8,128)(2,1)S(1)}, bf16[512,128]{1,0:T(8,128)(2,1)}, u32[]{:S(2)}) copy-start(bf16[512,128]{1,0:T(8,128)(2,1)} %refs_10_.1) | copy-start | bytes 393220
  128.0 38.0 %copy-start.5 = (bf16[128,128]{1,0:T(8,128)(2,1)S(1)}, bf16[128,128]{1,0:T(8,128)(2,1)}, u32[]{:S(2)}) copy-start(bf16[128,128]{1,0:T(8,128)(2,1)} %refs_4_.3) | copy-start | bytes 98308
  128.0 38.0 %copy-start.6 = (f32[512]{0:T(512)S(1)}, f32[512]{0:T(512)}, u32[]{:S(2)}) copy-start(f32[512]{0:T(512)} %param.32) | copy-start | bytes 6148
  128.0 38.0 %copy-start.9 = (f32[128]{0:T(128)S(1)}, f32[128]{0:T(128)}, u32[]{:S(2)}) copy-start(f32[128]{0:T(128)} %param.27) | copy-start | bytes 1540
  128.0 38.0 %copy-start.10 = (f32[128]{0:T(128)S(1)}, f32[128]{0:T(128)}, u32[]{:S(2)}) copy-start(f32[128]{0:T(128)} %param.30) | copy-start | bytes 1540

commit v9 on v5

--- a/solution.py
+++ b/solution.py
@@ -481,56 +481,46 @@
             m.b.at[:, pl.ds(pl.multiple_of(block_of(t) * JB, JB), JB)], m.bs, m.fetch_sem
         )
 
-    def copy(t, i, frm):
-        to = block_of(t) * per + i
-        ahead = lax.rem(to - me + n, n)
-        return to, pltpu.make_async_remote_copy(
-            src_ref=m.zs.at[lax.rem(t, 2), pl.ds(pl.multiple_of(i * rows, rows), rows)],
-            dst_ref=m.o.at[:, pl.ds(pl.multiple_of(rows * frm, rows), rows)],
-            send_sem=m.send_sem.at[ahead], recv_sem=m.recv_sem.at[ahead],
-            device_id=at(to), device_id_type=pl.DeviceIdType.MESH,
-        )
-
-    def own(t, i):
-        mine = pl.ds(pl.multiple_of(rows * me, rows), rows)
-        return pltpu.make_async_copy(
-            m.zs.at[lax.rem(t, 2), pl.ds(pl.multiple_of(i * rows, rows), rows)],
-            m.o.at[:, mine], m.own_sem,
-        )
+    mine = pl.ds(pl.multiple_of(rows * me, rows), rows)
 
     def send_block(t):
         def send(k, carry):
             i = lax.rem(k + me // nj, per)
-            to, c = copy(t, i, me)
+            to = block_of(t) * per + i
+            src = m.zs.at[lax.rem(t, 2), pl.ds(pl.multiple_of(i * rows, rows), rows)]
 
             @pl.when(to != me)
             def _():
-                c.start()
+                pltpu.make_async_remote_copy(
+                    src_ref=src, dst_ref=m.o.at[:, mine],
+                    send_sem=m.send_sem.at[lax.rem(t, 2)], recv_sem=m.recv_sem,
+                    device_id=at(to), device_id_type=pl.DeviceIdType.MESH,
+                ).start()
 
             @pl.when(to == me)
             def _():
-                own(t, i).start()
+                pltpu.make_async_copy(src, m.o.at[:, mine], m.own_sem).start()
 
             return carry
 
         lax.fori_loop(0, per, send, 0)
 
     def sent_block(t):
-        def sent(k, carry):
-            i = lax.rem(k + me // nj, per)
-            to, c = copy(t, i, me)
-
-            @pl.when(to != me)
-            def _():
-                c.wait_send()
-
-            @pl.when(to == me)
-            def _():
-                own(t, i).wait()
-
-            return carry
-
-        lax.fori_loop(0, per, sent, 0)
+        here = block_of(t) == me // per
+        slot = lax.rem(t, 2)
+
+        def sent(count):
+            piece = m.zs.at[slot, pl.ds(0, count * rows)]
+            pltpu.make_async_copy(piece, piece, m.send_sem.at[slot]).wait()
+
+        @pl.when(here)
+        def _():
+            sent(per - 1)
+            pltpu.make_async_copy(m.zs.at[slot, pl.ds(0, rows)], m.o.at[:, mine], m.own_sem).wait()
+
+        @pl.when(jnp.logical_not(here))
+        def _():
+            sent(per)
 
     fetch(0).start()
     tools.project_all()
@@ -571,40 +561,25 @@
     send_block(nj - 1)
     if trans:
         def flag(t, carry):
-            c = pltpu.make_async_remote_copy(
+            pltpu.make_async_remote_copy(
                 src_ref=m.good.at[pl.ds(0, 1)], dst_ref=m.flags.at[me, pl.ds(0, 1)],
-                send_sem=m.fsend.at[t], recv_sem=m.frecv.at[t],
+                send_sem=m.fsend, recv_sem=m.frecv,
                 device_id=at(lax.rem(me + t, n)), device_id_type=pl.DeviceIdType.MESH,
-            )
-            c.start()
+            ).start()
             return carry
 
         lax.fori_loop(1, n, flag, 0)
-        mine = pltpu.make_async_copy(m.good, m.flags.at[me], m.fsend.at[0])
-        mine.start()
-        mine.wait()
+        own_flag = pltpu.make_async_copy(m.good, m.flags.at[me], m.flag_sem)
+        own_flag.start()
+        own_flag.wait()
     sent_block(nj - 2)
     sent_block(nj - 1)
-
-    def land(t, carry):
-        frm = lax.rem(me + n - t, n)
-        pltpu.make_async_remote_copy(
-            src_ref=m.zs.at[0, pl.ds(0, rows)],
-            dst_ref=m.o.at[:, pl.ds(pl.multiple_of(rows * frm, rows), rows)],
-            send_sem=m.send_sem.at[t], recv_sem=m.recv_sem.at[t],
-            device_id=at(frm), device_id_type=pl.DeviceIdType.MESH,
-        ).wait_recv()
-        if trans:
-            c = pltpu.make_async_remote_copy(
-                src_ref=m.good.at[pl.ds(0, 1)], dst_ref=m.flags.at[frm, pl.ds(0, 1)],
-                send_sem=m.fsend.at[t], recv_sem=m.frecv.at[t],
-                device_id=at(frm), device_id_type=pl.DeviceIdType.MESH,
-            )
-            c.wait_recv()
-            c.wait_send()
-        return carry
-
-    lax.fori_loop(1, n, land, 0)
+    others = m.o.at[:, pl.ds(0, rows * (n - 1))]
+    pltpu.make_async_copy(others, others, m.recv_sem).wait()
+    if trans:
+        others = m.flags.at[pl.ds(0, n - 1), pl.ds(0, 1)]
+        pltpu.make_async_copy(others, others, m.fsend).wait()
+        pltpu.make_async_copy(others, others, m.frecv).wait()
 
 
 def fused_attention(cid, n, ins, bias, before):
@@ -614,8 +589,8 @@
     del scratch["ss"]
     scratch |= {
         "zs": pltpu.VMEM((2, JB, rows, chan), BF16),
-        "send_sem": pltpu.SemaphoreType.DMA((n,)),
-        "recv_sem": pltpu.SemaphoreType.DMA((n,)),
+        "send_sem": pltpu.SemaphoreType.DMA((2,)),
+        "recv_sem": pltpu.SemaphoreType.DMA,
         "fetch_sem": pltpu.SemaphoreType.DMA,
         "own_sem": pltpu.SemaphoreType.DMA,
     }
@@ -633,8 +608,9 @@
         out_specs.append(anywhere)
         scratch |= {
             "good": pltpu.VMEM((8, 128), F32),
-            "fsend": pltpu.SemaphoreType.DMA((n,)),
-            "frecv": pltpu.SemaphoreType.DMA((n,)),
+            "fsend": pltpu.SemaphoreType.DMA,
+            "frecv": pltpu.SemaphoreType.DMA,
+            "flag_sem": pltpu.SemaphoreType.DMA,
         }
     else:
         outs["good"] = jax.ShapeDtypeStruct((8, 128), F32)
@@ -651,8 +627,9 @@
     )(*args)
 
 
-def exchange_kernel(n, z_ref, o_ref, send_sem, recv_sem, own_sem):
-    rows = o_ref.shape[0]
+def exchange_kernel(n, whole, z_ref, o_ref, send_sem, recv_sem, own_sem):
+    rows = z_ref.shape[1]
+    cut = lambda d: z_ref if whole else z_ref.at[pl.ds(pl.multiple_of(rows * d, rows), rows)]
     gy = n // 16
     me = lax.axis_index("gx") * gy + lax.axis_index("gy")
     at = lambda d: {"gx": d // gy, "gy": lax.rem(d, gy)}
@@ -666,13 +643,13 @@
 
     lax.fori_loop(1, n, greet, 0)
     mine = pl.ds(pl.multiple_of(rows * me, rows), rows)
-    own = pltpu.make_async_copy(z_ref.at[mine], o_ref.at[:, mine], own_sem)
+    own = pltpu.make_async_copy(cut(me), o_ref.at[:, mine], own_sem)
     own.start()
     pl.semaphore_wait(barrier, n - 1)
 
     def copy(t, to, frm):
         return pltpu.make_async_remote_copy(
-            src_ref=z_ref.at[pl.ds(pl.multiple_of(rows * to, rows), rows)],
+            src_ref=cut(to),
             dst_ref=o_ref.at[:, pl.ds(pl.multiple_of(rows * frm, rows), rows)],
             send_sem=send_sem.at[t], recv_sem=recv_sem.at[t],
             device_id=at(to), device_id_type=pl.DeviceIdType.MESH,
@@ -693,11 +670,12 @@
     lax.fori_loop(1, n, land, 0)
 
 
-def exchange(cid, n, z, rows):
-    res, _, chan = z.shape
+def exchange(cid, n, z, whole=False):
+    lead, rows, width = z.shape
+    shape = (lead, n * rows, width) if whole else (rows, lead, width)
     return pl.pallas_call(
-        functools.partial(exchange_kernel, n),
-        out_shape=jax.ShapeDtypeStruct((rows, res, chan), BF16),
+        functools.partial(exchange_kernel, n, whole),
+        out_shape=jax.ShapeDtypeStruct(shape, BF16),
         in_specs=[pl.BlockSpec(memory_space=pl.ANY)],
         out_specs=pl.BlockSpec(memory_space=pl.ANY),
         scratch_shapes=[
@@ -742,16 +720,16 @@
 
     def end_inputs(cols):
         bias, normed = pair_bias(cols, row(norm_end), bias_w_end)
-        return [cols, normed] + ends, gather(1, bias)
+        return [cols, normed] + ends, bias
 
     def safe(bias):
-        cols = exchange(4, n, safe_attention(start, bias, False), rows)
+        cols = exchange(4, n, safe_attention(start, bias, False))
         ins, bias = end_inputs(cols)
-        return exchange(5, n, safe_attention(ins, bias, True), rows)
+        return exchange(5, n, safe_attention(ins, exchange(6, n, bias, True), True))
 
     cols, good = fused_attention(2, n, start, bias, None)
     ins, end_bias = end_inputs(cols)
-    out, flags = fused_attention(3, n, ins, end_bias, good)
+    out, flags = fused_attention(3, n, ins, gather(1, end_bias), good)
     return lax.cond(jnp.min(flags[:, 0]) > 0.5, lambda b: out, safe, bias)
 
 

time: 261 us -> 251 us (0.962)
  Pallas kernels: 247 us -> 237 us
    pallas_call x2, Pallas kernels: 160 us -> 150 us  [fused_attention(): pl.pallas_call(functools.partial(fused_kernel, trans, n, names + list(out...]
where the time goes in v9:
time: 251 us
  Pallas kernels  237 us (94%)
  local copies, waits for them, and re-layouts  8.89 us (4%)
  other arithmetic  3.25 us (1%)
    pallas_call x2, Pallas kernels, fused_attention(): pl.pallas_call(functools.partial(fused_kernel, trans, n, names + list(out...  150 us
    pallas_call x2, Pallas kernels, gather(): pl.pallas_call(functools.partial(gather_kernel, n), out_shape=outs, in_sp...  78 us
    pallas_call x2, Pallas kernels, pair_bias(): pl.pallas_call(bias_kernel, out_shape=[jax.ShapeDtypeStruct((HEADS, rows,...  8.94 us

profile of v9, /device:TPU:1, one launch (start us, length us, event | category | flops | bytes accessed | tf_op | source)
XLA Modules:
  0.0 250.8 jit_solution(5665905871221046982)
XLA Ops:
  0.0 0.0 copy-start
  0.0 0.0 copy-start.5
  0.0 0.0 copy-start.1
  0.0 0.0 copy-start.9
  0.0 0.8 convert_bitcast_fusion
  0.8 0.6 pad.15.refs_1_
  1.4 0.8 copy.23
  2.2 0.6 pad.14.bw_ref
  2.8 0.8 copy.26
  3.7 0.6 pad.16.bw_ref
  4.3 4.5 %shard_map.156 = (bf16[4,8,1024]{2,1,0:T(8,128)(2,1)}, bf16[8,1024,128]{2,1,0:T(8,128)(2,1)}) custom-call(bf16[8,1024,128]{2,1,0:T(8,128)(2,1)} %refs_0_.1, f32[1,128]{1,0:T(1,128)} %bitcast.33, bf16[128,128]{1,0:T(8,128)(2,1)} %pad.14.bw_ref), custom_call_target="tpu_custom_call" | custom-call | tf_op jit(solution)/shard_map/pallas_call | solution.py:45
  8.7 42.0 %shard_map.157 = (bf16[4,2,4,2,4,2,8,1024]{7,6,5,4,3,2,1,0:T(8,128)(2,1)}, f32[2,4,2,4,2,8,128]{6,5,4,3,2,1,0:T(8,128)}) custom-call(bf16[4,8,1024]{2,1,0:T(8,128)(2,1)} %get-tuple-element.73.refs_0_, f32[8,128]{1,0:T(8,128)} %pad.15.refs_1_), custom_call_target="tpu_custom_call" | custom-call | tf_op jit(solution)/shard_map/pallas_call | solution.py:207
  50.7 1.1 slice.8
  51.8 0.6 reduce_max.9
  53.1 0.1 select_n.30.refs_5_
  53.2 0.1 select_n.31
  53.3 1.0 copy.25.refs_6_
  54.3 0.0 copy-done
  54.3 0.0 copy-done.5
  54.3 0.0 copy-done.1
  54.3 0.0 copy-done.9
  54.3 0.0 copy-start.12
  54.3 64.4 %shard_map.158 = (bf16[8,1024,128]{2,1,0:T(8,128)(2,1)}, f32[8,128]{1,0:T(8,128)}) custom-call(bf16[8,1024,128]{2,1,0:T(8,128)(2,1)S(1)} %copy-done, bf16[8,1024,128]{2,1,0:T(8,128)(2,1)} %get-tuple-element.72.refs_1_, bf16[128,512]{1,0:T(8,128)(2,1)S(1)} %copy-done.1, f32[1,128]{1,0:T(1,128)S(1)} %bitcast.25, bf16[128,128]{1,0:T(8,128)(2,1)S(1)} %copy-done.5, ...), custom_call_target="tpu_custom_call" | custom-call | tf_op jit(solution)/shard_map/pallas_call | solution.py:618
  118.7 0.0 copy-done.12
  118.8 4.5 %shard_map.159 = (bf16[4,8,1024]{2,1,0:T(8,128)(2,1)}, bf16[8,1024,128]{2,1,0:T(8,128)(2,1)}) custom-call(bf16[8,1024,128]{2,1,0:T(8,128)(2,1)} %get-tuple-element.76.x_ref.refs_0_, f32[1,128]{1,0:T(1,128)S(1)} %bitcast.31, bf16[128,128]{1,0:T(8,128)(2,1)} %pad.16.bw_ref), custom_call_target="tpu_custom_call" | custom-call | tf_op jit(solution)/shard_map/pallas_call | solution.py:45
  123.2 0.0 copy-start.2
  123.2 0.0 copy-start.3
  123.2 0.0 copy-start.4
  123.3 0.0 copy-start.6
  123.3 0.0 copy-start.7
  123.3 0.0 copy-start.10
  123.3 0.0 copy-start.11
  123.3 36.0 %shard_map.160 = bf16[4,2,4,2,4,2,8,1024]{7,6,5,4,3,2,1,0:T(8,128)(2,1)} custom-call(bf16[4,8,1024]{2,1,0:T(8,128)(2,1)} %get-tuple-element.78.refs_0_), custom_call_target="tpu_custom_call" | custom-call | tf_op jit(solution)/shard_map/pallas_call | solution.py:207
  159.3 0.0 copy-done.2
  159.3 0.0 copy-done.3
  159.3 0.0 copy-done.4
  159.3 0.0 copy-done.6
  159.4 0.0 copy-done.7
  159.4 0.0 copy-done.10
  159.4 0.0 copy-done.11
  159.4 0.0 copy-start.8
  159.4 85.7 %shard_map.161 = (bf16[8,1024,128]{2,1,0:T(8,128)(2,1)}, f32[128,8,128]{2,1,0:T(8,128)}) custom-call(bf16[8,1024,128]{2,1,0:T(8,128)(2,1)} %get-tuple-element.76.x_ref.refs_0_, bf16[8,1024,128]{2,1,0:T(8,128)(2,1)} %get-tuple-element.77.refs_1_, bf16[128,512]{1,0:T(8,128)(2,1)S(1)} %copy-done.2, f32[1,128]{1,0:T(1,128)S(1)} %bitcast.27, ...), custom_call_target="tpu_custom_call" | custom-call | tf_op jit(solution)/shard_map/pallas_call | solution.py:618
  245.1 1.8 slice_reduce_fusion
  247.5 0.0 copy-done.8
  247.5 0.2 conditional.1
  247.8 3.1 %copy.34 = bf16[8,1024,128]{2,1,0:T(8,128)(2,1)} copy(bf16[8,1024,128]{2,1,0:T(8,128)(2,1)} %get-tuple-element.82) | data formatting | bytes 4194304
  (1 shorter events, 0.0 us)
Async XLA Ops:
  0.0 54.3 %copy-start = (bf16[8,1024,128]{2,1,0:T(8,128)(2,1)S(1)}, bf16[8,1024,128]{2,1,0:T(8,128)(2,1)}, u32[]{:S(2)}) copy-start(bf16[8,1024,128]{2,1,0:T(8,128)(2,1)} %refs_0_.1) | copy-start | bytes 6291460
  0.0 54.3 %copy-start.5 = (bf16[128,128]{1,0:T(8,128)(2,1)S(1)}, bf16[128,128]{1,0:T(8,128)(2,1)}, u32[]{:S(2)}) copy-start(bf16[128,128]{1,0:T(8,128)(2,1)} %refs_4_.2) | copy-start | bytes 98308
  0.0 54.3 %copy-start.1 = (bf16[128,512]{1,0:T(8,128)(2,1)S(1)}, bf16[128,512]{1,0:T(8,128)(2,1)}, u32[]{:S(2)}) copy-start(bf16[128,512]{1,0:T(8,128)(2,1)} %refs_2_.2) | copy-start | bytes 393220
  0.0 54.3 %copy-start.9 = (f32[128]{0:T(128)S(1)}, f32[128]{0:T(128)}, u32[]{:S(2)}) copy-start(f32[128]{0:T(128)} %param.22) | copy-start | bytes 1540
  54.3 64.4 %copy-start.12 = (f32[128]{0:T(128)S(1)}, f32[128]{0:T(128)}, u32[]{:S(2)}) copy-start(f32[128]{0:T(128)} %param.25) | copy-start | bytes 1540
  123.2 36.1 %copy-start.2 = (bf16[128,512]{1,0:T(8,128)(2,1)S(1)}, bf16[128,512]{1,0:T(8,128)(2,1)}, u32[]{:S(2)}) copy-start(bf16[128,512]{1,0:T(8,128)(2,1)} %refs_2_.3) | copy-start | bytes 393220
  123.2 36.1 %copy-start.3 = (bf16[128,512]{1,0:T(8,128)(2,1)S(1)}, bf16[128,512]{1,0:T(8,128)(2,1)}, u32[]{:S(2)}) copy-start(bf16[128,512]{1,0:T(8,128)(2,1)} %refs_8_.1) | copy-start | bytes 393220
  123.2 36.1 %copy-start.4 = (bf16[512,128]{1,0:T(8,128)(2,1)S(1)}, bf16[512,128]{1,0:T(8,128)(2,1)}, u32[]{:S(2)}) copy-start(bf16[512,128]{1,0:T(8,128)(2,1)} %refs_10_.1) | copy-start | bytes 393220
  123.3 36.1 %copy-start.6 = (bf16[128,128]{1,0:T(8,128)(2,1)S(1)}, bf16[128,128]{1,0:T(8,128)(2,1)}, u32[]{:S(2)}) copy-start(bf16[128,128]{1,0:T(8,128)(2,1)} %refs_4_.3) | copy-start | bytes 98308
  123.3 36.1 %copy-start.7 = (f32[512]{0:T(512)S(1)}, f32[512]{0:T(512)}, u32[]{:S(2)}) copy-start(f32[512]{0:T(512)} %param.32) | copy-start | bytes 6148
  123.3 36.1 %copy-start.10 = (f32[128]{0:T(128)S(1)}, f32[128]{0:T(128)}, u32[]{:S(2)}) copy-start(f32[128]{0:T(128)} %param.27) | copy-start | bytes 1540
  123.3 36.1 %copy-start.11 = (f32[128]{0:T(128)S(1)}, f32[128]{0:T(128)}, u32[]{:S(2)}) copy-start(f32[128]{0:T(128)} %param.30) | copy-start | bytes 1540
  159.4 88.1 %copy-start.8 = (bf16[128,4]{0,1:T(4,128)(2,1)S(1)}, bf16[128,4]{0,1:T(4,128)(2,1)}, u32[]{:S(2)}) copy-start(bf16[128,4]{0,1:T(4,128)(2,1)} %param.28) | copy-start | bytes 3076

commit v10 on v9

--- a/solution.py
+++ b/solution.py
@@ -29,21 +29,20 @@
     return (cent * lax.rsqrt(var + 1e-05) * gain).astype(BF16)
 
 
-def bias_kernel(x_ref, g_ref, bw_ref, o_ref, a_ref):
+def bias_kernel(first, x_ref, g_ref, bw_ref, o_ref, a_ref):
     bwt = bw_ref[...].astype(F32).T.astype(BF16)
     gain = g_ref[...]
     for r in range(x_ref.shape[0]):
         a = layer_norm(x_ref[r], gain)
         a_ref[r] = a
         b = lax.dot_general(bwt, a, NT, preferred_element_type=F32) * LOG2E
-        o_ref[:, r, :] = b[:HEADS].astype(BF16)
-
-
-def pair_bias(x, gain, bias_w):
+        o_ref[:, r, :] = b[first : first + HEADS].astype(BF16)
+
+
+def pair_bias(x, gain, bw, first):
     rows, res, chan = x.shape
-    bw = jnp.pad(bias_w, ((0, 0), (0, 128 - HEADS)))
     return pl.pallas_call(
-        bias_kernel,
+        functools.partial(bias_kernel, first),
         out_shape=[
             jax.ShapeDtypeStruct((HEADS, rows, res), BF16),
             jax.ShapeDtypeStruct(x.shape, BF16),
@@ -92,7 +91,7 @@
     me = place()
     barrier = pltpu.get_barrier_semaphore()
     sib = {**me, "c": 1 - me["c"]}
-    partners = [shift(me, d, by) for d in "xyz" for by in (1, -1)] + [sib]
+    partners = [shift(me, d, by) for d in "xyz" for by in (1, -1, 2)] + [sib]
     for at in partners:
         pl.semaphore_signal(barrier, inc=1, device_id=device(at), device_id_type=pl.DeviceIdType.MESH)
     pl.semaphore_wait(barrier, len(partners))
@@ -127,12 +126,18 @@
                 c = copy(own if p == 0 else src, src, ring, (idx, p, k), shift(at, d, by))
                 c.start()
                 sends.append(c)
+            if p == 0:
+                c = copy(own, src, ring, (idx, p, 2), shift(at, d, 2))
+                c.start()
+                sends.append(c)
 
         def step1(p, idx, own, sets, half):
             d, free = ORDERS[core][idx][p], ORDERS[core][idx][:p]
             for k, by in enumerate((1, -1)):
                 got = sets(shift(at, d, -by), free)
                 copy(got, got, ring, (idx, p, k), shift(at, d, by)).wait_recv()
+                if p == 0:
+                    continue
                 if half:
                     tail = (slice(None), pl.ds(k * half, half))
                     piece = sets(shift(at, d, -by), free, tail)
@@ -147,7 +152,7 @@
         def step2(p, idx, own, sets, half):
             d, free = ORDERS[core][idx][p], ORDERS[core][idx][:p]
             for k, by in enumerate((1, -1)):
-                if half:
+                if half and p > 0:
                     tail = (slice(None), pl.ds(k * half, half))
                     piece = sets(shift(at, d, 2), free, tail)
                 elif k == 0:
@@ -395,7 +400,7 @@
 
 
 def stage_names(trans):
-    names = ["x", "a", "w", "gb", "ow", "mrow", "mcol"]
+    names = ["x", "a", "w", "gb", "ow", "mrow"]
     return names + (["ng", "ti", "tb", "to"] if trans else [])
 
 
@@ -439,7 +444,7 @@
 def safe_attention(ins, bias, trans):
     rows, res, chan = ins[0].shape
     scratch = stage_scratch(rows, res, chan)
-    names = stage_names(trans) + ["b", "o"] + list(scratch)
+    names = stage_names(trans) + ["mcol", "b", "o"] + list(scratch)
     full = lambda a: pl.BlockSpec(a.shape, lambda j, n=a.ndim: (0,) * n)
     return pl.pallas_call(
         functools.partial(safe_kernel, trans, names),
@@ -461,17 +466,26 @@
     nj = res // JB
     per = JB // rows
     gy = n // 16
-    me = lax.axis_index("gx") * gy + lax.axis_index("gy")
+    gx_me, gy_me = lax.axis_index("gx"), lax.axis_index("gy")
+    me = gx_me * gy + gy_me
     at = lambda d: {"gx": d // gy, "gy": lax.rem(d, gy)}
     barrier = pltpu.get_barrier_semaphore()
-
-    def greet(t, carry):
-        pl.semaphore_signal(
-            barrier, inc=1, device_id=at(lax.rem(me + t, n)), device_id_type=pl.DeviceIdType.MESH
-        )
-        return carry
-
-    lax.fori_loop(1, n, greet, 0)
+    cols = [lax.rem(gy_me + b, gy) for b in range(gy)]
+
+    def everyone(act):
+        def ring(a, carry):
+            for col in cols:
+                act({"gx": lax.rem(gx_me + a, n // gy), "gy": col})
+            return carry
+
+        for col in cols[1:]:
+            act({"gx": gx_me, "gy": col})
+        lax.fori_loop(1, n // gy, ring, 0)
+
+    def greet(to):
+        pl.semaphore_signal(barrier, inc=1, device_id=to, device_id_type=pl.DeviceIdType.MESH)
+
+    everyone(greet)
 
     def block_of(t):
         return lax.rem(t + me, nj)
@@ -560,15 +574,14 @@
         m.good[...] = jnp.broadcast_to(good, m.good.shape)
     send_block(nj - 1)
     if trans:
-        def flag(t, carry):
+        def flag(to):
             pltpu.make_async_remote_copy(
                 src_ref=m.good.at[pl.ds(0, 1)], dst_ref=m.flags.at[me, pl.ds(0, 1)],
                 send_sem=m.fsend, recv_sem=m.frecv,
-                device_id=at(lax.rem(me + t, n)), device_id_type=pl.DeviceIdType.MESH,
+                device_id=to, device_id_type=pl.DeviceIdType.MESH,
             ).start()
-            return carry
-
-        lax.fori_loop(1, n, flag, 0)
+
+        everyone(flag)
         own_flag = pltpu.make_async_copy(m.good, m.flags.at[me], m.flag_sem)
         own_flag.start()
         own_flag.wait()
@@ -709,23 +722,26 @@
     n = lax.axis_size(("gx", "gy"))
     row = lambda v: v.reshape(1, -1)
     mine = jnp.pad(residue_mask.astype(F32).reshape(1, rows), ((0, 7), (0, 128 - rows)))
-    bias, normed = pair_bias(pair_in, row(norm_start), bias_w_start)
+    bias_w = jnp.concatenate([bias_w_start, bias_w_end], axis=1)
+    bias_w = jnp.pad(bias_w, ((0, 0), (0, 128 - 2 * HEADS)))
+    bias, normed = pair_bias(pair_in, row(norm_start), bias_w, 0)
     bias, mask = gather(0, bias, mine)
     mask = mask[:, 0, :rows].reshape(res)
     mask = jnp.where(jnp.max(mask) > 0.5, mask, 1.0)
-    mrow, mcol = mask.reshape(1, res), mask.reshape(res, 1)
-    start = [pair_in, normed, proj_start, row(gate_bias_start), out_w_start, mrow, mcol]
-    ends = [proj_end, row(gate_bias_end), out_w_end, mrow, mcol]
+    mrow = mask.reshape(1, res)
+    start = [pair_in, normed, proj_start, row(gate_bias_start), out_w_start, mrow]
+    ends = [proj_end, row(gate_bias_end), out_w_end, mrow]
     ends += [row(norm_trans), trans_in, row(trans_bias), trans_out]
 
     def end_inputs(cols):
-        bias, normed = pair_bias(cols, row(norm_end), bias_w_end)
+        bias, normed = pair_bias(cols, row(norm_end), bias_w, HEADS)
         return [cols, normed] + ends, bias
 
     def safe(bias):
-        cols = exchange(4, n, safe_attention(start, bias, False))
+        mcol = [mask.reshape(res, 1)]
+        cols = exchange(4, n, safe_attention(start + mcol, bias, False))
         ins, bias = end_inputs(cols)
-        return exchange(5, n, safe_attention(ins, exchange(6, n, bias, True), True))
+        return exchange(5, n, safe_attention(ins + mcol, exchange(6, n, bias, True), True))
 
     cols, good = fused_attention(2, n, start, bias, None)
     ins, end_bias = end_inputs(cols)

time: 251 us -> 240 us (0.956)
  Pallas kernels: 237 us -> 229 us
  local copies, waits for them, and re-layouts: 8.89 us -> 5.03 us
    pallas_call x2, Pallas kernels: 78 us -> 73.7 us  [gather(): pl.pallas_call(functools.partial(gather_kernel, n), out_shape=outs, in_sp...]
    pallas_call x2, Pallas kernels: 150 us -> 147 us  [fused_attention(): pl.pallas_call(functools.partial(fused_kernel, trans, n, names + list(out...]
where the time goes in v10:
time: 240 us
  Pallas kernels  229 us (95%)
  local copies, waits for them, and re-layouts  5.03 us (2%)
  other arithmetic  3.97 us (2%)
    pallas_call x2, Pallas kernels, fused_attention(): pl.pallas_call(functools.partial(fused_kernel, trans, n, names + list(out...  147 us
    pallas_call x2, Pallas kernels, gather(): pl.pallas_call(functools.partial(gather_kernel, n), out_shape=outs, in_sp...  73.7 us
    pallas_call x2, Pallas kernels, pair_bias(): pl.pallas_call(functools.partial(bias_kernel, first), out_shape=[jax.Shap...  8.94 us

profile of v10, /device:TPU:1, one launch (start us, length us, event | category | flops | bytes accessed | tf_op | source)
XLA Modules:
  0.0 240.0 jit_solution(9254428507778615738)
XLA Ops:
  0.0 0.0 copy-start
  0.0 0.0 copy-start.5
  0.0 0.0 copy-start.1
  0.0 0.0 copy-start.8
  0.0 0.8 convert_bitcast_fusion
  0.8 0.7 pad_maximum_fusion
  1.5 0.6 pad.9.refs_1_
  2.1 0.1 copy.29
  2.3 4.5 %shard_map.156 = (bf16[4,8,1024]{2,1,0:T(8,128)(2,1)}, bf16[8,1024,128]{2,1,0:T(8,128)(2,1)}) custom-call(bf16[8,1024,128]{2,1,0:T(8,128)(2,1)} %refs_0_.1, f32[1,128]{1,0:T(1,128)} %bitcast.34, bf16[128,128]{1,0:T(8,128)(2,1)S(1)} %pad.8.bw_ref), custom_call_target="tpu_custom_call" | custom-call | tf_op jit(solution)/shard_map/pallas_call | solution.py:44
  6.7 39.3 %shard_map.157 = (bf16[4,2,4,2,4,2,8,1024]{7,6,5,4,3,2,1,0:T(8,128)(2,1)}, f32[2,4,2,4,2,8,128]{6,5,4,3,2,1,0:T(8,128)}) custom-call(bf16[4,8,1024]{2,1,0:T(8,128)(2,1)} %get-tuple-element.81.refs_0_, f32[8,128]{1,0:T(8,128)} %pad.9.refs_1_), custom_call_target="tpu_custom_call" | custom-call | tf_op jit(solution)/shard_map/pallas_call | solution.py:212
  46.1 1.1 slice.8
  47.2 0.6 reduce_max.9
  48.4 0.1 select_n.34.refs_5_
  48.5 0.0 copy-done
  48.5 0.0 copy-done.5
  48.5 0.0 copy-done.1
  48.5 0.0 copy-done.8
  48.5 0.0 copy-start.11
  48.5 63.6 %shard_map.158 = (bf16[8,1024,128]{2,1,0:T(8,128)(2,1)}, f32[8,128]{1,0:T(8,128)}) custom-call(bf16[8,1024,128]{2,1,0:T(8,128)(2,1)S(1)} %copy-done, bf16[8,1024,128]{2,1,0:T(8,128)(2,1)} %get-tuple-element.80.refs_1_, bf16[128,512]{1,0:T(8,128)(2,1)S(1)} %copy-done.1, f32[1,128]{1,0:T(1,128)S(1)} %bitcast.26, bf16[128,128]{1,0:T(8,128)(2,1)S(1)} %copy-done.5, ...), custom_call_target="tpu_custom_call" | custom-call | tf_op jit(solution)/shard_map/pallas_call | solution.py:631
  112.1 0.0 copy-done.11
  112.1 4.5 %shard_map.159 = (bf16[4,8,1024]{2,1,0:T(8,128)(2,1)}, bf16[8,1024,128]{2,1,0:T(8,128)(2,1)}) custom-call(bf16[8,1024,128]{2,1,0:T(8,128)(2,1)} %get-tuple-element.84.x_ref.refs_0_, f32[1,128]{1,0:T(1,128)S(1)} %bitcast.32, bf16[128,128]{1,0:T(8,128)(2,1)S(1)} %pad.8.bw_ref), custom_call_target="tpu_custom_call" | custom-call | tf_op jit(solution)/shard_map/pallas_call | solution.py:44
  116.6 0.0 copy-start.2
  116.6 0.0 copy-start.3
  116.6 0.0 copy-start.4
  116.6 0.0 copy-start.6
  116.6 0.0 copy-start.7
  116.6 0.0 copy-start.9
  116.6 0.0 copy-start.10
  116.7 34.3 %shard_map.160 = bf16[4,2,4,2,4,2,8,1024]{7,6,5,4,3,2,1,0:T(8,128)(2,1)} custom-call(bf16[4,8,1024]{2,1,0:T(8,128)(2,1)} %get-tuple-element.86.refs_0_), custom_call_target="tpu_custom_call" | custom-call | tf_op jit(solution)/shard_map/pallas_call | solution.py:212
  151.0 0.0 copy-done.2
  151.0 0.0 copy-done.3
  151.0 0.0 copy-done.4
  151.0 0.0 copy-done.6
  151.0 0.0 copy-done.7
  151.0 0.0 copy-done.9
  151.0 0.0 copy-done.10
  151.1 83.2 %shard_map.161 = (bf16[8,1024,128]{2,1,0:T(8,128)(2,1)}, f32[128,8,128]{2,1,0:T(8,128)}) custom-call(bf16[8,1024,128]{2,1,0:T(8,128)(2,1)} %get-tuple-element.84.x_ref.refs_0_, bf16[8,1024,128]{2,1,0:T(8,128)(2,1)} %get-tuple-element.85.refs_1_, bf16[128,512]{1,0:T(8,128)(2,1)S(1)} %copy-done.2, f32[1,128]{1,0:T(1,128)S(1)} %bitcast.28, ...), custom_call_target="tpu_custom_call" | custom-call | tf_op jit(solution)/shard_map/pallas_call | solution.py:631
  234.2 1.8 slice_reduce_fusion
  236.7 0.2 conditional.1
  236.9 3.1 %copy.35 = bf16[8,1024,128]{2,1,0:T(8,128)(2,1)} copy(bf16[8,1024,128]{2,1,0:T(8,128)(2,1)} %get-tuple-element.90) | data formatting | bytes 4194304
  (2 shorter events, 0.0 us)
Async XLA Ops:
  0.0 48.5 %copy-start = (bf16[8,1024,128]{2,1,0:T(8,128)(2,1)S(1)}, bf16[8,1024,128]{2,1,0:T(8,128)(2,1)}, u32[]{:S(2)}) copy-start(bf16[8,1024,128]{2,1,0:T(8,128)(2,1)} %refs_0_.1) | copy-start | bytes 6291460
  0.0 48.5 %copy-start.5 = (bf16[128,128]{1,0:T(8,128)(2,1)S(1)}, bf16[128,128]{1,0:T(8,128)(2,1)}, u32[]{:S(2)}) copy-start(bf16[128,128]{1,0:T(8,128)(2,1)} %refs_4_.2) | copy-start | bytes 98308
  0.0 48.5 %copy-start.1 = (bf16[128,512]{1,0:T(8,128)(2,1)S(1)}, bf16[128,512]{1,0:T(8,128)(2,1)}, u32[]{:S(2)}) copy-start(bf16[128,512]{1,0:T(8,128)(2,1)} %refs_2_.2) | copy-start | bytes 393220
  0.0 48.5 %copy-start.8 = (f32[128]{0:T(128)S(1)}, f32[128]{0:T(128)}, u32[]{:S(2)}) copy-start(f32[128]{0:T(128)} %param.22) | copy-start | bytes 1540
  48.5 63.6 %copy-start.11 = (f32[128]{0:T(128)S(1)}, f32[128]{0:T(128)}, u32[]{:S(2)}) copy-start(f32[128]{0:T(128)} %param.25) | copy-start | bytes 1540
  116.6 34.4 %copy-start.2 = (bf16[128,512]{1,0:T(8,128)(2,1)S(1)}, bf16[128,512]{1,0:T(8,128)(2,1)}, u32[]{:S(2)}) copy-start(bf16[128,512]{1,0:T(8,128)(2,1)} %refs_2_.3) | copy-start | bytes 393220
  116.6 34.4 %copy-start.3 = (bf16[128,512]{1,0:T(8,128)(2,1)S(1)}, bf16[128,512]{1,0:T(8,128)(2,1)}, u32[]{:S(2)}) copy-start(bf16[128,512]{1,0:T(8,128)(2,1)} %refs_7_.1) | copy-start | bytes 393220
  116.6 34.4 %copy-start.4 = (bf16[512,128]{1,0:T(8,128)(2,1)S(1)}, bf16[512,128]{1,0:T(8,128)(2,1)}, u32[]{:S(2)}) copy-start(bf16[512,128]{1,0:T(8,128)(2,1)} %refs_9_.1) | copy-start | bytes 393220
  116.6 34.4 %copy-start.6 = (bf16[128,128]{1,0:T(8,128)(2,1)S(1)}, bf16[128,128]{1,0:T(8,128)(2,1)}, u32[]{:S(2)}) copy-start(bf16[128,128]{1,0:T(8,128)(2,1)} %refs_4_.3) | copy-start | bytes 98308
  116.6 34.4 %copy-start.7 = (f32[512]{0:T(512)S(1)}, f32[512]{0:T(512)}, u32[]{:S(2)}) copy-start(f32[512]{0:T(512)} %param.32) | copy-start | bytes 6148
  116.6 34.4 %copy-start.9 = (f32[128]{0:T(128)S(1)}, f32[128]{0:T(128)}, u32[]{:S(2)}) copy-start(f32[128]{0:T(128)} %param.27) | copy-start | bytes 1540
  116.6 34.4 %copy-start.10 = (f32[128]{0:T(128)S(1)}, f32[128]{0:T(128)}, u32[]{:S(2)}) copy-start(f32[128]{0:T(128)} %param.30) | copy-start | bytes 1540

commit v11 on v10

--- a/solution.py
+++ b/solution.py
@@ -13,7 +13,7 @@
 LOG2E = 1.4426950408889634
 JB = 256
 KB = 128
-UNROLL = 4
+UNROLL = 8
 F32 = jnp.float32
 BF16 = jnp.bfloat16
 NT = (((1,), (1,)), ((), ()))

time: 240 us -> 238 us (level)
    pallas_call x2, Pallas kernels: 147 us -> 144 us  [fused_attention(): pl.pallas_call(functools.partial(fused_kernel, trans, n, names + list(out...]
where the time goes in v11:
time: 238 us
  Pallas kernels  227 us (95%)
  local copies, waits for them, and re-layouts  5.03 us (2%)
  other arithmetic  3.97 us (2%)
    pallas_call x2, Pallas kernels, fused_attention(): pl.pallas_call(functools.partial(fused_kernel, trans, n, names + list(out...  144 us
    pallas_call x2, Pallas kernels, gather(): pl.pallas_call(functools.partial(gather_kernel, n), out_shape=outs, in_sp...  73.6 us
    pallas_call x2, Pallas kernels, pair_bias(): pl.pallas_call(functools.partial(bias_kernel, first), out_shape=[jax.Shap...  8.94 us

profile of v11, /device:TPU:1, one launch (start us, length us, event | category | flops | bytes accessed | tf_op | source)
XLA Modules:
  0.0 237.5 jit_solution(5082384806636598910)
XLA Ops:
  0.0 0.0 copy-start
  0.0 0.0 copy-start.5
  0.0 0.0 copy-start.1
  0.0 0.0 copy-start.8
  0.0 0.8 convert_bitcast_fusion
  0.8 0.7 pad_maximum_fusion
  1.5 0.6 pad.9.refs_1_
  2.1 0.1 copy.29
  2.3 4.5 %shard_map.156 = (bf16[4,8,1024]{2,1,0:T(8,128)(2,1)}, bf16[8,1024,128]{2,1,0:T(8,128)(2,1)}) custom-call(bf16[8,1024,128]{2,1,0:T(8,128)(2,1)} %refs_0_.1, f32[1,128]{1,0:T(1,128)} %bitcast.34, bf16[128,128]{1,0:T(8,128)(2,1)S(1)} %pad.8.bw_ref), custom_call_target="tpu_custom_call" | custom-call | tf_op jit(solution)/shard_map/pallas_call | solution.py:44
  6.7 39.3 %shard_map.157 = (bf16[4,2,4,2,4,2,8,1024]{7,6,5,4,3,2,1,0:T(8,128)(2,1)}, f32[2,4,2,4,2,8,128]{6,5,4,3,2,1,0:T(8,128)}) custom-call(bf16[4,8,1024]{2,1,0:T(8,128)(2,1)} %get-tuple-element.81.refs_0_, f32[8,128]{1,0:T(8,128)} %pad.9.refs_1_), custom_call_target="tpu_custom_call" | custom-call | tf_op jit(solution)/shard_map/pallas_call | solution.py:212
  46.1 1.1 slice.8
  47.2 0.6 reduce_max.9
  48.4 0.1 select_n.34.refs_5_
  48.5 0.0 copy-done
  48.5 0.0 copy-done.5
  48.5 0.0 copy-done.1
  48.5 0.0 copy-done.8
  48.5 0.0 copy-start.11
  48.5 62.6 %shard_map.158 = (bf16[8,1024,128]{2,1,0:T(8,128)(2,1)}, f32[8,128]{1,0:T(8,128)}) custom-call(bf16[8,1024,128]{2,1,0:T(8,128)(2,1)S(1)} %copy-done, bf16[8,1024,128]{2,1,0:T(8,128)(2,1)} %get-tuple-element.80.refs_1_, bf16[128,512]{1,0:T(8,128)(2,1)S(1)} %copy-done.1, f32[1,128]{1,0:T(1,128)S(1)} %bitcast.26, bf16[128,128]{1,0:T(8,128)(2,1)S(1)} %copy-done.5, ...), custom_call_target="tpu_custom_call" | custom-call | tf_op jit(solution)/shard_map/pallas_call | solution.py:631
  111.1 0.0 copy-done.11
  111.1 4.5 %shard_map.159 = (bf16[4,8,1024]{2,1,0:T(8,128)(2,1)}, bf16[8,1024,128]{2,1,0:T(8,128)(2,1)}) custom-call(bf16[8,1024,128]{2,1,0:T(8,128)(2,1)} %get-tuple-element.84.x_ref.refs_0_, f32[1,128]{1,0:T(1,128)S(1)} %bitcast.32, bf16[128,128]{1,0:T(8,128)(2,1)S(1)} %pad.8.bw_ref), custom_call_target="tpu_custom_call" | custom-call | tf_op jit(solution)/shard_map/pallas_call | solution.py:44
  115.6 0.0 copy-start.2
  115.6 0.0 copy-start.3
  115.6 0.0 copy-start.4
  115.6 0.0 copy-start.6
  115.6 0.0 copy-start.7
  115.7 0.0 copy-start.9
  115.7 0.0 copy-start.10
  115.7 34.3 %shard_map.160 = bf16[4,2,4,2,4,2,8,1024]{7,6,5,4,3,2,1,0:T(8,128)(2,1)} custom-call(bf16[4,8,1024]{2,1,0:T(8,128)(2,1)} %get-tuple-element.86.refs_0_), custom_call_target="tpu_custom_call" | custom-call | tf_op jit(solution)/shard_map/pallas_call | solution.py:212
  149.9 0.0 copy-done.2
  150.0 0.0 copy-done.3
  150.0 0.0 copy-done.4
  150.0 0.0 copy-done.6
  150.0 0.0 copy-done.7
  150.0 0.0 copy-done.9
  150.0 0.0 copy-done.10
  150.0 81.7 %shard_map.161 = (bf16[8,1024,128]{2,1,0:T(8,128)(2,1)}, f32[128,8,128]{2,1,0:T(8,128)}) custom-call(bf16[8,1024,128]{2,1,0:T(8,128)(2,1)} %get-tuple-element.84.x_ref.refs_0_, bf16[8,1024,128]{2,1,0:T(8,128)(2,1)} %get-tuple-element.85.refs_1_, bf16[128,512]{1,0:T(8,128)(2,1)S(1)} %copy-done.2, f32[1,128]{1,0:T(1,128)S(1)} %bitcast.28, ...), custom_call_target="tpu_custom_call" | custom-call | tf_op jit(solution)/shard_map/pallas_call | solution.py:631
  231.7 1.8 slice_reduce_fusion
  234.2 0.2 conditional.1
  234.4 3.1 %copy.35 = bf16[8,1024,128]{2,1,0:T(8,128)(2,1)} copy(bf16[8,1024,128]{2,1,0:T(8,128)(2,1)} %get-tuple-element.90) | data formatting | bytes 4194304
  (2 shorter events, 0.0 us)
Async XLA Ops:
  0.0 48.5 %copy-start = (bf16[8,1024,128]{2,1,0:T(8,128)(2,1)S(1)}, bf16[8,1024,128]{2,1,0:T(8,128)(2,1)}, u32[]{:S(2)}) copy-start(bf16[8,1024,128]{2,1,0:T(8,128)(2,1)} %refs_0_.1) | copy-start | bytes 6291460
  0.0 48.5 %copy-start.5 = (bf16[128,128]{1,0:T(8,128)(2,1)S(1)}, bf16[128,128]{1,0:T(8,128)(2,1)}, u32[]{:S(2)}) copy-start(bf16[128,128]{1,0:T(8,128)(2,1)} %refs_4_.2) | copy-start | bytes 98308
  0.0 48.5 %copy-start.1 = (bf16[128,512]{1,0:T(8,128)(2,1)S(1)}, bf16[128,512]{1,0:T(8,128)(2,1)}, u32[]{:S(2)}) copy-start(bf16[128,512]{1,0:T(8,128)(2,1)} %refs_2_.2) | copy-start | bytes 393220
  0.0 48.5 %copy-start.8 = (f32[128]{0:T(128)S(1)}, f32[128]{0:T(128)}, u32[]{:S(2)}) copy-start(f32[128]{0:T(128)} %param.22) | copy-start | bytes 1540
  48.5 62.6 %copy-start.11 = (f32[128]{0:T(128)S(1)}, f32[128]{0:T(128)}, u32[]{:S(2)}) copy-start(f32[128]{0:T(128)} %param.25) | copy-start | bytes 1540
  115.6 34.3 %copy-start.2 = (bf16[128,512]{1,0:T(8,128)(2,1)S(1)}, bf16[128,512]{1,0:T(8,128)(2,1)}, u32[]{:S(2)}) copy-start(bf16[128,512]{1,0:T(8,128)(2,1)} %refs_2_.3) | copy-start | bytes 393220
  115.6 34.3 %copy-start.3 = (bf16[128,512]{1,0:T(8,128)(2,1)S(1)}, bf16[128,512]{1,0:T(8,128)(2,1)}, u32[]{:S(2)}) copy-start(bf16[128,512]{1,0:T(8,128)(2,1)} %refs_7_.1) | copy-start | bytes 393220
  115.6 34.3 %copy-start.4 = (bf16[512,128]{1,0:T(8,128)(2,1)S(1)}, bf16[512,128]{1,0:T(8,128)(2,1)}, u32[]{:S(2)}) copy-start(bf16[512,128]{1,0:T(8,128)(2,1)} %refs_9_.1) | copy-start | bytes 393220
  115.6 34.3 %copy-start.6 = (bf16[128,128]{1,0:T(8,128)(2,1)S(1)}, bf16[128,128]{1,0:T(8,128)(2,1)}, u32[]{:S(2)}) copy-start(bf16[128,128]{1,0:T(8,128)(2,1)} %refs_4_.3) | copy-start | bytes 98308
  115.6 34.3 %copy-start.7 = (f32[512]{0:T(512)S(1)}, f32[512]{0:T(512)}, u32[]{:S(2)}) copy-start(f32[512]{0:T(512)} %param.32) | copy-start | bytes 6148
  115.7 34.3 %copy-start.9 = (f32[128]{0:T(128)S(1)}, f32[128]{0:T(128)}, u32[]{:S(2)}) copy-start(f32[128]{0:T(128)} %param.27) | copy-start | bytes 1540
  115.7 34.3 %copy-start.10 = (f32[128]{0:T(128)S(1)}, f32[128]{0:T(128)}, u32[]{:S(2)}) copy-start(f32[128]{0:T(128)} %param.30) | copy-start | bytes 1540
